TPU v7x, 32 devices: a whole 2x2x4 slice. The times are simulated.
32 devices in a mesh: group: 2 (over y), seq: 16 (over z, x, core).
Axes of the slice: x: 2, y: 2, z: 4, core: 2. Of those that a mesh axis runs over, the one named last changes fastest.
Arguments:
- tiles: bfloat16 [2, 6144, 1536], P('group', 'seq'), may hold values from -6 to 6
- tile_counts: int32 [2, 16], P('group', 'seq'), may hold values from 1 to 352, as said below
- w_gate: bfloat16 [1536, 2048], P(None, ('group', 'seq')), may hold values from -0.15625 to 0.15625
- w_up: bfloat16 [1536, 2048], P(None, ('group', 'seq')), may hold values from -0.15625 to 0.15625
- w_down_t: bfloat16 [1536, 2048], P(None, ('group', 'seq')), may hold values from -0.125 to 0.125
- w_embed: bfloat16 [1536, 768], replicated, may hold values from -0.15625 to 0.15625
- w_query: bfloat16 [768, 768], replicated, may hold values from -2 to 2
- w_key: bfloat16 [768, 768], replicated, may hold values from -2 to 2
- w_value: bfloat16 [768, 768], replicated, may hold values from -0.21875 to 0.21875
- w_out: bfloat16 [768, 768], replicated, may hold values from -0.21875 to 0.21875
- cotangent: bfloat16 [2, 6144, 768], P('group', 'seq'), may hold values from -6 to 6
Outputs:
- slide_out: bfloat16 [2, 6144, 768], P('group', 'seq')
- grad_value: float32 [768, 768], P('seq')
- grad_out: float32 [768, 768], P('seq')
Inputs may be any that keep to these rules, and one draw needn't show every extreme that they name: `tile_counts`: the counts of slides 2i and 2i+1 at the same block index, each rounded up to whole blocks of 32 tiles, add up to at most 12 blocks; in every draw some pair reaches that. The tissue tiles of a block are its first positions.
All inputs are finite; a program needn't handle non-finite values.
Results may differ from a plain program's by a relative error of at most 0.03.
Values may be sent and summed in bfloat16 or wider, within the bound.
No kernel may reach another device: no remote copies, remote signals or barrier semaphores. Data moves between devices by JAX's collectives and lax.ppermute only.
A program may use at most 128 MiB of HBM per device.

v0:
```python
import math

import jax
import jax.numpy as jnp
from jax import lax
from jax.sharding import PartitionSpec as P

HEADS = 16
HEAD = 48
RATE = 16


epsilon = 1e-06


def rms_rows(values):
    values = values.astype(jnp.float32)
    return values * lax.rsqrt(jnp.mean(values * values, axis=-1, keepdims=True) + epsilon)


def hidden_term(normed, gate_piece, up_piece, down_piece):
    gate_proj = jnp.dot(normed, gate_piece, preferred_element_type=jnp.float32)
    upward = jnp.dot(normed, up_piece, preferred_element_type=jnp.float32)
    active = (jax.nn.silu(gate_proj) * upward).astype(jnp.bfloat16)
    return lax.dot_general(
        active, down_piece, (((1,), (1,)), ((), ())), preferred_element_type=jnp.float32
    )


def finish_tiles(tile_rows, mixed, w_embed):
    encoded = tile_rows.astype(jnp.float32) + mixed
    embedded = rms_rows(encoded).astype(jnp.bfloat16)
    return jnp.dot(embedded, w_embed, preferred_element_type=jnp.float32).astype(jnp.bfloat16)


def encode_whole(tile_rows, w_gate, w_up, w_down_t, w_embed):
    normed = rms_rows(tile_rows).astype(jnp.bfloat16)
    mixed = hidden_term(
        normed,
        lax.all_gather(w_gate, ("group", "seq"), axis=1, tiled=True),
        lax.all_gather(w_up, ("group", "seq"), axis=1, tiled=True),
        lax.all_gather(w_down_t, ("group", "seq"), axis=1, tiled=True),
    )
    return finish_tiles(tile_rows, mixed, w_embed)


def shards(
    tiles, tile_counts, w_gate, w_up, w_down_t, w_embed, w_query, w_key, w_value, w_out, cotangent
):
    tile_rows = tiles[0]
    row_count = tile_counts[0, 0]
    seq_len = tile_rows.shape[0]
    slide_tok = encode_whole(tile_rows, w_gate, w_up, w_down_t, w_embed)
    score_scale = 1.0 / math.sqrt(HEAD)
    is_valid = jnp.arange(seq_len) < row_count
    valid_f = is_valid.astype(jnp.float32)
    slide_normed = rms_rows(slide_tok).astype(jnp.bfloat16)
    queries = jnp.dot(slide_normed, w_query, preferred_element_type=jnp.float32).astype(
        jnp.bfloat16
    )
    key_rows = jnp.dot(slide_normed, w_key, preferred_element_type=jnp.float32).astype(jnp.bfloat16)
    value_rows = jnp.dot(slide_normed, w_value, preferred_element_type=jnp.float32).astype(
        jnp.bfloat16
    )
    feature_width = key_rows.shape[1]
    dilated = seq_len // RATE
    own_keys = key_rows.reshape(dilated, RATE, feature_width)[:, 0]
    own_values = value_rows.reshape(dilated, RATE, feature_width)[:, 0]
    own_flags = valid_f.reshape(dilated, RATE)[:, 0].astype(jnp.bfloat16)
    far_keys, far_values, far_flags = (
        lax.all_gather(own_keys, "seq", axis=0, tiled=True),
        lax.all_gather(own_values, "seq", axis=0, tiled=True),
        lax.all_gather(own_flags, "seq", axis=0, tiled=True),
    )
    key_set = jnp.concatenate([key_rows, far_keys], axis=0).reshape(-1, HEADS, HEAD)
    value_set = jnp.concatenate([value_rows, far_values], axis=0).reshape(-1, HEADS, HEAD)
    key_valid = jnp.concatenate([valid_f, far_flags.astype(jnp.float32)]) > 0.5
    query_heads = queries.reshape(seq_len, HEADS, HEAD)
    scores = (
        jnp.einsum("phd,jhd->hpj", query_heads, key_set, preferred_element_type=jnp.float32)
        * score_scale
    )
    scores = jnp.where(key_valid[None, None, :], scores, -1e30)
    row_max = jnp.max(scores, axis=2, keepdims=True)
    exponent = jnp.exp(scores - row_max)
    weights = (exponent / jnp.sum(exponent, axis=2, keepdims=True)).astype(jnp.bfloat16)
    attended = jnp.einsum("hpj,jhd->phd", weights, value_set, preferred_element_type=jnp.float32)
    attended = attended.reshape(seq_len, feature_width).astype(jnp.bfloat16)
    output = slide_tok.astype(jnp.float32) + jnp.dot(
        attended, w_out, preferred_element_type=jnp.float32
    )
    slide_out = jnp.where(is_valid[:, None], output, 0.0).astype(jnp.bfloat16)
    grad_y = jnp.where(is_valid[:, None], cotangent[0], jnp.zeros_like(cotangent[0]))
    part_out = lax.dot_general(
        attended, grad_y, (((0,), (0,)), ((), ())), preferred_element_type=jnp.float32
    )
    grad_att = lax.dot_general(
        grad_y, w_out, (((1,), (1,)), ((), ())), preferred_element_type=jnp.float32
    )
    grad_heads = grad_att.astype(jnp.bfloat16).reshape(seq_len, HEADS, HEAD)
    local_grad = jnp.einsum(
        "hpj,phd->jhd", weights[:, :, :seq_len], grad_heads, preferred_element_type=jnp.float32
    )
    local_grad = local_grad.reshape(seq_len, feature_width)
    far_weights = weights[:, :, seq_len:]
    far_grad = lax.psum_scatter(
        jnp.einsum("hpj,phd->jhd", far_weights, grad_heads, preferred_element_type=jnp.float32)
        .reshape(dilated * lax.axis_size("seq"), feature_width)
        .astype(jnp.bfloat16),
        "seq",
        scatter_dimension=0,
        tiled=True,
    ).astype(jnp.float32)
    grouped = local_grad.reshape(dilated, RATE, feature_width)
    leading = grouped[:, :1] + far_grad[:, None]
    grad_values = (
        jnp.concatenate([leading, grouped[:, 1:]], axis=1)
        .reshape(seq_len, feature_width)
        .astype(jnp.bfloat16)
    )
    part_value = lax.dot_general(
        slide_normed, grad_values, (((0,), (0,)), ((), ())), preferred_element_type=jnp.float32
    )
    rows_value, rows_out = (
        lax.psum_scatter(
            part_value.astype(jnp.bfloat16), "seq", scatter_dimension=0, tiled=True
        ).astype(jnp.float32),
        lax.psum_scatter(
            part_out.astype(jnp.bfloat16), "seq", scatter_dimension=0, tiled=True
        ).astype(jnp.float32),
    )
    grad_value, grad_out = (
        lax.psum(rows_value.astype(jnp.bfloat16), "group").astype(jnp.float32),
        lax.psum(rows_out.astype(jnp.bfloat16), "group").astype(jnp.float32),
    )
    return (slide_out[None], grad_value, grad_out)


def solution(mesh):
    placed = (
        P("group", "seq", None),
        P("group", "seq"),
        P(None, ("group", "seq")),
        P(None, ("group", "seq")),
        P(None, ("group", "seq")),
        P(),
        P(),
        P(),
        P(),
        P(),
        P("group", "seq", None),
    )
    return jax.shard_map(
        shards,
        mesh=mesh,
        in_specs=placed,
        out_specs=(P("group", "seq", None), P("seq", None), P("seq", None)),
        check_vma=False,
    )
```

profile of v0, /device:TPU:0, one launch (start us, length us, event | category | flops | bytes accessed | tf_op | source)
XLA Modules:
  0.0 495.6 jit_solution(5722972642607966426)
XLA Ops:
  7.2 0.0 copy-start
  7.2 0.0 all-gather.7.cloned.1.call-start
  7.2 0.7 all-gather.7.cloned.1.call-update
  7.9 0.0 all-gather.11.cloned.1.call-start
  8.0 0.7 all-gather.11.cloned.1.call-update
  8.7 0.0 all-gather.9.cloned.1.call-start
  8.7 0.7 all-gather.9.cloned.1.call-update
  9.4 0.0 reduce-scatter.4.cloned.1.call-start
  10.1 1.2 dynamic-slice
  12.0 0.2 dynamic-update-slice
  12.3 35.4 %all-reduce = bf16[384]{0:T(512)(128)(2,1)S(1)} all-reduce(bf16[384]{0:T(512)(128)(2,1)S(1)} %dynamic-update-slice), channel_id=3, replica_groups=mesh['group'=2,'seq'=16] {'seq'}, use_global_device_ids=true, to_apply=%add | all-reduce | flops 384 | bytes 1536
  47.6 2.1 convolution_convert_fusion.3
  49.8 0.3 copy.33
  50.1 1.6 fusion.9
  51.7 31.1 %all-gather.7.cloned.1.call-done = bf16[1536,2048]{0,1:T(8,128)(2,1)} async-done(((bf16[1536,64]{0,1:T(8,128)(2,1)}), bf16[1536,2048]{0,1:T(8,128)(2,1)}) %all-gather.7.cloned.1.call-update) | async-done | bytes 6291472 | tf_op jit(solution)/shard_map/all_gather | solution.py:40
  82.8 7.5 %fusion.31 = f32[384,2048]{1,0:T(8,128)} fusion(bf16[1536,2048]{0,1:T(8,128)(2,1)} %all-gather.7.cloned.1.call-done, bf16[1,384,1536]{2,1,0:T(8,128)(2,1)} %param.11, f32[384]{0:T(512)S(1)} %add_rsqrt_fusion.2), kind=kOutput, calls=%fused_computation.49 | convolution fusion | flops 2417688576 | bytes 10618368 | tf_op jit(solution)/shard_map/dot_general | solution.py:22
  90.3 63.1 %all-gather.11.cloned.1.call-done = bf16[1536,2048]{0,1:T(8,128)(2,1)} async-done(((bf16[1536,64]{0,1:T(8,128)(2,1)}), bf16[1536,2048]{0,1:T(8,128)(2,1)}) %all-gather.11.cloned.1.call-update) | async-done | bytes 6291472 | tf_op jit(solution)/shard_map/all_gather | solution.py:42
  153.5 70.6 %all-gather.9.cloned.1.call-done = bf16[1536,2048]{0,1:T(8,128)(2,1)} async-done(((bf16[1536,64]{0,1:T(8,128)(2,1)}), bf16[1536,2048]{0,1:T(8,128)(2,1)}) %all-gather.9.cloned.1.call-update) | async-done | bytes 6291472 | tf_op jit(solution)/shard_map/all_gather | solution.py:41
  224.1 12.6 %multiply_reduce_fusion = (f32[384]{0:T(512)S(1)}, f32[384,1536]{1,0:T(8,128)}) fusion(bf16[1536,2048]{0,1:T(8,128)(2,1)} %all-gather.11.cloned.1.call-done, f32[384,2048]{1,0:T(8,128)} %fusion.31, bf16[1536,2048]{0,1:T(8,128)(2,1)} %all-gather.9.cloned.1.call-done, bf16[1,384,1536]{2,1,0:T(8,128)(2,1)} %param.11, f32[384]{0:T(512)S(1)} %add_rsqrt_fusion.2), kind=kOutput, calls=%fused_computation.19 | convolution fusion | flops 4840685056 | bytes 19270656 | tf_op jit(solution)/shard_map/dot_general | solution.py:25
  236.7 3.0 fusion.22
  239.7 0.7 convolution_convert_fusion.5
  240.4 0.1 copy-done.7
  240.6 21.6 %all-gather.2 = bf16[384,1,768]{2,0,1:T(8,128)(2,1)S(1)} all-gather(bf16[24,1,768]{2,0,1:T(8,128)(2,1)S(1)} %copy.39), channel_id=4, replica_groups=mesh['group'=2,'seq'=16] {'seq'}, dimensions={0}, use_global_device_ids=true | all-gather | bytes 626688 | tf_op jit(solution)/shard_map/all_gather | solution.py:71
  262.2 0.1 pad_maximum_fusion.1
  262.3 1.5 copy.32
  263.7 1.9 convolution_convert_fusion.6
  265.7 0.3 copy.30
  266.0 1.0 copy-done.3
  266.9 10.4 %fusion.50 = (f32[16,384]{1,0:T(8,128)S(1)}, f32[16,384,768]{2,1,0:T(8,128)}) fusion(pred[768]{0:T(1024)(128)(4,1)S(1)} %maximum_compare_fusion, bf16[384,16,48]{0,2,1:T(8,128)(2,1)S(1)} %bitcast.76, bf16[768,16,48]{0,2,1:T(8,128)(2,1)S(1)} %bitcast.70), kind=kOutput, calls=%fused_computation.70 | convolution fusion | flops 471859968 | bytes 20669184 | tf_op jit(solution)/shard_map/sub | solution.py:85
  277.3 7.6 %divide_convert_fusion = bf16[16,384,768]{2,1,0:T(8,128)(2,1)S(1)} fusion(f32[16,384,768]{2,1,0:T(8,128)} %get-tuple-element.10, f32[16,384]{1,0:T(8,128)S(1)} %get-tuple-element.9), kind=kLoop, calls=%fused_computation.1 | loop fusion | flops 9437184 | bytes 28336128 | tf_op jit(solution)/shard_map/convert_element_type | solution.py:86
  284.9 3.6 copy-done.2
  288.5 0.8 fusion.18
  289.4 1.1 copy.36
  290.4 0.0 reduce-scatter.4.cloned.1.call-update
  290.5 0.0 reduce-scatter.8.cloned.1.call-start
  290.5 0.2 copy-done.5
  290.8 0.2 copy-done.9
  291.0 0.7 convolution_convert_fusion.7
  291.7 19.1 %all-gather = bf16[384,1,768]{2,0,1:T(8,128)(2,1)S(1)} all-gather(bf16[24,1,768]{2,0,1:T(8,128)(2,1)S(1)} %copy.38), channel_id=2, replica_groups=mesh['group'=2,'seq'=16] {'seq'}, dimensions={0}, use_global_device_ids=true | all-gather | bytes 626688 | tf_op jit(solution)/shard_map/all_gather | solution.py:72
  310.8 0.1 pad_maximum_fusion
  310.9 0.6 copy.29
  311.5 0.0 copy-start.6
  311.5 6.5 %convolution_convert_fusion.4 = bf16[16,48,384]{2,1,0:T(8,128)(2,1)S(1)} fusion(bf16[768,16,48]{0,2,1:T(8,128)(2,1)S(1)} %bitcast.66, bf16[16,384,768]{2,1,0:T(8,128)(2,1)} %copy-done.2), kind=kOutput, calls=%fused_computation.32 | convolution fusion | flops 453279744 | bytes 11206656 | tf_op jit(solution)/shard_map/hpj,jhd->phd/dot_general | solution.py:87
  318.1 1.9 convolution_convert_fusion
  320.0 0.0 reduce-scatter.8.cloned.1.call-update
  320.0 0.3 reduce-scatter.6.cloned.1.call-start
  320.3 3.2 fusion.14
  323.5 2.3 copy.34
  325.7 2.8 reshape_reshape.3
  328.6 0.1 slice.53
  328.7 12.5 %reduce-scatter.4.cloned.1.call-done = bf16[24,768]{1,0:T(8,128)(2,1)} async-done(((bf16[384,768]{1,0:T(8,128)(2,1)}), bf16[24,768]{1,0:T(8,128)(2,1)}) %reduce-scatter.4.cloned.1.call-update) | async-done | bytes 36880 | tf_op jit(solution)/shard_map/reduce_scatter | solution.py:106
  341.2 0.8 fusion.35
  342.0 0.1 copy.37
  342.0 0.2 pad_maximum_fusion.2
  342.3 1.9 convolution_convert_fusion.1
  344.2 0.0 reduce-scatter.6.cloned.1.call-update
  344.3 0.0 all-reduce.4.cloned.1.call-start
  344.3 57.5 %reduce-scatter.8.cloned.1.call-done = bf16[48,768]{1,0:T(8,128)(2,1)} async-done(((bf16[768,768]{1,0:T(8,128)(2,1)}), bf16[48,768]{1,0:T(8,128)(2,1)}) %reduce-scatter.8.cloned.1.call-update) | async-done | bytes 73744 | tf_op jit(solution)/shard_map/reduce_scatter | solution.py:128
  401.8 60.7 %reduce-scatter.6.cloned.1.call-done = bf16[48,768]{1,0:T(8,128)(2,1)} async-done(((bf16[768,768]{1,0:T(8,128)(2,1)}), bf16[48,768]{1,0:T(8,128)(2,1)}) %reduce-scatter.6.cloned.1.call-update) | async-done | bytes 73744 | tf_op jit(solution)/shard_map/reduce_scatter | solution.py:125
  462.5 0.0 all-reduce.4.cloned.1.call-update
  462.6 2.9 fusion.21
  465.5 20.2 %all-reduce.4.cloned.1.call-done = (bf16[48,768]{1,0:T(8,128)(2,1)}, bf16[48,768]{1,0:T(8,128)(2,1)}) async-done(((bf16[48,768]{1,0:T(8,128)(2,1)}, bf16[48,768]{1,0:T(8,128)(2,1)}), (bf16[48,768]{1,0:T(8,128)(2,1)}, bf16[48,768]{1,0:T(8,128)(2,1)})) %all-reduce.4.cloned.1.call-update) | async-done | bytes 147472 | tf_op jit(solution)/shard_map/psum | solution.py:133
  485.7 1.6 convert_element_type.126
  487.2 1.6 convert_element_type.128
  (28 shorter events, 0.2 us)
Async XLA Ops:
  7.2 229.5 %copy-start = (bf16[1536,768]{1,0:T(8,128)(2,1)S(1)}, bf16[1536,768]{1,0:T(8,128)(2,1)}, u32[]{:S(2)}) copy-start(bf16[1536,768]{1,0:T(8,128)(2,1)} %param.16) | copy-start | bytes 7077892
  7.2 75.7 %all-gather.7.cloned.1.call-start = ((), (), s32[]{:S(2)}) async-start(), calls=%async_computation.3 | async-start | bytes 6488064 | tf_op jit(solution)/shard_map/all_gather | solution.py:40
  7.9 145.5 %all-gather.11.cloned.1.call-start = ((), (), s32[]{:S(2)}) async-start(), calls=%async_computation.5 | async-start | bytes 6488064 | tf_op jit(solution)/shard_map/all_gather | solution.py:42
  8.7 215.4 %all-gather.9.cloned.1.call-start = ((), (), s32[]{:S(2)}) async-start(), calls=%async_computation.4 | async-start | bytes 6488064 | tf_op jit(solution)/shard_map/all_gather | solution.py:41
  9.4 331.8 %reduce-scatter.4.cloned.1.call-start = ((), (), s32[]{:S(2)}) async-start(), calls=%async_computation.6 | async-start | bytes 626688 | tf_op jit(solution)/shard_map/reduce_scatter | solution.py:106
  236.7 3.0 copy-start.4
  239.7 0.8 copy-start.7
  262.2 1.5 copy-start.8
  265.7 1.3 copy-start.3
  284.9 3.6 copy-start.2
  289.4 1.4 copy-start.5
  289.4 1.6 copy-start.9
  290.5 111.4 %reduce-scatter.8.cloned.1.call-start = ((), (), s32[]{:S(2)}) async-start(), calls=%async_computation.8 | async-start | bytes 1253376 | tf_op jit(solution)/shard_map/reduce_scatter | solution.py:128
  311.5 6.5 %copy-start.6 = (bf16[1,384,768]{2,1,0:T(8,128)(2,1)S(1)}, bf16[1,384,768]{2,1,0:T(8,128)(2,1)}, u32[]{:S(2)}) copy-start(bf16[1,384,768]{2,1,0:T(8,128)(2,1)} %param.21) | copy-start | bytes 1769476
  320.0 142.5 %reduce-scatter.6.cloned.1.call-start = ((), (), s32[]{:S(2)}) async-start(), calls=%async_computation.7 | async-start | bytes 1253376 | tf_op jit(solution)/shard_map/reduce_scatter | solution.py:125
  328.6 13.7 %copy-start.10 = (bf16[384,768]{1,0:T(8,128)(2,1)S(1)}, bf16[384,768]{1,0:T(8,128)(2,1)}, u32[]{:S(2)}) copy-start(bf16[384,768]{1,0:T(8,128)(2,1)} %copy-done.7) | copy-start | bytes 1769476
  344.3 141.4 %all-reduce.4.cloned.1.call-start = ((), (), s32[]{:S(2)}) async-start(), calls=%async_computation.9 | async-start | bytes 294912 | tf_op jit(solution)/shard_map/psum | solution.py:133
  462.6 26.2 %copy-start.1 = (bf16[1536,768]{1,0:T(8,128)(2,1)S(1)}, bf16[1536,768]{1,0:T(8,128)(2,1)}, u32[]{:S(2)}) copy-start(bf16[1536,768]{1,0:T(8,128)(2,1)} %param.16) | copy-start | bytes 7077892
Sparse Core Ops, SparseCore 0:
  10.9 71.9 all-gather.6
  85.7 67.6 all-gather.10
  156.3 67.6 all-gather.8
  290.6 50.5 reduce-scatter.3
  344.7 57.1 reduce-scatter.7
  405.3 57.1 reduce-scatter.5
  464.9 20.7 all-reduce.3
where the time goes:
time: 496 us
  waiting for transfers between devices  318 us (64%)
  blocking collectives  76 us (15%)
  matrix products  56.1 us (11%)
  local copies, waits for them, and re-layouts  15.8 us (3%)
  between operations  15.7 us (3%)
  other arithmetic  13.5 us (3%)
    all_gather x1, waiting for transfers between devices, encode_whole(): lax.all_gather(w_up, ('group', 'seq'), axis=1, tiled=True)  70.6 us
    all_gather x1, waiting for transfers between devices, encode_whole(): lax.all_gather(w_down_t, ('group', 'seq'), axis=1, tiled=True)  63.1 us
    reduce_scatter x1, waiting for transfers between devices, shards(): lax.psum_scatter(part_value.astype(jnp.bfloat16), 'seq', scatter_dimensio...  60.7 us
    reduce_scatter x1, waiting for transfers between devices, shards(): lax.psum_scatter(part_out.astype(jnp.bfloat16), 'seq', scatter_dimension=...  57.5 us
    unnamed x1, blocking collectives  35.4 us
    all_gather x1, waiting for transfers between devices, encode_whole(): lax.all_gather(w_gate, ('group', 'seq'), axis=1, tiled=True)  31.1 us
    all_gather x1, blocking collectives, shards(): lax.all_gather(own_keys, 'seq', axis=0, tiled=True)  21.6 us
    psum x1, waiting for transfers between devices, shards(): lax.psum(rows_value.astype(jnp.bfloat16), 'group').astype(jnp.float32)  20.2 us
  transfers between devices with their start and end apart: 7, of which 7 were waited for; matrix products, arithmetic and copies ran while one was open for 7% of the time, Pallas kernels for 0%

commit v1 on v0

v1 whole, which is shorter than its diff:
```python
import math

import jax
import jax.numpy as jnp
from jax import lax
from jax.sharding import PartitionSpec as P

HEADS = 16
HEAD = 48
RATE = 16
BLOCK = 32

epsilon = 1e-06
BOTH = ("group", "seq")


def rms_rows(values):
    values = values.astype(jnp.float32)
    return values * lax.rsqrt(jnp.mean(values * values, axis=-1, keepdims=True) + epsilon)


def mm(left, right):
    return jnp.dot(left, right, preferred_element_type=jnp.float32)


def mm_nt(left, right):
    return lax.dot_general(
        left, right, (((1,), (1,)), ((), ())), preferred_element_type=jnp.float32
    )


def mm_tn(left, right):
    return lax.dot_general(
        left, right, (((0,), (0,)), ((), ())), preferred_element_type=jnp.float32
    )


class Moves:
    def __init__(self, groups, seqs):
        self.groups, self.seqs = groups, seqs
        self.rests = seqs // 4
        self.ring = (groups // 2) * self.rests

    def seq_xor(self, value, bit):
        return lax.ppermute(value, "seq", [(s, s ^ bit) for s in range(self.seqs)])

    def core(self, value):
        return self.seq_xor(value, 1)

    def x(self, value):
        return self.seq_xor(value, 2)

    def y(self, value):
        return lax.ppermute(value, "group", [(g, g ^ 1) for g in range(self.groups)])

    def rest_shift(self, value, step):
        pairs = []
        for s in range(self.seqs):
            target = ((s // 4 + step) % self.rests) * 4 + s % 4
            pairs.append((s, target))
        return lax.ppermute(value, "seq", pairs)

    def ring_next(self, value):
        pairs = []
        for g in range(self.groups):
            for s in range(self.seqs):
                place = ((g // 2) * self.rests + s // 4 + 1) % self.ring
                to_g = (place // self.rests) * 2 + g % 2
                to_s = (place % self.rests) * 4 + s % 4
                pairs.append((g * self.seqs + s, to_g * self.seqs + to_s))
        return lax.ppermute(value, BOTH, pairs)


def take(array, index, axis):
    return lax.dynamic_index_in_dim(array, index, axis, keepdims=False)


def ffn_term(rows, chunks, hidden):
    gate = jnp.concatenate([c[:hidden] for c in chunks], axis=0)
    upward = jnp.concatenate([c[hidden : 2 * hidden] for c in chunks], axis=0)
    down = jnp.concatenate([c[2 * hidden :] for c in chunks], axis=0)
    active = (jax.nn.silu(mm_nt(rows, gate)) * mm_nt(rows, upward)).astype(jnp.bfloat16)
    return mm(active, down)


def flip_blocks(rows):
    width = rows.shape[1]
    return rows.reshape(-1, BLOCK, width)[::-1].reshape(-1, width)


def encode(moves, tile_rows, row_count, w_gate, w_up, w_down_t, w_embed):
    hidden = w_gate.shape[1]
    half = tile_rows.shape[0] // 2
    spare = half - BLOCK
    chunk = jnp.concatenate([w_gate.T, w_up.T, w_down_t.T], axis=0)
    ringed = [chunk]
    for _ in range(moves.ring - 1):
        ringed.append(moves.ring_next(ringed[-1]))
    chunks = [[c, moves.core(c)] for c in ringed]
    extra = moves.y(flip_blocks(tile_rows[half : half + spare]))
    own_blocks = (row_count + BLOCK - 1) // BLOCK
    kept = (1 + jnp.arange(spare) // BLOCK) < own_blocks
    level = jnp.concatenate(
        [tile_rows[:BLOCK], jnp.where(kept[:, None], tile_rows[BLOCK:half], extra)], axis=0
    )
    normed = rms_rows(level).astype(jnp.bfloat16)
    part = half // 2
    first, second = normed[:part], normed[part:]
    first = jnp.concatenate([first, moves.x(first)], axis=0)
    second = jnp.concatenate([second, moves.y(second)], axis=0)
    rows = jnp.concatenate([first, second, moves.y(first), moves.x(second)], axis=0)
    early = [c for pair in chunks[:-1] for c in pair]
    mixed = ffn_term(rows, chunks[-1], hidden)
    if early:
        mixed = mixed + ffn_term(rows, early, hidden)
    low = mixed.astype(jnp.bfloat16)
    first = mixed[: 2 * part] + moves.y(low[4 * part : 6 * part]).astype(jnp.float32)
    second = mixed[2 * part : 4 * part] + moves.x(low[6 * part :]).astype(jnp.float32)
    first = first[:part] + moves.x(first[part:].astype(jnp.bfloat16)).astype(jnp.float32)
    second = second[:part] + moves.y(second[part:].astype(jnp.bfloat16)).astype(jnp.float32)
    mixed = jnp.concatenate([first, second], axis=0)
    embedded = rms_rows(level.astype(jnp.float32) + mixed).astype(jnp.bfloat16)
    slide_part = mm(embedded, w_embed).astype(jnp.bfloat16)
    back = moves.y(flip_blocks(slide_part[BLOCK:]))
    return jnp.concatenate([slide_part, back], axis=0)


def reduce_grads(moves, part_value, part_out):
    seqs = moves.seqs
    features, width = part_value.shape
    seq_index, group_index = lax.axis_index("seq"), lax.axis_index("group")
    core_bit, x_bit, rest = seq_index % 2, (seq_index // 2) % 2, seq_index // 4
    y_bit = group_index % 2
    share = features // seqs // 2
    low = jnp.bfloat16

    def halve(array, bit, axis, move):
        kept = take(array, bit, axis).astype(jnp.float32)
        return kept + move(take(array, 1 - bit, axis).astype(low)).astype(jnp.float32)

    def split(array):
        return array.reshape(moves.rests, 2, 2, 2, share, width)

    value = halve(split(part_value), core_bit, 2, moves.core)
    out = halve(split(part_out), core_bit, 2, moves.core)
    value = halve(value, x_bit, 1, moves.x)
    out = halve(out, y_bit, 2, moves.y)
    value = halve(value, y_bit, 1, moves.y)
    out = halve(out, x_bit, 1, moves.x)
    both = jnp.concatenate([value, out], axis=2)
    total = take(both, rest, 0)
    sent = both.astype(low)
    for step in range(1, moves.rests):
        block = take(sent, (rest + step) % moves.rests, 0)
        total = total + moves.rest_shift(block, step).astype(jnp.float32)
    total = total.astype(low)
    if moves.groups > 2:
        fellows = [list(range(bit, moves.groups, 2)) for bit in range(2)]
        everyone = lax.all_gather(total, "group", axis=0, axis_index_groups=fellows)
        total = jnp.sum(everyone.astype(jnp.float32), axis=0).astype(low)
    other = moves.y(total)
    top = jnp.where(y_bit == 0, total, other)
    bottom = jnp.where(y_bit == 0, other, total)
    full = jnp.concatenate([top, bottom], axis=0).astype(jnp.float32)
    return full[:, :width], full[:, width:]


def gather_far(moves, block):
    bit = moves.seqs // 2
    while bit >= 1:
        block = jnp.concatenate([block, moves.seq_xor(block, bit)], axis=0)
        bit //= 2
    return block


def shards(
    tiles, tile_counts, w_gate, w_up, w_down_t, w_embed, w_query, w_key, w_value, w_out, cotangent
):
    moves = Moves(lax.axis_size("group"), lax.axis_size("seq"))
    tile_rows = tiles[0]
    row_count = tile_counts[0, 0]
    seq_len = tile_rows.shape[0]
    live = seq_len - BLOCK
    is_valid = jnp.arange(live) < row_count
    grad_y = jnp.where(is_valid[:, None], cotangent[0, :live], jnp.zeros((), cotangent.dtype))
    grad_att = mm_nt(grad_y, w_out).astype(jnp.bfloat16)

    slide_tok = encode(moves, tile_rows, row_count, w_gate, w_up, w_down_t, w_embed)
    score_scale = 1.0 / math.sqrt(HEAD)
    slide_normed = rms_rows(slide_tok).astype(jnp.bfloat16)
    width = slide_normed.shape[1]
    dilated = seq_len // RATE
    held = live // RATE
    far_count = ((row_count + RATE - 1) // RATE).astype(jnp.bfloat16)
    far_rows = gather_far(
        moves,
        jnp.concatenate(
            [
                slide_normed.reshape(held, RATE, width)[:, 0],
                jnp.full((dilated - held, width), far_count, jnp.bfloat16),
            ],
            axis=0,
        ),
    )
    far_blocks = far_rows.reshape(moves.seqs, dilated, width)
    far_valid = (
        jnp.arange(dilated)[None, :] < far_blocks[:, dilated - 1, :1].astype(jnp.float32)
    ).reshape(-1)
    queries = mm(slide_normed, w_query).astype(jnp.bfloat16)
    all_rows = jnp.concatenate([slide_normed, far_rows], axis=0)
    key_set = mm(all_rows, w_key).astype(jnp.bfloat16).reshape(-1, HEADS, HEAD)
    value_set = mm(all_rows, w_value).astype(jnp.bfloat16).reshape(-1, HEADS, HEAD)
    key_valid = jnp.concatenate([is_valid, far_valid])
    query_heads = queries.reshape(live, HEADS, HEAD)
    scores = (
        jnp.einsum("phd,jhd->hpj", query_heads, key_set, preferred_element_type=jnp.float32)
        * score_scale
    )
    scores = jnp.where(key_valid[None, None, :], scores, -1e30)
    row_max = jnp.max(scores, axis=2, keepdims=True)
    exponent = jnp.exp(scores - row_max)
    weights = (exponent / jnp.sum(exponent, axis=2, keepdims=True)).astype(jnp.bfloat16)
    attended = jnp.einsum("hpj,jhd->phd", weights, value_set, preferred_element_type=jnp.float32)
    attended = attended.reshape(live, width).astype(jnp.bfloat16)
    output = slide_tok.astype(jnp.float32) + mm(attended, w_out)
    slide_out = jnp.where(is_valid[:, None], output, 0.0).astype(jnp.bfloat16)
    slide_out = jnp.concatenate([slide_out, jnp.zeros((BLOCK, width), jnp.bfloat16)], axis=0)
    part_out = mm_tn(attended, grad_y)
    grad_heads = grad_att.reshape(live, HEADS, HEAD)
    grad_values = jnp.einsum(
        "hpj,phd->jhd", weights, grad_heads, preferred_element_type=jnp.float32
    )
    grad_values = grad_values.reshape(-1, width).astype(jnp.bfloat16)
    part_value = mm_tn(all_rows, grad_values)
    grad_value, grad_out = reduce_grads(moves, part_value, part_out)
    return (slide_out[None], grad_value, grad_out)


def solution(mesh):
    placed = (
        P("group", "seq", None),
        P("group", "seq"),
        P(None, ("group", "seq")),
        P(None, ("group", "seq")),
        P(None, ("group", "seq")),
        P(),
        P(),
        P(),
        P(),
        P(),
        P("group", "seq", None),
    )
    return jax.shard_map(
        shards,
        mesh=mesh,
        in_specs=placed,
        out_specs=(P("group", "seq", None), P("seq", None), P("seq", None)),
        check_vma=False,
    )
```

time: 496 us -> 206 us (0.42)
  waiting for transfers between devices: 318 us -> 82.1 us
  blocking collectives: 76 us -> 0 us
  starting transfers between devices: 0.5 us -> 31.5 us
  between operations: 15.7 us -> 1.94 us
  local copies, waits for them, and re-layouts: 15.8 us -> 22.6 us
    all_gather x3 -> x0, waiting for transfers between devices: 165 us -> none  [the longest x1 70.6 us: encode_whole(): lax.all_gather(w_up, ('group', 'seq'), axis=1, tiled=True)]
    reduce_scatter x3 -> x0, waiting for transfers between devices: 131 us -> none  [the longest x1 60.7 us: shards(): lax.psum_scatter(part_value.astype(jnp.bfloat16), 'seq', scatter_dimensio...]
    ppermute x0 -> x31, waiting for transfers between devices: none -> 82.1 us  [the longest x9 42.6 us: y(): lax.ppermute(value, 'group', [(g, g ^ 1) for g in range(self.groups)])]
    all_gather x2 -> x0, blocking collectives: 40.6 us -> none  [the longest x1 21.6 us: shards(): lax.all_gather(own_keys, 'seq', axis=0, tiled=True)]
    unnamed x1 -> x0, blocking collectives: 35.4 us -> none
    ppermute x0 -> x31, starting transfers between devices: none -> 31.5 us  [the longest x9 12.9 us: y(): lax.ppermute(value, 'group', [(g, g ^ 1) for g in range(self.groups)])]
    psum x1 -> x0, waiting for transfers between devices: 20.2 us -> none  [shards(): lax.psum(rows_value.astype(jnp.bfloat16), 'group').astype(jnp.float32)]
    slice x4 -> x13, local copies, waits for them, and re-layouts: 0.22 us -> 6.96 us  [the longest x2 3.81 us: ffn_term(): upward = jnp.concatenate([c[hidden:2 * hidden] for c in chunks], axis=0)]
  transfers between devices with their start and end apart: 7 -> 31, of which waited for: 7 -> 20; matrix products, arithmetic and copies ran while one was open for 7% -> 17% of each run, Pallas kernels for 0% -> 0%
where the time goes in v1:
time: 206 us
  waiting for transfers between devices  82.1 us (40%)
  matrix products  52.3 us (25%)
  starting transfers between devices  31.5 us (15%)
  local copies, waits for them, and re-layouts  22.6 us (11%)
  other arithmetic  15.4 us (7%)
    ppermute x9, waiting for transfers between devices, y(): lax.ppermute(value, 'group', [(g, g ^ 1) for g in range(self.groups)])  42.6 us
    dot_general x7, matrix products, mm(): return jnp.dot(left, right, preferred_element_type=jnp.float32)  25.3 us
    ppermute x16, waiting for transfers between devices, seq_xor(): return lax.ppermute(value, 'seq', [(s, s ^ bit) for s in range(self.seqs)])  21.1 us
    ppermute x3, waiting for transfers between devices, ring_next(): return lax.ppermute(value, BOTH, pairs)  15.5 us
    ppermute x9, starting transfers between devices, y(): lax.ppermute(value, 'group', [(g, g ^ 1) for g in range(self.groups)])  12.9 us
    sub x1, matrix products, shards(): exponent = jnp.exp(scores - row_max)  10.8 us
    ppermute x16, starting transfers between devices, seq_xor(): return lax.ppermute(value, 'seq', [(s, s ^ bit) for s in range(self.seqs)])  10.1 us
    dot_general x3, matrix products, mm_nt(): lax.dot_general(left, right, (((1,), (1,)), ((), ())), preferred_element_...  7.61 us
  transfers between devices with their start and end apart: 31, of which 20 were waited for; matrix products, arithmetic and copies ran while one was open for 17% of the time, Pallas kernels for 0%

profile of v1, /device:TPU:0, one launch (start us, length us, event | category | flops | bytes accessed | tf_op | source)
XLA Modules:
  0.0 205.8 jit_solution(10917387725955664249)
XLA Ops:
  0.7 2.1 %pad_maximum_fusion.4 = bf16[192,1536]{1,0:T(8,128)(2,1)} fusion(bf16[64,1536]{1,0:T(8,128)(2,1)} %bitcast.135, bf16[64,1536]{1,0:T(8,128)(2,1)} %bitcast.137, bf16[64,1536]{1,0:T(8,128)(2,1)} %bitcast.136), kind=kLoop, calls=%fused_computation.50 | loop fusion | flops 1769472 | bytes 1179648 | tf_op jit(solution)/shard_map/concatenate | solution.py:95
  2.8 3.1 %collective-permute-start.5 = (bf16[192,1536]{1,0:T(8,128)(2,1)}, bf16[192,1536]{1,0:T(8,128)(2,1)}, u32[]{:S(2)}, u32[]{:S(2)}) collective-permute-start(bf16[192,1536]{1,0:T(8,128)(2,1)} %pad_maximum_fusion.4), channel_id=1, source_target_pairs={{0,4},{1,5},{2,6},{3,7},{4,8},{5,9},{6,10},{7,11},{8,12},{9,13},{1... | collective-permute-start | bytes 1769480 | tf_op jit(solution)/shard_map/ppermute | solution.py:71
  6.7 1.5 collective-permute-start
  8.8 0.9 slice_bitcast_fusion
  10.5 10.1 %collective-permute-done = bf16[160,1536]{1,0:T(8,128)(2,1)} collective-permute-done((bf16[160,1536]{1,0:T(8,128)(2,1)}, bf16[160,1536]{1,0:T(8,128)(2,1)}, u32[]{:S(2)}, u32[]{:S(2)}) %collective-permute-start) | collective-permute-done | bytes 491552 | tf_op jit(solution)/shard_map/ppermute | solution.py:54
  20.6 1.3 bitcast_select_fusion.2
  22.4 1.6 collective-permute-start.1
  23.9 1.5 collective-permute-start.2
  25.4 1.6 collective-permute-start.6
  27.0 1.2 slice_dynamic-update-slice_fusion.14
  28.2 1.2 slice_dynamic-update-slice_fusion.13
  29.4 1.6 collective-permute-done.1
  31.0 1.6 collective-permute-start.3
  32.7 1.6 collective-permute-start.4
  34.3 7.5 %collective-permute-done.6 = bf16[192,1536]{1,0:T(8,128)(2,1)S(1)} collective-permute-done((bf16[192,1536]{1,0:T(8,128)(2,1)}, bf16[192,1536]{1,0:T(8,128)(2,1)S(1)}, u32[]{:S(2)}, u32[]{:S(2)}) %collective-permute-start.6) | collective-permute-done | bytes 589856 | tf_op jit(solution)/shard_map/ppermute | solution.py:71
  41.9 3.3 %collective-permute-done.3 = bf16[192,1536]{1,0:T(8,128)(2,1)S(1)} collective-permute-done((bf16[192,1536]{1,0:T(8,128)(2,1)S(1)}, bf16[192,1536]{1,0:T(8,128)(2,1)S(1)}, u32[]{:S(2)}, u32[]{:S(2)}) %collective-permute-start.3) | collective-permute-done | bytes 589856 | tf_op jit(solution)/shard_map/ppermute | solution.py:54
  45.3 1.2 collective-permute-done.4
  46.6 2.5 %fusion.78 = f32[768,384]{1,0:T(8,128)} fusion(bf16[768,1536]{1,0:T(8,128)(2,1)S(1)} %constant_dynamic-update-slice_fusion, bf16[384,1536]{1,0:T(8,128)(2,1)S(1)} %get-tuple-element.13), kind=kOutput, calls=%fused_computation.167 | convolution fusion | flops 905969664 | bytes 4718592 | tf_op jit(solution)/shard_map/dot_general | solution.py:27
  49.1 8.0 %collective-permute-done.7 = bf16[192,1536]{1,0:T(8,128)(2,1)} collective-permute-done((bf16[192,1536]{1,0:T(8,128)(2,1)S(1)}, bf16[192,1536]{1,0:T(8,128)(2,1)}, u32[]{:S(2)}, u32[]{:S(2)}) %collective-permute-start.7) | collective-permute-done | bytes 589856 | tf_op jit(solution)/shard_map/ppermute | solution.py:71
  57.2 1.8 fusion.68
  59.0 7.5 %fusion.12 = f32[768,1536]{1,0:T(8,128)} fusion(bf16[384,1536]{1,0:T(8,128)(2,1)} %copy-done.19, f32[768,384]{1,0:T(8,128)} %fusion.78, bf16[768,1536]{1,0:T(8,128)(2,1)} %copy-done.5, bf16[384,1536]{1,0:T(8,128)(2,1)} %copy-done.20), kind=kOutput, calls=%fused_computation.40 | convolution fusion | flops 1813708800 | bytes 10616832 | tf_op jit(solution)/shard_map/dot_general | solution.py:23
  66.5 2.0 fusion.69
  68.5 3.2 %fusion.24 = f32[768,128]{1,0:T(8,128)} fusion(bf16[768,1536]{1,0:T(8,128)(2,1)} %copy-done.5, bf16[64,1536]{1,0:T(8,128)(2,1)S(1)} %get-tuple-element.12, bf16[64,1536]{1,0:T(8,128)(2,1)S(1)} %copy-done.17), kind=kOutput, calls=%fused_computation.68 | convolution fusion | flops 302776320 | bytes 3145728 | tf_op jit(solution)/shard_map/dot_general | solution.py:27
  71.7 8.9 %fusion.72 = (bf16[768,1536]{1,0:T(8,128)(2,1)}, f32[768,1536]{1,0:T(8,128)}) fusion(f32[768,1536]{1,0:T(8,128)} %fusion.12, bf16[64,1536]{1,0:T(8,128)(2,1)} %get-tuple-element.11, bf16[64,1536]{1,0:T(8,128)(2,1)S(1)} %get-tuple-element.8, f32[768,128]{1,0:T(8,128)} %fusion.24, bf16[768,1536]{1,0:T(8,128)(2,1)} %copy-done.5, ...), kind=kOutput, calls=%fused_computation.164 | convolution fusion | flops 608501760 | bytes 15335424 | tf_op jit(solution)/shard_map/dot_general | solution.py:23
  80.5 1.3 fusion.67
  82.9 14.7 %collective-permute-done.12 = bf16[192,1536]{1,0:T(8,128)(2,1)S(1)} collective-permute-done((bf16[192,1536]{1,0:T(8,128)(2,1)S(1)}, bf16[192,1536]{1,0:T(8,128)(2,1)S(1)}, u32[]{:S(2)}, u32[]{:S(2)}) %collective-permute-start.12) | collective-permute-done | bytes 589856 | tf_op jit(solution)/shard_map/ppermute | solution.py:54
  97.9 2.0 slice_add_fusion.1
  100.5 1.6 collective-permute-start.15
  102.1 6.2 %collective-permute-done.13 = bf16[96,1536]{1,0:T(8,128)(2,1)S(1)} collective-permute-done((bf16[96,1536]{1,0:T(8,128)(2,1)S(1)}, bf16[96,1536]{1,0:T(8,128)(2,1)S(1)}, u32[]{:S(2)}, u32[]{:S(2)}) %collective-permute-start.13) | collective-permute-done | bytes 294944 | tf_op jit(solution)/shard_map/ppermute | solution.py:45
  109.7 1.5 collective-permute-start.16
  111.3 4.7 %collective-permute-done.16 = bf16[160,768]{1,0:T(8,128)(2,1)S(1)} collective-permute-done((bf16[160,768]{1,0:T(8,128)(2,1)S(1)}, bf16[160,768]{1,0:T(8,128)(2,1)S(1)}, u32[]{:S(2)}, u32[]{:S(2)}) %collective-permute-start.16) | collective-permute-done | bytes 245792 | tf_op jit(solution)/shard_map/ppermute | solution.py:54
  116.7 4.8 %collective-permute-done.17 = bf16[24,768]{1,0:T(8,128)(2,1)S(1)} collective-permute-done((bf16[24,768]{1,0:T(8,128)(2,1)S(1)}, bf16[24,768]{1,0:T(8,128)(2,1)S(1)}, u32[]{:S(2)}, u32[]{:S(2)}) %collective-permute-start.17) | collective-permute-done | bytes 36896 | tf_op jit(solution)/shard_map/ppermute | solution.py:45
  121.6 4.3 %collective-permute-done.18 = bf16[48,768]{1,0:T(8,128)(2,1)S(1)} collective-permute-done((bf16[48,768]{1,0:T(8,128)(2,1)S(1)}, bf16[48,768]{1,0:T(8,128)(2,1)S(1)}, u32[]{:S(2)}, u32[]{:S(2)}) %collective-permute-start.18) | collective-permute-done | bytes 73760 | tf_op jit(solution)/shard_map/ppermute | solution.py:45
  126.0 1.6 collective-permute-start.19
  127.6 1.9 convolution_convert_fusion.4
  129.5 1.1 copy.31
  131.8 1.9 convolution_convert_fusion.5
  133.6 1.1 copy.28
  135.8 2.3 %convolution_convert_fusion.1 = bf16[736,768]{1,0:T(8,128)(2,1)S(1)} fusion(bf16[736,768]{1,0:T(8,128)(2,1)S(1)} %concatenate.92, bf16[768,768]{1,0:T(8,128)(2,1)} %param.18), kind=kOutput, calls=%fused_computation.14 | convolution fusion | flops 868786176 | bytes 3440640 | tf_op jit(solution)/shard_map/dot_general | solution.py:23
  138.8 3.4 %convolution_convert_fusion.2 = bf16[736,768]{1,0:T(8,128)(2,1)} fusion(bf16[736,768]{1,0:T(8,128)(2,1)S(1)} %concatenate.92, bf16[768,768]{1,0:T(8,128)(2,1)} %param.19), kind=kOutput, calls=%fused_computation.15 | convolution fusion | flops 868786176 | bytes 3440640 | tf_op jit(solution)/shard_map/dot_general | solution.py:23
  142.2 1.6 copy.26
  143.7 10.8 %fusion.75 = (f32[16,352]{1,0:T(8,128)S(1)}, f32[16,352,736]{2,1,0:T(8,128)}) fusion(bf16[352,16,48]{0,2,1:T(8,128)(2,1)} %bitcast.139, bf16[736,16,48]{0,2,1:T(8,128)(2,1)S(1)} %bitcast.132, pred[736]{0:T(1024)(128)(4,1)S(1)} %pad_add_fusion), kind=kOutput, calls=%fused_computation.165 | convolution fusion | flops 414515936 | bytes 18275040 | tf_op jit(solution)/shard_map/sub | solution.py:221
  154.5 6.8 %divide_convert_fusion = bf16[16,352,736]{2,1,0:T(8,128)(2,1)S(1)} fusion(f32[16,352,736]{2,1,0:T(8,128)} %get-tuple-element.41, f32[16,352]{1,0:T(8,128)S(1)} %get-tuple-element.40), kind=kLoop, calls=%fused_computation.1 | loop fusion | flops 8290304 | bytes 24893440 | tf_op jit(solution)/shard_map/convert_element_type | solution.py:222
  161.3 2.5 %convolution_convert_fusion.3 = bf16[16,48,352]{2,1,0:T(8,128)(2,1)S(1)} fusion(bf16[736,16,48]{0,2,1:T(8,128)(2,1)S(1)} %bitcast.124, bf16[16,352,736]{2,1,0:T(8,128)(2,1)S(1)} %divide_convert_fusion), kind=kOutput, calls=%fused_computation.18 | convolution fusion | flops 398204928 | bytes 9961472 | tf_op jit(solution)/shard_map/hpj,jhd->phd/dot_general | solution.py:223
  164.6 0.9 fusion.17
  165.5 0.9 fusion.14
  166.9 2.6 %convolution_convert_fusion = bf16[16,48,736]{2,1,0:T(8,128)(2,1)} fusion(bf16[352,16,48]{0,2,1:T(8,128)(2,1)S(1)} %bitcast.126, bf16[16,352,736]{2,1,0:T(8,128)(2,1)S(1)} %divide_convert_fusion), kind=kOutput, calls=%fused_computation.13 | convolution fusion | flops 398499840 | bytes 9961472 | tf_op jit(solution)/shard_map/hpj,phd->jhd/dot_general | solution.py:230
  169.4 1.4 copy.30
  170.9 2.7 %fusion.79 = f32[4,2,2,2,24,768]{5,4,3,2,1,0:T(8,128)S(1)} fusion(bf16[4,2,2,2,24,736]{5,4,3,2,1,0:T(8,128)(2,1)} %bitcast.133, bf16[736,768,1,1,1,1]{0,1,5,4,3,2:T(8,128)(2,1)} %bitcast.127), kind=kOutput, calls=%fused_computation.168 | convolution fusion | flops 868220928 | bytes 4620288 | tf_op jit(solution)/shard_map/dot_general | solution.py:33
  173.6 1.4 copy-done.10
  175.5 1.3 bitcast_add_fusion
  176.9 1.5 collective-permute-start.25
  178.6 1.6 collective-permute-start.22
  180.2 5.9 %collective-permute-done.25 = bf16[4,2,24,768]{3,2,0,1:T(8,128)(2,1)S(1)} collective-permute-done((bf16[4,2,24,768]{3,2,0,1:T(8,128)(2,1)S(1)}, bf16[4,2,24,768]{3,2,0,1:T(8,128)(2,1)S(1)}, u32[]{:S(2)}, u32[]{:S(2)}) %collective-permute-start.25) | collective-permute-done | bytes 294944 | tf_op jit(solution)/shard_map/ppermute | solution.py:54
  186.1 1.6 collective-permute-start.26
  187.8 1.5 collective-permute-start.23
  189.4 2.0 collective-permute-done.26
  191.4 1.6 collective-permute-done.23
  193.4 3.6 %collective-permute-start.29 = (bf16[24,1536]{1,0:T(8,128)(2,1)S(1)}, bf16[24,1536]{1,0:T(8,128)(2,1)S(1)}, u32[]{:S(2)}, u32[]{:S(2)}) collective-permute-start(bf16[24,1536]{1,0:T(8,128)(2,1)S(1)} %get-tuple-element.34), channel_id=1, source_target_pairs={{0,12},{1,13},{2,14},{3,15},{4,0},{5,1},{6,2},{7,3},{8,4},{9,5},{1... | collective-permute-start | bytes 221192 | tf_op jit(solution)/shard_map/ppermute | solution.py:61
  197.7 1.8 collective-permute-done.27
  199.5 1.0 collective-permute-done.28
  200.6 1.5 collective-permute-start.30
  202.1 0.9 pad_bitcast_fusion
  202.9 2.0 collective-permute-done.30
  (142 shorter events, 13.5 us)
Async XLA Ops:
  0.6 108.3 %copy-start = (bf16[1536,768]{1,0:T(8,128)(2,1)S(1)}, bf16[1536,768]{1,0:T(8,128)(2,1)}, u32[]{:S(2)}) copy-start(bf16[1536,768]{1,0:T(8,128)(2,1)} %param.16) | copy-start | bytes 7077892
  0.6 5.2 %slice-start = ((bf16[1,384,1536]{2,1,0:T(8,128)(2,1)}), bf16[1,160,1536]{2,1,0:T(8,128)(2,1)S(1)}, s32[]{:S(2)}) async-start(bf16[1,384,1536]{2,1,0:T(8,128)(2,1)} %param.11), calls=%async_computation | async-start | bytes 983040 | tf_op jit(solution)/shard_map/slice | solution.py:100
  2.8 7.0 %copy-start.12 = (bf16[1536,64]{0,1:T(8,128)(2,1)S(1)}, bf16[1536,64]{0,1:T(8,128)(2,1)}, u32[]{:S(2)}) copy-start(bf16[1536,64]{0,1:T(8,128)(2,1)} %param.15) | copy-start | bytes 589828
  2.8 7.7 %copy-start.13 = (bf16[1536,64]{0,1:T(8,128)(2,1)S(1)}, bf16[1536,64]{0,1:T(8,128)(2,1)}, u32[]{:S(2)}) copy-start(bf16[1536,64]{0,1:T(8,128)(2,1)} %param.13) | copy-start | bytes 589828
  2.8 7.7 %copy-start.14 = (bf16[1536,64]{0,1:T(8,128)(2,1)S(1)}, bf16[1536,64]{0,1:T(8,128)(2,1)}, u32[]{:S(2)}) copy-start(bf16[1536,64]{0,1:T(8,128)(2,1)} %param.14) | copy-start | bytes 589828
  2.8 22.7 %collective-permute-start.5 = (bf16[192,1536]{1,0:T(8,128)(2,1)}, bf16[192,1536]{1,0:T(8,128)(2,1)}, u32[]{:S(2)}, u32[]{:S(2)}) collective-permute-start(bf16[192,1536]{1,0:T(8,128)(2,1)} %pad_maximum_fusion.4), channel_id=1, source_target_pairs={{0,4},{1,5},{2,6},{3,7},{4,8},{5,9},{6,10},{7,11},{8,12},{9,13},{1... | collective-permute-start | bytes 1769480 | tf_op jit(solution)/shard_map/ppermute | solution.py:71
  5.8 21.2 %collective-permute-start.9 = (bf16[192,1536]{1,0:T(8,128)(2,1)}, bf16[192,1536]{1,0:T(8,128)(2,1)}, u32[]{:S(2)}, u32[]{:S(2)}) collective-permute-start(bf16[192,1536]{1,0:T(8,128)(2,1)} %pad_maximum_fusion.4), channel_id=1, source_target_pairs={{0,1},{1,0},{2,3},{3,2},{4,5},{5,4},{6,7},{7,6},{8,9},{9,8},{10,11... | collective-permute-start | bytes 1769480 | tf_op jit(solution)/shard_map/ppermute | solution.py:45
  6.7 13.9 %collective-permute-start = (bf16[160,1536]{1,0:T(8,128)(2,1)}, bf16[160,1536]{1,0:T(8,128)(2,1)}, u32[]{:S(2)}, u32[]{:S(2)}) collective-permute-start(bf16[160,1536]{1,0:T(8,128)(2,1)} %bitcast.140), channel_id=1, source_target_pairs={{0,16},{16,0},{1,17},{17,1},{2,18},{18,2},{3,19},{19,3},{4,20},{20... | collective-permute-start | bytes 1474568 | tf_op jit(solution)/shard_map/ppermute | solution.py:54
  22.1 4.9 %copy-start.18 = (bf16[384,1536]{1,0:T(8,128)(2,1)S(1)}, bf16[384,1536]{1,0:T(8,128)(2,1)}, u32[]{:S(2)}) copy-start(bf16[384,1536]{1,0:T(8,128)(2,1)} %constant_dynamic-update-slice_fusion.8) | copy-start | bytes 3538948
  22.4 8.6 %collective-permute-start.1 = (bf16[96,1536]{1,0:T(8,128)(2,1)S(1)}, bf16[96,1536]{1,0:T(8,128)(2,1)S(1)}, u32[]{:S(2)}, u32[]{:S(2)}) collective-permute-start(bf16[96,1536]{1,0:T(8,128)(2,1)S(1)} %get-tuple-element.30), channel_id=1, source_target_pairs={{0,2},{1,3},{2,0},{3,1},{4,6},{5,7},{6,4},{7,5},{8,10},{9,11},{10,... | collective-permute-start | bytes 884744 | tf_op jit(solution)/shard_map/ppermute | solution.py:45
  23.9 8.7 %collective-permute-start.2 = (bf16[96,1536]{1,0:T(8,128)(2,1)S(1)}, bf16[96,1536]{1,0:T(8,128)(2,1)S(1)}, u32[]{:S(2)}, u32[]{:S(2)}) collective-permute-start(bf16[96,1536]{1,0:T(8,128)(2,1)S(1)} %get-tuple-element.28), channel_id=1, source_target_pairs={{0,16},{16,0},{1,17},{17,1},{2,18},{18,2},{3,19},{19,3},{4,20},{20... | collective-permute-start | bytes 884744 | tf_op jit(solution)/shard_map/ppermute | solution.py:54
  25.4 16.3 %collective-permute-start.6 = (bf16[192,1536]{1,0:T(8,128)(2,1)}, bf16[192,1536]{1,0:T(8,128)(2,1)S(1)}, u32[]{:S(2)}, u32[]{:S(2)}) collective-permute-start(bf16[192,1536]{1,0:T(8,128)(2,1)} %collective-permute-done.5), channel_id=1, source_target_pairs={{0,4},{1,5},{2,6},{3,7},{4,8},{5,9},{6,10},{7,11},{8,12},{9,13},{1... | collective-permute-start | bytes 1769480 | tf_op jit(solution)/shard_map/ppermute | solution.py:71
  27.0 14.8 %collective-permute-start.10 = (bf16[192,1536]{1,0:T(8,128)(2,1)}, bf16[192,1536]{1,0:T(8,128)(2,1)S(1)}, u32[]{:S(2)}, u32[]{:S(2)}) collective-permute-start(bf16[192,1536]{1,0:T(8,128)(2,1)} %collective-permute-done.5), channel_id=1, source_target_pairs={{0,1},{1,0},{2,3},{3,2},{4,5},{5,4},{6,7},{7,6},{8,9},{9,8},{10,11... | collective-permute-start | bytes 1769480 | tf_op jit(solution)/shard_map/ppermute | solution.py:45
  31.0 14.2 %collective-permute-start.3 = (bf16[192,1536]{1,0:T(8,128)(2,1)S(1)}, bf16[192,1536]{1,0:T(8,128)(2,1)S(1)}, u32[]{:S(2)}, u32[]{:S(2)}) collective-permute-start(bf16[192,1536]{1,0:T(8,128)(2,1)S(1)} %pad_maximum_fusion.2), channel_id=1, source_target_pairs={{0,16},{16,0},{1,17},{17,1},{2,18},{18,2},{3,19},{19,3},{4,20},{20... | collective-permute-start | bytes 1769480 | tf_op jit(solution)/shard_map/ppermute | solution.py:54
  32.7 13.8 %collective-permute-start.4 = (bf16[192,1536]{1,0:T(8,128)(2,1)S(1)}, bf16[192,1536]{1,0:T(8,128)(2,1)S(1)}, u32[]{:S(2)}, u32[]{:S(2)}) collective-permute-start(bf16[192,1536]{1,0:T(8,128)(2,1)S(1)} %pad_maximum_fusion.3), channel_id=1, source_target_pairs={{0,2},{1,3},{2,0},{3,1},{4,6},{5,7},{6,4},{7,5},{8,10},{9,11},{10,... | collective-permute-start | bytes 1769480 | tf_op jit(solution)/shard_map/ppermute | solution.py:45
  41.8 15.4 %collective-permute-start.7 = (bf16[192,1536]{1,0:T(8,128)(2,1)S(1)}, bf16[192,1536]{1,0:T(8,128)(2,1)}, u32[]{:S(2)}, u32[]{:S(2)}) collective-permute-start(bf16[192,1536]{1,0:T(8,128)(2,1)S(1)} %collective-permute-done.6), channel_id=1, source_target_pairs={{0,4},{1,5},{2,6},{3,7},{4,8},{5,9},{6,10},{7,11},{8,12},{9,13},{1... | collective-permute-start | bytes 1769480 | tf_op jit(solution)/shard_map/ppermute | solution.py:71
  41.8 4.8 %collective-permute-start.11 = (bf16[192,1536]{1,0:T(8,128)(2,1)S(1)}, bf16[192,1536]{1,0:T(8,128)(2,1)S(1)}, u32[]{:S(2)}, u32[]{:S(2)}) collective-permute-start(bf16[192,1536]{1,0:T(8,128)(2,1)S(1)} %collective-permute-done.6), channel_id=1, source_target_pairs={{0,1},{1,0},{2,3},{3,2},{4,5},{5,4},{6,7},{7,6},{8,9},{9,8},{10,11... | collective-permute-start | bytes 1769480 | tf_op jit(solution)/shard_map/ppermute | solution.py:45
  46.5 2.6 %copy-start.5 = (bf16[768,1536]{1,0:T(8,128)(2,1)}, bf16[768,1536]{1,0:T(8,128)(2,1)S(1)}, u32[]{:S(2)}) copy-start(bf16[768,1536]{1,0:T(8,128)(2,1)S(1)} %constant_dynamic-update-slice_fusion) | copy-start | bytes 7077892
  46.6 2.5 %copy-start.19 = (bf16[384,1536]{1,0:T(8,128)(2,1)}, bf16[384,1536]{1,0:T(8,128)(2,1)S(1)}, u32[]{:S(2)}) copy-start(bf16[384,1536]{1,0:T(8,128)(2,1)S(1)} %get-tuple-element.14) | copy-start | bytes 3538948
  46.6 2.5 %copy-start.20 = (bf16[384,1536]{1,0:T(8,128)(2,1)}, bf16[384,1536]{1,0:T(8,128)(2,1)S(1)}, u32[]{:S(2)}) copy-start(bf16[384,1536]{1,0:T(8,128)(2,1)S(1)} %get-tuple-element.15) | copy-start | bytes 3538948
  57.1 9.3 %collective-permute-start.8 = (bf16[192,1536]{1,0:T(8,128)(2,1)}, bf16[192,1536]{1,0:T(8,128)(2,1)}, u32[]{:S(2)}, u32[]{:S(2)}) collective-permute-start(bf16[192,1536]{1,0:T(8,128)(2,1)} %collective-permute-done.7), channel_id=1, source_target_pairs={{0,1},{1,0},{2,3},{3,2},{4,5},{5,4},{6,7},{7,6},{8,9},{9,8},{10,11... | collective-permute-start | bytes 1769480 | tf_op jit(solution)/shard_map/ppermute | solution.py:45
  66.5 2.0 copy-start.17
  81.8 15.8 %collective-permute-start.12 = (bf16[192,1536]{1,0:T(8,128)(2,1)S(1)}, bf16[192,1536]{1,0:T(8,128)(2,1)S(1)}, u32[]{:S(2)}, u32[]{:S(2)}) collective-permute-start(bf16[192,1536]{1,0:T(8,128)(2,1)S(1)} %get-tuple-element.5), channel_id=1, source_target_pairs={{0,16},{16,0},{1,17},{17,1},{2,18},{18,2},{3,19},{19,3},{4,20},{20... | collective-permute-start | bytes 1769480 | tf_op jit(solution)/shard_map/ppermute | solution.py:54
  82.4 15.5 %collective-permute-start.14 = (bf16[192,1536]{1,0:T(8,128)(2,1)S(1)}, bf16[192,1536]{1,0:T(8,128)(2,1)S(1)}, u32[]{:S(2)}, u32[]{:S(2)}) collective-permute-start(bf16[192,1536]{1,0:T(8,128)(2,1)S(1)} %get-tuple-element.6), channel_id=1, source_target_pairs={{0,2},{1,3},{2,0},{3,1},{4,6},{5,7},{6,4},{7,5},{8,10},{9,11},{10,... | collective-permute-start | bytes 1769480 | tf_op jit(solution)/shard_map/ppermute | solution.py:45
  99.9 8.4 %collective-permute-start.13 = (bf16[96,1536]{1,0:T(8,128)(2,1)S(1)}, bf16[96,1536]{1,0:T(8,128)(2,1)S(1)}, u32[]{:S(2)}, u32[]{:S(2)}) collective-permute-start(bf16[96,1536]{1,0:T(8,128)(2,1)S(1)} %slice.242), channel_id=1, source_target_pairs={{0,2},{1,3},{2,0},{3,1},{4,6},{5,7},{6,4},{7,5},{8,10},{9,11},{10,... | collective-permute-start | bytes 884744 | tf_op jit(solution)/shard_map/ppermute | solution.py:45
  100.5 8.1 %collective-permute-start.15 = (bf16[96,1536]{1,0:T(8,128)(2,1)S(1)}, bf16[96,1536]{1,0:T(8,128)(2,1)S(1)}, u32[]{:S(2)}, u32[]{:S(2)}) collective-permute-start(bf16[96,1536]{1,0:T(8,128)(2,1)S(1)} %slice.241), channel_id=1, source_target_pairs={{0,16},{16,0},{1,17},{17,1},{2,18},{18,2},{3,19},{19,3},{4,20},{20... | collective-permute-start | bytes 884744 | tf_op jit(solution)/shard_map/ppermute | solution.py:54
  109.7 21.9 %copy-start.2 = (bf16[192,768]{1,0:T(8,128)(2,1)}, bf16[192,768]{1,0:T(8,128)(2,1)S(1)}, u32[]{:S(2)}) copy-start(bf16[192,768]{1,0:T(8,128)(2,1)S(1)} %convolution_convert_fusion.6) | copy-start | bytes 884740
  109.7 6.3 %collective-permute-start.16 = (bf16[160,768]{1,0:T(8,128)(2,1)S(1)}, bf16[160,768]{1,0:T(8,128)(2,1)S(1)}, u32[]{:S(2)}, u32[]{:S(2)}) collective-permute-start(bf16[160,768]{1,0:T(8,128)(2,1)S(1)} %bitcast.141), channel_id=1, source_target_pairs={{0,16},{16,0},{1,17},{17,1},{2,18},{18,2},{3,19},{19,3},{4,20},{20... | collective-permute-start | bytes 737288 | tf_op jit(solution)/shard_map/ppermute | solution.py:54
  111.3 16.3 %copy-start.15 = (bf16[1,384,768]{2,1,0:T(8,128)(2,1)S(1)}, bf16[1,384,768]{2,1,0:T(8,128)(2,1)}, u32[]{:S(2)}) copy-start(bf16[1,384,768]{2,1,0:T(8,128)(2,1)} %param.21) | copy-start | bytes 1769476
  116.0 15.6 %copy-start.8 = (bf16[160,768]{1,0:T(8,128)(2,1)}, bf16[160,768]{1,0:T(8,128)(2,1)S(1)}, u32[]{:S(2)}) copy-start(bf16[160,768]{1,0:T(8,128)(2,1)S(1)} %collective-permute-done.16) | copy-start | bytes 737284
  116.6 4.9 %collective-permute-start.17 = (bf16[24,768]{1,0:T(8,128)(2,1)S(1)}, bf16[24,768]{1,0:T(8,128)(2,1)S(1)}, u32[]{:S(2)}, u32[]{:S(2)}) collective-permute-start(bf16[24,768]{1,0:T(8,128)(2,1)S(1)} %concatenate.88), channel_id=1, source_target_pairs={{0,8},{1,9},{2,10},{3,11},{4,12},{5,13},{6,14},{7,15},{8,0},{9,1},... | collective-permute-start | bytes 110600 | tf_op jit(solution)/shard_map/ppermute | solution.py:45
  121.6 4.4 %collective-permute-start.18 = (bf16[48,768]{1,0:T(8,128)(2,1)S(1)}, bf16[48,768]{1,0:T(8,128)(2,1)S(1)}, u32[]{:S(2)}, u32[]{:S(2)}) collective-permute-start(bf16[48,768]{1,0:T(8,128)(2,1)S(1)} %pad_maximum_fusion.7), channel_id=1, source_target_pairs={{0,4},{1,5},{2,6},{3,7},{4,0},{5,1},{6,2},{7,3},{8,12},{9,13},{10,... | collective-permute-start | bytes 221192 | tf_op jit(solution)/shard_map/ppermute | solution.py:45
  126.0 5.2 %collective-permute-start.19 = (bf16[96,768]{1,0:T(8,128)(2,1)S(1)}, bf16[96,768]{1,0:T(8,128)(2,1)S(1)}, u32[]{:S(2)}, u32[]{:S(2)}) collective-permute-start(bf16[96,768]{1,0:T(8,128)(2,1)S(1)} %pad_maximum_fusion.6), channel_id=1, source_target_pairs={{0,2},{1,3},{2,0},{3,1},{4,6},{5,7},{6,4},{7,5},{8,10},{9,11},{10,... | collective-permute-start | bytes 442376 | tf_op jit(solution)/shard_map/ppermute | solution.py:45
  131.5 3.2 %collective-permute-start.20 = (bf16[192,768]{1,0:T(8,128)(2,1)S(1)}, bf16[192,768]{1,0:T(8,128)(2,1)S(1)}, u32[]{:S(2)}, u32[]{:S(2)}) collective-permute-start(bf16[192,768]{1,0:T(8,128)(2,1)S(1)} %concatenate.91), channel_id=1, source_target_pairs={{0,1},{1,0},{2,3},{3,2},{4,5},{5,4},{6,7},{7,6},{8,9},{9,8},{10,11... | collective-permute-start | bytes 884744 | tf_op jit(solution)/shard_map/ppermute | solution.py:45
  161.2 3.3 %copy-start.16 = (bf16[1,384,768]{2,1,0:T(8,128)(2,1)S(1)}, bf16[1,384,768]{2,1,0:T(8,128)(2,1)}, u32[]{:S(2)}) copy-start(bf16[1,384,768]{2,1,0:T(8,128)(2,1)} %param.21) | copy-start | bytes 1769476
  163.8 0.8 copy-start.6
  165.5 1.4 copy-start.4
  166.4 9.2 %collective-permute-start.24 = (bf16[4,2,2,24,768]{4,3,0,1,2:T(8,128)(2,1)}, bf16[4,2,2,24,768]{4,3,0,1,2:T(8,128)(2,1)}, u32[]{:S(2)}, u32[]{:S(2)}) collective-permute-start(bf16[4,2,2,24,768]{4,3,0,1,2:T(8,128)(2,1)} %fusion.14), channel_id=1, source_target_pairs={{0,1},{1,0},{2,3},{3,2},{4,5},{5,4},{6,7},{7,6},{8,9},{9,8},{10,11... | collective-permute-start | bytes 1769480 | tf_op jit(solution)/shard_map/ppermute | solution.py:45
  173.6 1.4 copy-start.10
  175.1 3.3 %collective-permute-start.21 = (bf16[4,2,2,24,768]{4,3,2,1,0:T(8,128)(2,1)S(1)}, bf16[4,2,2,24,768]{4,3,2,1,0:T(8,128)(2,1)S(1)}, u32[]{:S(2)}, u32[]{:S(2)}) collective-permute-start(bf16[4,2,2,24,768]{4,3,2,1,0:T(8,128)(2,1)S(1)} %fusion.13), channel_id=1, source_target_pairs={{0,1},{1,0},{2,3},{3,2},{4,5},{5,4},{6,7},{7,6},{8,9},{9,8},{10,11... | collective-permute-start | bytes 1769480 | tf_op jit(solution)/shard_map/ppermute | solution.py:45
  175.5 2.9 %copy-start.11 = (f32[4,2,2,2,24,768]{5,4,3,2,1,0:T(8,128)S(1)}, f32[4,2,2,2,24,768]{5,4,3,2,1,0:T(8,128)}, u32[]{:S(2)}) copy-start(f32[4,2,2,2,24,768]{5,4,3,2,1,0:T(8,128)} %copy-done.10) | copy-start | bytes 7077892
  176.9 9.2 %collective-permute-start.25 = (bf16[4,2,24,768]{3,2,0,1:T(8,128)(2,1)S(1)}, bf16[4,2,24,768]{3,2,0,1:T(8,128)(2,1)S(1)}, u32[]{:S(2)}, u32[]{:S(2)}) collective-permute-start(bf16[4,2,24,768]{3,2,0,1:T(8,128)(2,1)S(1)} %fusion.36), channel_id=1, source_target_pairs={{0,16},{16,0},{1,17},{17,1},{2,18},{18,2},{3,19},{19,3},{4,20},{20... | collective-permute-start | bytes 884744 | tf_op jit(solution)/shard_map/ppermute | solution.py:54
  178.6 9.1 %collective-permute-start.22 = (bf16[4,2,24,768]{3,2,1,0:T(8,128)(2,1)S(1)}, bf16[4,2,24,768]{3,2,1,0:T(8,128)(2,1)S(1)}, u32[]{:S(2)}, u32[]{:S(2)}) collective-permute-start(bf16[4,2,24,768]{3,2,1,0:T(8,128)(2,1)S(1)} %fusion.35), channel_id=1, source_target_pairs={{0,2},{1,3},{2,0},{3,1},{4,6},{5,7},{6,4},{7,5},{8,10},{9,11},{10,... | collective-permute-start | bytes 884744 | tf_op jit(solution)/shard_map/ppermute | solution.py:45
  186.1 5.2 %collective-permute-start.26 = (bf16[4,24,768]{2,1,0:T(8,128)(2,1)S(1)}, bf16[4,24,768]{2,1,0:T(8,128)(2,1)S(1)}, u32[]{:S(2)}, u32[]{:S(2)}) collective-permute-start(bf16[4,24,768]{2,1,0:T(8,128)(2,1)S(1)} %fusion.45), channel_id=1, source_target_pairs={{0,2},{1,3},{2,0},{3,1},{4,6},{5,7},{6,4},{7,5},{8,10},{9,11},{10,... | collective-permute-start | bytes 442376 | tf_op jit(solution)/shard_map/ppermute | solution.py:45
  187.8 5.2 %collective-permute-start.23 = (bf16[4,24,768]{2,1,0:T(8,128)(2,1)S(1)}, bf16[4,24,768]{2,1,0:T(8,128)(2,1)S(1)}, u32[]{:S(2)}, u32[]{:S(2)}) collective-permute-start(bf16[4,24,768]{2,1,0:T(8,128)(2,1)S(1)} %fusion.44), channel_id=1, source_target_pairs={{0,16},{16,0},{1,17},{17,1},{2,18},{18,2},{3,19},{19,3},{4,20},{20... | collective-permute-start | bytes 442376 | tf_op jit(solution)/shard_map/ppermute | solution.py:54
  191.4 5.7 %copy-start.21 = (bf16[768,768]{1,0:T(8,128)(2,1)S(1)}, bf16[768,768]{1,0:T(8,128)(2,1)}, u32[]{:S(2)}) copy-start(bf16[768,768]{1,0:T(8,128)(2,1)} %param.20) | copy-start | bytes 3538948
  191.4 5.6 %copy-start.3 = (bf16[192,768]{1,0:T(8,128)(2,1)S(1)}, bf16[192,768]{1,0:T(8,128)(2,1)}, u32[]{:S(2)}) copy-start(bf16[192,768]{1,0:T(8,128)(2,1)} %copy-done.2) | copy-start | bytes 884740
  191.4 5.6 %copy-start.7 = (bf16[16,48,352]{2,1,0:T(8,128)(2,1)S(1)}, bf16[16,48,352]{2,1,0:T(8,128)(2,1)}, u32[]{:S(2)}) copy-start(bf16[16,48,352]{2,1,0:T(8,128)(2,1)} %copy-done.6) | copy-start | bytes 1622020
  191.4 5.6 %copy-start.9 = (bf16[160,768]{1,0:T(8,128)(2,1)S(1)}, bf16[160,768]{1,0:T(8,128)(2,1)}, u32[]{:S(2)}) copy-start(bf16[160,768]{1,0:T(8,128)(2,1)} %copy-done.8) | copy-start | bytes 737284
  193.1 6.3 %collective-permute-start.27 = (bf16[24,1536]{1,0:T(8,128)(2,1)S(1)}, bf16[24,1536]{1,0:T(8,128)(2,1)S(1)}, u32[]{:S(2)}, u32[]{:S(2)}) collective-permute-start(bf16[24,1536]{1,0:T(8,128)(2,1)S(1)} %get-tuple-element.33), channel_id=1, source_target_pairs={{0,4},{1,5},{2,6},{3,7},{4,8},{5,9},{6,10},{7,11},{8,12},{9,13},{1... | collective-permute-start | bytes 221192 | tf_op jit(solution)/shard_map/ppermute | solution.py:61
  193.2 7.3 %collective-permute-start.28 = (bf16[24,1536]{1,0:T(8,128)(2,1)S(1)}, bf16[24,1536]{1,0:T(8,128)(2,1)S(1)}, u32[]{:S(2)}, u32[]{:S(2)}) collective-permute-start(bf16[24,1536]{1,0:T(8,128)(2,1)S(1)} %get-tuple-element.35), channel_id=1, source_target_pairs={{0,8},{1,9},{2,10},{3,11},{4,12},{5,13},{6,14},{7,15},{8,0},{9,1},... | collective-permute-start | bytes 221192 | tf_op jit(solution)/shard_map/ppermute | solution.py:61
  193.4 7.1 %collective-permute-start.29 = (bf16[24,1536]{1,0:T(8,128)(2,1)S(1)}, bf16[24,1536]{1,0:T(8,128)(2,1)S(1)}, u32[]{:S(2)}, u32[]{:S(2)}) collective-permute-start(bf16[24,1536]{1,0:T(8,128)(2,1)S(1)} %get-tuple-element.34), channel_id=1, source_target_pairs={{0,12},{1,13},{2,14},{3,15},{4,0},{5,1},{6,2},{7,3},{8,4},{9,5},{1... | collective-permute-start | bytes 221192 | tf_op jit(solution)/shard_map/ppermute | solution.py:61
  200.5 5.2 %copy-start.1 = (bf16[1536,768]{1,0:T(8,128)(2,1)S(1)}, bf16[1536,768]{1,0:T(8,128)(2,1)}, u32[]{:S(2)}) copy-start(bf16[1536,768]{1,0:T(8,128)(2,1)} %param.16) | copy-start | bytes 7077892
  200.6 4.4 %collective-permute-start.30 = (bf16[24,1536]{1,0:T(8,128)(2,1)S(1)}, bf16[24,1536]{1,0:T(8,128)(2,1)S(1)}, u32[]{:S(2)}, u32[]{:S(2)}) collective-permute-start(bf16[24,1536]{1,0:T(8,128)(2,1)S(1)} %fusion.51), channel_id=1, source_target_pairs={{0,16},{16,0},{1,17},{17,1},{2,18},{18,2},{3,19},{19,3},{4,20},{20... | collective-permute-start | bytes 221192 | tf_op jit(solution)/shard_map/ppermute | solution.py:54

commit v2 on v1

--- a/solution.py
+++ b/solution.py
@@ -3,6 +3,8 @@
 import jax
 import jax.numpy as jnp
 from jax import lax
+from jax.experimental import pallas as pl
+from jax.experimental.pallas import tpu as pltpu
 from jax.sharding import PartitionSpec as P
 
 HEADS = 16
@@ -33,6 +35,110 @@
     return lax.dot_general(
         left, right, (((0,), (0,)), ((), ())), preferred_element_type=jnp.float32
     )
+
+
+def mm_tt(left, right):
+    return lax.dot_general(
+        left, right, (((0,), (1,)), ((), ())), preferred_element_type=jnp.float32
+    )
+
+
+def project_t(weight, rows):
+    return mm_tt(weight, rows).astype(jnp.bfloat16)
+
+
+HEADS_A_STEP = 4
+
+
+def own_body(q_ref, k_ref, v_ref, bias_ref, e_ref, m_ref, l_ref, o_ref):
+    bias = bias_ref[...]
+    for h in range(HEADS_A_STEP):
+        at = slice(h * HEAD, (h + 1) * HEAD)
+        scores = mm_tn(k_ref[at], q_ref[at]) * (1.0 / math.sqrt(HEAD)) + bias
+        top = jnp.max(scores, axis=0, keepdims=True)
+        exponent = jnp.exp(scores - top)
+        m_ref[h] = top
+        l_ref[h] = jnp.sum(exponent, axis=0, keepdims=True)
+        low = exponent.astype(jnp.bfloat16)
+        e_ref[h] = low
+        o_ref[at] = mm(v_ref[at], low)
+
+
+def far_body(
+    q_ref, k_ref, v_ref, bias_ref, g_ref, e_ref, m_ref, l_ref, o_ref, att_ref, own_ref, far_ref
+):
+    bias = bias_ref[...]
+    for h in range(HEADS_A_STEP):
+        at = slice(h * HEAD, (h + 1) * HEAD)
+        scores = mm_tn(k_ref[at], q_ref[at]) * (1.0 / math.sqrt(HEAD)) + bias
+        top = jnp.maximum(jnp.max(scores, axis=0, keepdims=True), m_ref[h])
+        ratio = jnp.exp(m_ref[h] - top)
+        exponent = jnp.exp(scores - top)
+        norm = 1.0 / (l_ref[h] * ratio + jnp.sum(exponent, axis=0, keepdims=True))
+        low = exponent.astype(jnp.bfloat16)
+        att_ref[at] = ((o_ref[at] * ratio + mm(v_ref[at], low)) * norm).astype(jnp.bfloat16)
+        grads = g_ref[at].astype(jnp.float32) * norm
+        far_ref[at] = mm_nt(grads.astype(jnp.bfloat16), low).astype(jnp.bfloat16)
+        own_ref[at] = mm_nt((grads * ratio).astype(jnp.bfloat16), e_ref[h]).astype(jnp.bfloat16)
+
+
+def head_specs(*arrays):
+    specs = []
+    for array in arrays:
+        if array.ndim == 3:
+            specs.append(pl.BlockSpec((HEADS_A_STEP,) + array.shape[1:], lambda i: (i, 0, 0)))
+        elif array.shape[1] == 1:
+            specs.append(pl.BlockSpec(array.shape, lambda i: (0, 0)))
+        else:
+            specs.append(pl.BlockSpec((HEADS_A_STEP * HEAD, array.shape[1]), lambda i: (i, 0)))
+    return specs
+
+
+def attend_own(queries, keys, values, bias):
+    rows = queries.shape[1]
+    outs = [
+        jax.ShapeDtypeStruct((HEADS, keys.shape[1], rows), jnp.bfloat16),
+        jax.ShapeDtypeStruct((HEADS, 1, rows), jnp.float32),
+        jax.ShapeDtypeStruct((HEADS, 1, rows), jnp.float32),
+        jax.ShapeDtypeStruct(queries.shape, jnp.float32),
+    ]
+    args = (queries, keys, values, bias)
+    return pl.pallas_call(
+        own_body,
+        grid=(HEADS // HEADS_A_STEP,),
+        in_specs=head_specs(*args),
+        out_specs=head_specs(*outs),
+        out_shape=outs,
+        cost_estimate=pl.CostEstimate(
+            flops=40 * HEADS * rows * rows * HEAD,
+            transcendentals=HEADS * rows * rows,
+            bytes_accessed=2 * HEADS * rows * rows,
+        ),
+        name="attend_own",
+    )(*args)
+
+
+def attend_far(queries, keys, values, bias, grads, own):
+    rows = queries.shape[1]
+    outs = [
+        jax.ShapeDtypeStruct(queries.shape, jnp.bfloat16),
+        jax.ShapeDtypeStruct(queries.shape, jnp.bfloat16),
+        jax.ShapeDtypeStruct(keys.shape, jnp.bfloat16),
+    ]
+    args = (queries, keys, values, bias, grads) + tuple(own)
+    return pl.pallas_call(
+        far_body,
+        grid=(HEADS // HEADS_A_STEP,),
+        in_specs=head_specs(*args),
+        out_specs=head_specs(*outs),
+        out_shape=outs,
+        cost_estimate=pl.CostEstimate(
+            flops=40 * HEADS * rows * rows * HEAD,
+            transcendentals=HEADS * rows * rows,
+            bytes_accessed=2 * HEADS * rows * rows,
+        ),
+        name="attend_far",
+    )(*args)
 
 
 class Moves:
@@ -81,6 +187,43 @@
     down = jnp.concatenate([c[2 * hidden :] for c in chunks], axis=0)
     active = (jax.nn.silu(mm_nt(rows, gate)) * mm_nt(rows, upward)).astype(jnp.bfloat16)
     return mm(active, down)
+
+
+def ffn_body(count, hidden, has_start, rows_ref, *refs):
+    chunks, out_ref = refs[:count], refs[-1]
+    rows = rows_ref[...]
+    total = refs[count][...] if has_start else None
+    for at in range(0, count, 2):
+        pair = chunks[at : at + 2]
+        proj = jnp.concatenate(
+            [c[:hidden] for c in pair] + [c[hidden : 2 * hidden] for c in pair], axis=0
+        )
+        down = jnp.concatenate([c[2 * hidden :] for c in pair], axis=0)
+        both = mm_nt(rows, proj)
+        gate, upward = both[:, : 2 * hidden], both[:, 2 * hidden :]
+        active = (gate / (1.0 + jnp.exp(-gate)) * upward).astype(jnp.bfloat16)
+        term = mm(active, down)
+        total = term if total is None else total + term
+    out_ref[...] = total.astype(out_ref.dtype)
+
+
+def ffn_kernel(rows, chunks, hidden, start, first, steps, block, dtype):
+    width = rows.shape[1]
+    row_spec = pl.BlockSpec((block, width), lambda i: (i + first, 0))
+    whole = [pl.BlockSpec(c.shape, lambda i: (0, 0)) for c in chunks]
+    return pl.pallas_call(
+        lambda *refs: ffn_body(len(chunks), hidden, start is not None, *refs),
+        grid=(steps,),
+        in_specs=[row_spec] + whole + ([row_spec] if start is not None else []),
+        out_specs=pl.BlockSpec((block, width), lambda i: (i, 0)),
+        out_shape=jax.ShapeDtypeStruct((steps * block, width), dtype),
+        cost_estimate=pl.CostEstimate(
+            flops=6 * steps * block * width * hidden * len(chunks),
+            transcendentals=steps * block * hidden * len(chunks),
+            bytes_accessed=2 * width * (steps * block + 3 * hidden * len(chunks)),
+        ),
+        name="ffn_term",
+    )(rows, *chunks, *([start] if start is not None else []))
 
 
 def flip_blocks(rows):
@@ -108,14 +251,17 @@
     first, second = normed[:part], normed[part:]
     first = jnp.concatenate([first, moves.x(first)], axis=0)
     second = jnp.concatenate([second, moves.y(second)], axis=0)
-    rows = jnp.concatenate([first, second, moves.y(first), moves.x(second)], axis=0)
+    rows = jnp.concatenate([moves.y(first), moves.x(second), first, second], axis=0)
     early = [c for pair in chunks[:-1] for c in pair]
-    mixed = ffn_term(rows, chunks[-1], hidden)
-    if early:
-        mixed = mixed + ffn_term(rows, early, hidden)
-    low = mixed.astype(jnp.bfloat16)
-    first = mixed[: 2 * part] + moves.y(low[4 * part : 6 * part]).astype(jnp.float32)
-    second = mixed[2 * part : 4 * part] + moves.x(low[6 * part :]).astype(jnp.float32)
+    if hidden % 16 == 0 and early:
+        begun = ffn_kernel(rows, early, hidden, None, 0, 2, 2 * half, jnp.float32)
+        low = ffn_kernel(rows, chunks[-1], hidden, begun, 0, 2, half, jnp.bfloat16)
+        mixed = ffn_kernel(rows, chunks[-1], hidden, begun, 2, 2, half, jnp.float32)
+    else:
+        mixed = ffn_term(rows, [c for pair in chunks for c in pair], hidden)
+        low, mixed = mixed[: 2 * half].astype(jnp.bfloat16), mixed[2 * half :]
+    first = mixed[:half] + moves.y(low[:half]).astype(jnp.float32)
+    second = mixed[half:] + moves.x(low[half:]).astype(jnp.float32)
     first = first[:part] + moves.x(first[part:].astype(jnp.bfloat16)).astype(jnp.float32)
     second = second[:part] + moves.y(second[part:].astype(jnp.bfloat16)).astype(jnp.float32)
     mixed = jnp.concatenate([first, second], axis=0)
@@ -183,10 +329,9 @@
     live = seq_len - BLOCK
     is_valid = jnp.arange(live) < row_count
     grad_y = jnp.where(is_valid[:, None], cotangent[0, :live], jnp.zeros((), cotangent.dtype))
-    grad_att = mm_nt(grad_y, w_out).astype(jnp.bfloat16)
+    grad_att = mm_nt(w_out, grad_y).astype(jnp.bfloat16)
 
     slide_tok = encode(moves, tile_rows, row_count, w_gate, w_up, w_down_t, w_embed)
-    score_scale = 1.0 / math.sqrt(HEAD)
     slide_normed = rms_rows(slide_tok).astype(jnp.bfloat16)
     width = slide_normed.shape[1]
     dilated = seq_len // RATE
@@ -206,32 +351,20 @@
     far_valid = (
         jnp.arange(dilated)[None, :] < far_blocks[:, dilated - 1, :1].astype(jnp.float32)
     ).reshape(-1)
-    queries = mm(slide_normed, w_query).astype(jnp.bfloat16)
-    all_rows = jnp.concatenate([slide_normed, far_rows], axis=0)
-    key_set = mm(all_rows, w_key).astype(jnp.bfloat16).reshape(-1, HEADS, HEAD)
-    value_set = mm(all_rows, w_value).astype(jnp.bfloat16).reshape(-1, HEADS, HEAD)
-    key_valid = jnp.concatenate([is_valid, far_valid])
-    query_heads = queries.reshape(live, HEADS, HEAD)
-    scores = (
-        jnp.einsum("phd,jhd->hpj", query_heads, key_set, preferred_element_type=jnp.float32)
-        * score_scale
-    )
-    scores = jnp.where(key_valid[None, None, :], scores, -1e30)
-    row_max = jnp.max(scores, axis=2, keepdims=True)
-    exponent = jnp.exp(scores - row_max)
-    weights = (exponent / jnp.sum(exponent, axis=2, keepdims=True)).astype(jnp.bfloat16)
-    attended = jnp.einsum("hpj,jhd->phd", weights, value_set, preferred_element_type=jnp.float32)
-    attended = attended.reshape(live, width).astype(jnp.bfloat16)
-    output = slide_tok.astype(jnp.float32) + mm(attended, w_out)
+    bias_own = jnp.where(is_valid, 0.0, -1e30).astype(jnp.float32)[:, None]
+    bias_far = jnp.where(far_valid, 0.0, -1e30).astype(jnp.float32)[:, None]
+    queries = project_t(w_query, slide_normed)
+    own = attend_own(
+        queries, project_t(w_key, slide_normed), project_t(w_value, slide_normed), bias_own
+    )
+    attended, grads_own, grads_far = attend_far(
+        queries, project_t(w_key, far_rows), project_t(w_value, far_rows), bias_far, grad_att, own
+    )
+    output = slide_tok.astype(jnp.float32) + mm_tn(attended, w_out)
     slide_out = jnp.where(is_valid[:, None], output, 0.0).astype(jnp.bfloat16)
     slide_out = jnp.concatenate([slide_out, jnp.zeros((BLOCK, width), jnp.bfloat16)], axis=0)
-    part_out = mm_tn(attended, grad_y)
-    grad_heads = grad_att.reshape(live, HEADS, HEAD)
-    grad_values = jnp.einsum(
-        "hpj,phd->jhd", weights, grad_heads, preferred_element_type=jnp.float32
-    )
-    grad_values = grad_values.reshape(-1, width).astype(jnp.bfloat16)
-    part_value = mm_tn(all_rows, grad_values)
+    part_out = mm(attended, grad_y)
+    part_value = mm_tt(slide_normed, grads_own) + mm_tt(far_rows, grads_far)
     grad_value, grad_out = reduce_grads(moves, part_value, part_out)
     return (slide_out[None], grad_value, grad_out)
 

time: 206 us -> 194 us (0.942)
  Pallas kernels: 0 us -> 39.1 us
  matrix products: 52.3 us -> 13.8 us
  waiting for transfers between devices: 82.1 us -> 76.6 us
  other arithmetic: 15.4 us -> 10.3 us
  starting transfers between devices: 31.5 us -> 29.4 us
    pallas_call x0 -> x5, Pallas kernels: none -> 39.1 us  [the longest x3 18.7 us: ffn_kernel(): pl.pallas_call(lambda *refs: ffn_body(len(chunks), hidden, start is not N...]
    dot_general x7 -> x2, matrix products: 25.3 us -> 2.78 us  [mm(): return jnp.dot(left, right, preferred_element_type=jnp.float32)]
    ppermute x9, waiting for transfers between devices: 42.6 us -> 29.7 us  [y(): lax.ppermute(value, 'group', [(g, g ^ 1) for g in range(self.groups)])]
    sub x1 -> x0, matrix products: 10.8 us -> none  [shards(): exponent = jnp.exp(scores - row_max)]
    ppermute x3, waiting for transfers between devices: 15.5 us -> 24.4 us  [ring_next(): return lax.ppermute(value, BOTH, pairs)]
    convert_element_type x3 -> x1, other arithmetic: 6.98 us -> 0.07 us  [shards(): output = slide_tok.astype(jnp.float32) + mm_tn(attended, w_out)]
    dot_general x3 -> x1, matrix products: 7.61 us -> 2.07 us  [mm_nt(): lax.dot_general(left, right, (((1,), (1,)), ((), ())), preferred_element_...]
    dot_general x2 -> x7, matrix products: 5.06 us -> 8.32 us  [mm_tt(): lax.dot_general(left, right, (((0,), (1,)), ((), ())), preferred_element_...]
  transfers between devices with their start and end apart: 31 -> 31, of which waited for: 20 -> 21; matrix products, arithmetic and copies ran while one was open for 17% -> 13% of each run, Pallas kernels for 0% -> 12%
where the time goes in v2:
time: 194 us; the launch traced here: 193 us
  waiting for transfers between devices  76.6 us (39%)
  Pallas kernels  39.1 us (20%)
  starting transfers between devices  29.4 us (15%)
  local copies, waits for them, and re-layouts  21.9 us (11%)
  matrix products  13.8 us (7%)
  other arithmetic  10.3 us (5%)
    ppermute x9, waiting for transfers between devices, y(): lax.ppermute(value, 'group', [(g, g ^ 1) for g in range(self.groups)])  29.7 us
    ppermute x3, waiting for transfers between devices, ring_next(): return lax.ppermute(value, BOTH, pairs)  24.4 us
    ppermute x16, waiting for transfers between devices, seq_xor(): return lax.ppermute(value, 'seq', [(s, s ^ bit) for s in range(self.seqs)])  19.7 us
    pallas_call x3, Pallas kernels, ffn_kernel(): pl.pallas_call(lambda *refs: ffn_body(len(chunks), hidden, start is not N...  18.7 us
    ppermute x9, starting transfers between devices, y(): lax.ppermute(value, 'group', [(g, g ^ 1) for g in range(self.groups)])  12.7 us
    pallas_call x1, Pallas kernels, attend_far(): pl.pallas_call(far_body, grid=(HEADS // HEADS_A_STEP,), in_specs=head_spe...  11.9 us
    ppermute x16, starting transfers between devices, seq_xor(): return lax.ppermute(value, 'seq', [(s, s ^ bit) for s in range(self.seqs)])  9.63 us
    pallas_call x1, Pallas kernels, attend_own(): pl.pallas_call(own_body, grid=(HEADS // HEADS_A_STEP,), in_specs=head_spe...  8.47 us
  transfers between devices with their start and end apart: 31, of which 21 were waited for; matrix products, arithmetic and copies ran while one was open for 13% of the time, Pallas kernels for 12%

profile of v2, /device:TPU:0, one launch (start us, length us, event | category | flops | bytes accessed | tf_op | source)
XLA Modules:
  0.0 193.0 jit_solution(10053452076327960152)
XLA Ops:
  0.7 1.7 slice-done
  2.4 0.8 rev.6
  3.2 3.0 %collective-permute-start = (bf16[160,1536]{1,0:T(8,128)(2,1)}, bf16[160,1536]{1,0:T(8,128)(2,1)}, u32[]{:S(2)}, u32[]{:S(2)}) collective-permute-start(bf16[160,1536]{1,0:T(8,128)(2,1)} %bitcast.110), channel_id=1, source_target_pairs={{0,16},{16,0},{1,17},{17,1},{2,18},{18,2},{3,19},{19,3},{4,20},{20... | collective-permute-start | bytes 1474568 | tf_op jit(solution)/shard_map/ppermute | solution.py:160
  6.2 2.0 %pad_maximum_fusion.4.refs_1_ = bf16[192,1536]{1,0:T(8,128)(2,1)} fusion(bf16[64,1536]{1,0:T(8,128)(2,1)} %bitcast.112, bf16[64,1536]{1,0:T(8,128)(2,1)} %bitcast.113, bf16[64,1536]{1,0:T(8,128)(2,1)} %bitcast.114), kind=kLoop, calls=%fused_computation.41 | loop fusion | flops 1769472 | bytes 1179648 | tf_op jit(solution)/shard_map/concatenate | solution.py:238
  8.2 1.6 collective-permute-start.5
  10.5 7.3 %collective-permute-done = bf16[160,1536]{1,0:T(8,128)(2,1)} collective-permute-done((bf16[160,1536]{1,0:T(8,128)(2,1)}, bf16[160,1536]{1,0:T(8,128)(2,1)}, u32[]{:S(2)}, u32[]{:S(2)}) %collective-permute-start) | collective-permute-done | bytes 491552 | tf_op jit(solution)/shard_map/ppermute | solution.py:160
  17.7 1.3 bitcast_select_fusion.2
  19.5 1.8 collective-permute-start.1
  21.3 1.5 collective-permute-start.3
  22.8 2.4 %collective-permute-done.5.refs_3_ = bf16[192,1536]{1,0:T(8,128)(2,1)} collective-permute-done((bf16[192,1536]{1,0:T(8,128)(2,1)}, bf16[192,1536]{1,0:T(8,128)(2,1)}, u32[]{:S(2)}, u32[]{:S(2)}) %collective-permute-start.5) | collective-permute-done | bytes 589856 | tf_op jit(solution)/shard_map/ppermute | solution.py:177
  25.1 2.6 %collective-permute-done.1 = bf16[96,1536]{1,0:T(8,128)(2,1)S(1)} collective-permute-done((bf16[96,1536]{1,0:T(8,128)(2,1)S(1)}, bf16[96,1536]{1,0:T(8,128)(2,1)S(1)}, u32[]{:S(2)}, u32[]{:S(2)}) %collective-permute-start.1) | collective-permute-done | bytes 294944 | tf_op jit(solution)/shard_map/ppermute | solution.py:151
  27.8 1.5 collective-permute-start.2
  29.3 1.6 collective-permute-start.4
  31.4 9.7 %collective-permute-done.6.refs_5_ = bf16[192,1536]{1,0:T(8,128)(2,1)S(1)} collective-permute-done((bf16[192,1536]{1,0:T(8,128)(2,1)}, bf16[192,1536]{1,0:T(8,128)(2,1)S(1)}, u32[]{:S(2)}, u32[]{:S(2)}) %collective-permute-start.6) | collective-permute-done | bytes 589856 | tf_op jit(solution)/shard_map/ppermute | solution.py:177
  41.5 1.6 collective-permute-start.7
  43.1 0.9 constant_dynamic-update-slice_fusion.5
  44.0 0.9 constant_dynamic-update-slice_fusion.4
  46.4 12.3 %collective-permute-done.7.refs_1_ = bf16[192,1536]{1,0:T(8,128)(2,1)S(1)} collective-permute-done((bf16[192,1536]{1,0:T(8,128)(2,1)S(1)}, bf16[192,1536]{1,0:T(8,128)(2,1)S(1)}, u32[]{:S(2)}, u32[]{:S(2)}) %collective-permute-start.7) | collective-permute-done | bytes 589856 | tf_op jit(solution)/shard_map/ppermute | solution.py:177
  60.2 9.3 %ffn_term.3.refs_3_ = f32[768,1536]{1,0:T(8,128)} custom-call(bf16[768,1536]{1,0:T(8,128)(2,1)} %constant_dynamic-update-slice_fusion.refs_0_, bf16[192,1536]{1,0:T(8,128)(2,1)} %pad_maximum_fusion.4.refs_1_, bf16[192,1536]{1,0:T(8,128)(2,1)} %collective-permute-done.9.refs_2_, bf16[192,1536]{1,0:T(8,128)(2,1)} %collective-permute-done.5.refs_3_, ...), custom_call_target="tpu_custom_call" | custom-call | flops 2717908992 | bytes 5898240 | tf_op jit(solution)/shard_map/ffn_term/pallas_call | solution.py:214
  69.6 4.6 %ffn_term.5 = bf16[384,1536]{1,0:T(8,128)(2,1)} custom-call(bf16[768,1536]{1,0:T(8,128)(2,1)} %constant_dynamic-update-slice_fusion.refs_0_, bf16[192,1536]{1,0:T(8,128)(2,1)} %copy-done.6, bf16[192,1536]{1,0:T(8,128)(2,1)} %collective-permute-done.8.refs_2_, f32[768,1536]{1,0:T(8,128)} %ffn_term.3.refs_3_), custom_call_target="tpu_custom_call" | custom-call | flops 452984832 | bytes 2359296 | tf_op jit(solution)/shard_map/ffn_term/pallas_call | solution.py:214
  74.2 2.4 %fusion.40 = (bf16[192,1536]{1,0:T(8,128)(2,1)}, bf16[192,1536]{1,0:T(8,128)(2,1)}) fusion(bf16[384,1536]{1,0:T(8,128)(2,1)} %ffn_term.5), kind=kLoop, calls=%fused_computation.115 | loop fusion | bytes 2359296 | tf_op jit(solution)/shard_map/slice | solution.py:263
  76.6 1.0 collective-permute-start.12
  77.5 1.3 collective-permute-start.14
  78.8 4.8 %ffn_term.4 = f32[384,1536]{1,0:T(8,128)} custom-call(bf16[768,1536]{1,0:T(8,128)(2,1)} %constant_dynamic-update-slice_fusion.refs_0_, bf16[192,1536]{1,0:T(8,128)(2,1)} %copy-done.6, bf16[192,1536]{1,0:T(8,128)(2,1)} %collective-permute-done.8.refs_2_, f32[768,1536]{1,0:T(8,128)} %ffn_term.3.refs_3_), custom_call_target="tpu_custom_call" | custom-call | flops 452984832 | bytes 2359296 | tf_op jit(solution)/shard_map/ffn_term/pallas_call | solution.py:214
  83.6 8.9 %collective-permute-done.12 = bf16[192,1536]{1,0:T(8,128)(2,1)S(1)} collective-permute-done((bf16[192,1536]{1,0:T(8,128)(2,1)}, bf16[192,1536]{1,0:T(8,128)(2,1)S(1)}, u32[]{:S(2)}, u32[]{:S(2)}) %collective-permute-start.12) | collective-permute-done | bytes 589856 | tf_op jit(solution)/shard_map/ppermute | solution.py:160
  93.2 2.1 %slice_add_fusion.1 = (f32[192,1536]{1,0:T(8,128)S(1)}, f32[192,1536]{1,0:T(8,128)S(1)}) fusion(f32[384,1536]{1,0:T(8,128)} %ffn_term.4, bf16[192,1536]{1,0:T(8,128)(2,1)S(1)} %collective-permute-done.12, bf16[192,1536]{1,0:T(8,128)(2,1)} %collective-permute-done.14), kind=kLoop, calls=%fused_computation.19 | loop fusion | flops 1179648 | bytes 5898240 | tf_op jit(solution)/shard_map/add | solution.py:263
  95.4 1.4 collective-permute-start.13
  96.8 1.4 collective-permute-start.15
  98.1 5.5 %collective-permute-done.13 = bf16[96,1536]{1,0:T(8,128)(2,1)S(1)} collective-permute-done((bf16[96,1536]{1,0:T(8,128)(2,1)S(1)}, bf16[96,1536]{1,0:T(8,128)(2,1)S(1)}, u32[]{:S(2)}, u32[]{:S(2)}) %collective-permute-start.13) | collective-permute-done | bytes 294944 | tf_op jit(solution)/shard_map/ppermute | solution.py:151
  103.7 1.1 collective-permute-done.15
  105.9 1.4 collective-permute-start.16
  107.3 2.1 %convolution_convert_fusion.4 = bf16[352,768]{1,0:T(8,128)(2,1)S(1)} fusion(bf16[768,768]{1,0:T(8,128)(2,1)} %param.20, pred[352]{0:T(512)(128)(4,1)S(1)} %iota_compare_fusion.1, bf16[1,384,768]{2,1,0:T(8,128)(2,1)} %param.21), kind=kOutput, calls=%fused_computation.11 | convolution fusion | flops 415776768 | bytes 2261344 | tf_op jit(solution)/shard_map/dot_general | solution.py:29
  109.4 1.1 copy.49
  111.1 1.0 collective-permute-done.16
  112.8 2.0 %convolution_convert_fusion.2 = bf16[352,768]{1,0:T(8,128)(2,1)S(1)} fusion(bf16[768,768]{1,0:T(8,128)(2,1)} %param.19, f32[352]{0:T(512)S(1)} %add_rsqrt_fusion, bf16[160,768]{1,0:T(8,128)(2,1)S(1)} %collective-permute-done.16, bf16[192,768]{1,0:T(8,128)(2,1)S(1)} %convolution_convert_fusion.6), kind=kOutput, calls=%fused_computation.9 | convolution fusion | flops 417128448 | bytes 2262400 | tf_op jit(solution)/shard_map/dot_general | solution.py:41
  114.8 2.9 %collective-permute-done.17 = bf16[24,768]{1,0:T(8,128)(2,1)S(1)} collective-permute-done((bf16[24,768]{1,0:T(8,128)(2,1)S(1)}, bf16[24,768]{1,0:T(8,128)(2,1)S(1)}, u32[]{:S(2)}, u32[]{:S(2)}) %collective-permute-start.17) | collective-permute-done | bytes 36896 | tf_op jit(solution)/shard_map/ppermute | solution.py:151
  118.4 1.1 copy.51
  119.5 1.1 copy.50
  120.6 1.5 collective-permute-done.18
  123.6 1.1 copy.44
  124.6 2.7 %collective-permute-done.19 = bf16[96,768]{1,0:T(8,128)(2,1)S(1)} collective-permute-done((bf16[96,768]{1,0:T(8,128)(2,1)S(1)}, bf16[96,768]{1,0:T(8,128)(2,1)S(1)}, u32[]{:S(2)}, u32[]{:S(2)}) %collective-permute-start.19) | collective-permute-done | bytes 147488 | tf_op jit(solution)/shard_map/ppermute | solution.py:151
  127.5 8.5 %attend_own.1 = (bf16[16,352,352]{2,1,0:T(8,128)(2,1)}, f32[16,1,352]{2,1,0:T(1,128)}, f32[16,1,352]{2,1,0:T(1,128)}, f32[768,352]{1,0:T(8,128)}) custom-call(bf16[768,352]{1,0:T(8,128)(2,1)} %bitcast.105, bf16[768,352]{1,0:T(8,128)(2,1)} %bitcast.108, bf16[768,352]{1,0:T(8,128)(2,1)} %bitcast.107, f32[352,1]{1,0:T(8,128)} %fusion.21.bias_ref), custom_call_target="tpu_custom_call" | custom-call | flops 3806330880 | bytes 3964928 | tf_op jit(solution)/shard_map/attend_own/pallas_call | solution.py:106
  136.2 1.0 copy-done.16
  137.3 1.7 fusion.2.k_ref
  138.9 1.6 fusion.3.v_ref
  141.7 11.9 %attend_far.1 = (bf16[768,352]{1,0:T(8,128)(2,1)}, bf16[768,352]{1,0:T(8,128)(2,1)}, bf16[768,384]{1,0:T(8,128)(2,1)}) custom-call(bf16[768,352]{1,0:T(8,128)(2,1)} %bitcast.106, bf16[768,384]{1,0:T(8,128)(2,1)} %fusion.2.k_ref, bf16[768,384]{1,0:T(8,128)(2,1)} %fusion.3.v_ref, f32[384,1]{1,0:T(8,128)} %select_n.177.bias_ref, bf16[768,352]{1,0:T(8,128)(2,1)} %bitcast.104, ...), custom_call_target="tpu_custom_call" | custom-call | flops 3806330880 | bytes 3964928 | tf_op jit(solution)/shard_map/attend_far/pallas_call | solution.py:129
  153.6 2.1 %fusion.10 = f32[4,2,2,2,24,768]{5,4,3,2,1,0:T(8,128)S(1)} fusion(bf16[4,2,2,2,24,352]{5,4,3,2,1,0:T(8,128)(2,1)} %bitcast.109, pred[352]{0:T(512)(128)(4,1)S(1)} %iota_compare_fusion.1, bf16[1,384,768]{2,1,0:T(8,128)(2,1)} %param.21), kind=kOutput, calls=%fused_computation.49 | convolution fusion | flops 415506432 | bytes 3490144 | tf_op jit(solution)/shard_map/dot_general | solution.py:25
  155.7 0.9 fusion.7
  157.1 0.9 fusion.39
  159.1 1.4 copy-done.2
  160.5 0.9 fusion.8
  161.8 1.3 bitcast_add_fusion
  163.2 1.4 collective-permute-start.25
  164.6 1.2 bitcast_add_fusion.1
  166.4 5.9 %collective-permute-done.25 = bf16[4,2,24,768]{3,2,1,0:T(8,128)(2,1)S(1)} collective-permute-done((bf16[4,2,24,768]{3,2,1,0:T(8,128)(2,1)S(1)}, bf16[4,2,24,768]{3,2,1,0:T(8,128)(2,1)S(1)}, u32[]{:S(2)}, u32[]{:S(2)}) %collective-permute-start.25) | collective-permute-done | bytes 294944 | tf_op jit(solution)/shard_map/ppermute | solution.py:160
  173.2 1.8 collective-permute-done.22
  175.8 2.0 %collective-permute-done.26 = bf16[4,24,768]{2,1,0:T(8,128)(2,1)S(1)} collective-permute-done((bf16[4,24,768]{2,1,0:T(8,128)(2,1)S(1)}, bf16[4,24,768]{2,1,0:T(8,128)(2,1)S(1)}, u32[]{:S(2)}, u32[]{:S(2)}) %collective-permute-start.26) | collective-permute-done | bytes 147488 | tf_op jit(solution)/shard_map/ppermute | solution.py:151
  177.9 2.4 %collective-permute-done.23 = bf16[4,24,768]{2,1,0:T(8,128)(2,1)S(1)} collective-permute-done((bf16[4,24,768]{2,1,0:T(8,128)(2,1)S(1)}, bf16[4,24,768]{2,1,0:T(8,128)(2,1)S(1)}, u32[]{:S(2)}, u32[]{:S(2)}) %collective-permute-start.23) | collective-permute-done | bytes 147488 | tf_op jit(solution)/shard_map/ppermute | solution.py:160
  181.1 3.1 %collective-permute-start.29 = (bf16[24,1536]{1,0:T(8,128)(2,1)S(1)}, bf16[24,1536]{1,0:T(8,128)(2,1)S(1)}, u32[]{:S(2)}, u32[]{:S(2)}) collective-permute-start(bf16[24,1536]{1,0:T(8,128)(2,1)S(1)} %get-tuple-element.26), channel_id=1, source_target_pairs={{0,12},{1,13},{2,14},{3,15},{4,0},{5,1},{6,2},{7,3},{8,4},{9,5},{1... | collective-permute-start | bytes 221192 | tf_op jit(solution)/shard_map/ppermute | solution.py:167
  184.9 1.8 collective-permute-done.27
  186.7 1.0 collective-permute-done.28
  187.8 0.8 collective-permute-start.30
  188.6 0.9 pad_bitcast_fusion
  189.5 2.7 %collective-permute-done.30 = bf16[24,1536]{1,0:T(8,128)(2,1)S(1)} collective-permute-done((bf16[24,1536]{1,0:T(8,128)(2,1)S(1)}, bf16[24,1536]{1,0:T(8,128)(2,1)S(1)}, u32[]{:S(2)}, u32[]{:S(2)}) %collective-permute-start.30) | collective-permute-done | bytes 73760 | tf_op jit(solution)/shard_map/ppermute | solution.py:160
  (123 shorter events, 18.1 us)
Async XLA Ops:
  0.6 104.5 %copy-start = (bf16[1536,768]{1,0:T(8,128)(2,1)S(1)}, bf16[1536,768]{1,0:T(8,128)(2,1)}, u32[]{:S(2)}) copy-start(bf16[1536,768]{1,0:T(8,128)(2,1)} %param.16) | copy-start | bytes 7077892
  0.6 1.7 slice-start
  3.2 7.2 %copy-start.7 = (bf16[1,384,1536]{2,1,0:T(8,128)(2,1)S(1)}, bf16[1,384,1536]{2,1,0:T(8,128)(2,1)}, u32[]{:S(2)}) copy-start(bf16[1,384,1536]{2,1,0:T(8,128)(2,1)} %param.11) | copy-start | bytes 3538948
  3.2 14.5 %collective-permute-start = (bf16[160,1536]{1,0:T(8,128)(2,1)}, bf16[160,1536]{1,0:T(8,128)(2,1)}, u32[]{:S(2)}, u32[]{:S(2)}) collective-permute-start(bf16[160,1536]{1,0:T(8,128)(2,1)} %bitcast.110), channel_id=1, source_target_pairs={{0,16},{16,0},{1,17},{17,1},{2,18},{18,2},{3,19},{19,3},{4,20},{20... | collective-permute-start | bytes 1474568 | tf_op jit(solution)/shard_map/ppermute | solution.py:160
  8.2 17.0 %collective-permute-start.5 = (bf16[192,1536]{1,0:T(8,128)(2,1)}, bf16[192,1536]{1,0:T(8,128)(2,1)}, u32[]{:S(2)}, u32[]{:S(2)}) collective-permute-start(bf16[192,1536]{1,0:T(8,128)(2,1)} %pad_maximum_fusion.4.refs_1_), channel_id=1, source_target_pairs={{0,4},{1,5},{2,6},{3,7},{4,8},{5,9},{6,10},{7,11},{8,12},{9,13},{1... | collective-permute-start | bytes 1769480 | tf_op jit(solution)/shard_map/ppermute | solution.py:177
  10.5 9.0 %copy-start.8 = (bf16[32,1536]{1,0:T(8,128)(2,1)}, bf16[32,1536]{1,0:T(8,128)(2,1)S(1)}, u32[]{:S(2)}) copy-start(bf16[32,1536]{1,0:T(8,128)(2,1)S(1)} %slice_bitcast_fusion) | copy-start | bytes 294916
  19.5 8.2 %collective-permute-start.1 = (bf16[96,1536]{1,0:T(8,128)(2,1)S(1)}, bf16[96,1536]{1,0:T(8,128)(2,1)S(1)}, u32[]{:S(2)}, u32[]{:S(2)}) collective-permute-start(bf16[96,1536]{1,0:T(8,128)(2,1)S(1)} %get-tuple-element.22), channel_id=1, source_target_pairs={{0,2},{1,3},{2,0},{3,1},{4,6},{5,7},{6,4},{7,5},{8,10},{9,11},{10,... | collective-permute-start | bytes 884744 | tf_op jit(solution)/shard_map/ppermute | solution.py:151
  21.3 8.0 %collective-permute-start.3 = (bf16[96,1536]{1,0:T(8,128)(2,1)S(1)}, bf16[96,1536]{1,0:T(8,128)(2,1)S(1)}, u32[]{:S(2)}, u32[]{:S(2)}) collective-permute-start(bf16[96,1536]{1,0:T(8,128)(2,1)S(1)} %get-tuple-element.21), channel_id=1, source_target_pairs={{0,16},{16,0},{1,17},{17,1},{2,18},{18,2},{3,19},{19,3},{4,20},{20... | collective-permute-start | bytes 884744 | tf_op jit(solution)/shard_map/ppermute | solution.py:160
  25.1 16.0 %collective-permute-start.6 = (bf16[192,1536]{1,0:T(8,128)(2,1)}, bf16[192,1536]{1,0:T(8,128)(2,1)S(1)}, u32[]{:S(2)}, u32[]{:S(2)}) collective-permute-start(bf16[192,1536]{1,0:T(8,128)(2,1)} %collective-permute-done.5.refs_3_), channel_id=1, source_target_pairs={{0,4},{1,5},{2,6},{3,7},{4,8},{5,9},{6,10},{7,11},{8,12},{9,13},{1... | collective-permute-start | bytes 1769480 | tf_op jit(solution)/shard_map/ppermute | solution.py:177
  27.8 13.8 %collective-permute-start.2 = (bf16[192,1536]{1,0:T(8,128)(2,1)S(1)}, bf16[192,1536]{1,0:T(8,128)(2,1)S(1)}, u32[]{:S(2)}, u32[]{:S(2)}) collective-permute-start(bf16[192,1536]{1,0:T(8,128)(2,1)S(1)} %pad_maximum_fusion.2), channel_id=1, source_target_pairs={{0,16},{16,0},{1,17},{17,1},{2,18},{18,2},{3,19},{19,3},{4,20},{20... | collective-permute-start | bytes 1769480 | tf_op jit(solution)/shard_map/ppermute | solution.py:160
  29.3 14.7 %collective-permute-start.4 = (bf16[192,1536]{1,0:T(8,128)(2,1)S(1)}, bf16[192,1536]{1,0:T(8,128)(2,1)S(1)}, u32[]{:S(2)}, u32[]{:S(2)}) collective-permute-start(bf16[192,1536]{1,0:T(8,128)(2,1)S(1)} %pad_maximum_fusion.3), channel_id=1, source_target_pairs={{0,2},{1,3},{2,0},{3,1},{4,6},{5,7},{6,4},{7,5},{8,10},{9,11},{10,... | collective-permute-start | bytes 1769480 | tf_op jit(solution)/shard_map/ppermute | solution.py:151
  30.9 29.3 %collective-permute-start.9 = (bf16[192,1536]{1,0:T(8,128)(2,1)}, bf16[192,1536]{1,0:T(8,128)(2,1)}, u32[]{:S(2)}, u32[]{:S(2)}) collective-permute-start(bf16[192,1536]{1,0:T(8,128)(2,1)} %pad_maximum_fusion.4.refs_1_), channel_id=1, source_target_pairs={{0,1},{1,0},{2,3},{3,2},{4,5},{5,4},{6,7},{7,6},{8,9},{9,8},{10,11... | collective-permute-start | bytes 1769480 | tf_op jit(solution)/shard_map/ppermute | solution.py:151
  30.9 29.3 %collective-permute-start.10 = (bf16[192,1536]{1,0:T(8,128)(2,1)}, bf16[192,1536]{1,0:T(8,128)(2,1)}, u32[]{:S(2)}, u32[]{:S(2)}) collective-permute-start(bf16[192,1536]{1,0:T(8,128)(2,1)} %collective-permute-done.5.refs_3_), channel_id=1, source_target_pairs={{0,1},{1,0},{2,3},{3,2},{4,5},{5,4},{6,7},{7,6},{8,9},{9,8},{10,11... | collective-permute-start | bytes 1769480 | tf_op jit(solution)/shard_map/ppermute | solution.py:151
  41.1 3.8 %copy-start.13 = (bf16[192,1536]{1,0:T(8,128)(2,1)}, bf16[192,1536]{1,0:T(8,128)(2,1)S(1)}, u32[]{:S(2)}) copy-start(bf16[192,1536]{1,0:T(8,128)(2,1)S(1)} %collective-permute-done.6.refs_5_) | copy-start | bytes 1769476
  41.1 19.1 %collective-permute-start.11 = (bf16[192,1536]{1,0:T(8,128)(2,1)S(1)}, bf16[192,1536]{1,0:T(8,128)(2,1)}, u32[]{:S(2)}, u32[]{:S(2)}) collective-permute-start(bf16[192,1536]{1,0:T(8,128)(2,1)S(1)} %collective-permute-done.6.refs_5_), channel_id=1, source_target_pairs={{0,1},{1,0},{2,3},{3,2},{4,5},{5,4},{6,7},{7,6},{8,9},{9,8},{10,11... | collective-permute-start | bytes 1769480 | tf_op jit(solution)/shard_map/ppermute | solution.py:151
  41.5 17.2 %collective-permute-start.7 = (bf16[192,1536]{1,0:T(8,128)(2,1)S(1)}, bf16[192,1536]{1,0:T(8,128)(2,1)S(1)}, u32[]{:S(2)}, u32[]{:S(2)}) collective-permute-start(bf16[192,1536]{1,0:T(8,128)(2,1)S(1)} %collective-permute-done.6.refs_5_), channel_id=1, source_target_pairs={{0,4},{1,5},{2,6},{3,7},{4,8},{5,9},{6,10},{7,11},{8,12},{9,13},{1... | collective-permute-start | bytes 1769480 | tf_op jit(solution)/shard_map/ppermute | solution.py:177
  58.7 10.9 %copy-start.6 = (bf16[192,1536]{1,0:T(8,128)(2,1)}, bf16[192,1536]{1,0:T(8,128)(2,1)S(1)}, u32[]{:S(2)}) copy-start(bf16[192,1536]{1,0:T(8,128)(2,1)S(1)} %collective-permute-done.7.refs_1_) | copy-start | bytes 1769476
  58.7 10.9 %collective-permute-start.8 = (bf16[192,1536]{1,0:T(8,128)(2,1)S(1)}, bf16[192,1536]{1,0:T(8,128)(2,1)}, u32[]{:S(2)}, u32[]{:S(2)}) collective-permute-start(bf16[192,1536]{1,0:T(8,128)(2,1)S(1)} %collective-permute-done.7.refs_1_), channel_id=1, source_target_pairs={{0,1},{1,0},{2,3},{3,2},{4,5},{5,4},{6,7},{7,6},{8,9},{9,8},{10,11... | collective-permute-start | bytes 1769480 | tf_op jit(solution)/shard_map/ppermute | solution.py:151
  76.6 15.9 %collective-permute-start.12 = (bf16[192,1536]{1,0:T(8,128)(2,1)}, bf16[192,1536]{1,0:T(8,128)(2,1)S(1)}, u32[]{:S(2)}, u32[]{:S(2)}) collective-permute-start(bf16[192,1536]{1,0:T(8,128)(2,1)} %get-tuple-element.19), channel_id=1, source_target_pairs={{0,16},{16,0},{1,17},{17,1},{2,18},{18,2},{3,19},{19,3},{4,20},{20... | collective-permute-start | bytes 1769480 | tf_op jit(solution)/shard_map/ppermute | solution.py:160
  77.5 15.7 %collective-permute-start.14 = (bf16[192,1536]{1,0:T(8,128)(2,1)}, bf16[192,1536]{1,0:T(8,128)(2,1)}, u32[]{:S(2)}, u32[]{:S(2)}) collective-permute-start(bf16[192,1536]{1,0:T(8,128)(2,1)} %get-tuple-element.20), channel_id=1, source_target_pairs={{0,2},{1,3},{2,0},{3,1},{4,6},{5,7},{6,4},{7,5},{8,10},{9,11},{10,... | collective-permute-start | bytes 1769480 | tf_op jit(solution)/shard_map/ppermute | solution.py:151
  95.4 8.3 %collective-permute-start.13 = (bf16[96,1536]{1,0:T(8,128)(2,1)S(1)}, bf16[96,1536]{1,0:T(8,128)(2,1)S(1)}, u32[]{:S(2)}, u32[]{:S(2)}) collective-permute-start(bf16[96,1536]{1,0:T(8,128)(2,1)S(1)} %slice.125), channel_id=1, source_target_pairs={{0,2},{1,3},{2,0},{3,1},{4,6},{5,7},{6,4},{7,5},{8,10},{9,11},{10,... | collective-permute-start | bytes 884744 | tf_op jit(solution)/shard_map/ppermute | solution.py:151
  96.7 8.1 %copy-start.9 = (bf16[32,1536]{1,0:T(8,128)(2,1)S(1)}, bf16[32,1536]{1,0:T(8,128)(2,1)}, u32[]{:S(2)}) copy-start(bf16[32,1536]{1,0:T(8,128)(2,1)} %copy-done.8) | copy-start | bytes 294916
  96.8 8.0 %collective-permute-start.15 = (bf16[96,1536]{1,0:T(8,128)(2,1)S(1)}, bf16[96,1536]{1,0:T(8,128)(2,1)S(1)}, u32[]{:S(2)}, u32[]{:S(2)}) collective-permute-start(bf16[96,1536]{1,0:T(8,128)(2,1)S(1)} %slice.124), channel_id=1, source_target_pairs={{0,16},{16,0},{1,17},{17,1},{2,18},{18,2},{3,19},{19,3},{4,20},{20... | collective-permute-start | bytes 884744 | tf_op jit(solution)/shard_map/ppermute | solution.py:160
  105.9 6.3 %collective-permute-start.16 = (bf16[160,768]{1,0:T(8,128)(2,1)S(1)}, bf16[160,768]{1,0:T(8,128)(2,1)S(1)}, u32[]{:S(2)}, u32[]{:S(2)}) collective-permute-start(bf16[160,768]{1,0:T(8,128)(2,1)S(1)} %bitcast.111), channel_id=1, source_target_pairs={{0,16},{16,0},{1,17},{17,1},{2,18},{18,2},{3,19},{19,3},{4,20},{20... | collective-permute-start | bytes 737288 | tf_op jit(solution)/shard_map/ppermute | solution.py:160
  112.7 5.0 %copy-start.15 = (bf16[768,768]{1,0:T(8,128)(2,1)S(1)}, bf16[768,768]{1,0:T(8,128)(2,1)}, u32[]{:S(2)}) copy-start(bf16[768,768]{1,0:T(8,128)(2,1)} %param.18) | copy-start | bytes 3538948
  112.7 4.9 %collective-permute-start.17 = (bf16[24,768]{1,0:T(8,128)(2,1)S(1)}, bf16[24,768]{1,0:T(8,128)(2,1)S(1)}, u32[]{:S(2)}, u32[]{:S(2)}) collective-permute-start(bf16[24,768]{1,0:T(8,128)(2,1)S(1)} %concatenate.57), channel_id=1, source_target_pairs={{0,8},{1,9},{2,10},{3,11},{4,12},{5,13},{6,14},{7,15},{8,0},{9,1},... | collective-permute-start | bytes 110600 | tf_op jit(solution)/shard_map/ppermute | solution.py:151
  117.7 4.4 %collective-permute-start.18 = (bf16[48,768]{1,0:T(8,128)(2,1)S(1)}, bf16[48,768]{1,0:T(8,128)(2,1)S(1)}, u32[]{:S(2)}, u32[]{:S(2)}) collective-permute-start(bf16[48,768]{1,0:T(8,128)(2,1)S(1)} %pad_maximum_fusion.7), channel_id=1, source_target_pairs={{0,4},{1,5},{2,6},{3,7},{4,0},{5,1},{6,2},{7,3},{8,12},{9,13},{10,... | collective-permute-start | bytes 221192 | tf_op jit(solution)/shard_map/ppermute | solution.py:151
  118.4 4.5 %copy-start.14 = (bf16[768,768]{1,0:T(8,128)(2,1)S(1)}, bf16[768,768]{1,0:T(8,128)(2,1)}, u32[]{:S(2)}) copy-start(bf16[768,768]{1,0:T(8,128)(2,1)} %param.17) | copy-start | bytes 3538948
  122.1 5.2 %collective-permute-start.19 = (bf16[96,768]{1,0:T(8,128)(2,1)S(1)}, bf16[96,768]{1,0:T(8,128)(2,1)S(1)}, u32[]{:S(2)}, u32[]{:S(2)}) collective-permute-start(bf16[96,768]{1,0:T(8,128)(2,1)S(1)} %pad_maximum_fusion.6), channel_id=1, source_target_pairs={{0,2},{1,3},{2,0},{3,1},{4,6},{5,7},{6,4},{7,5},{8,10},{9,11},{10,... | collective-permute-start | bytes 442376 | tf_op jit(solution)/shard_map/ppermute | solution.py:151
  127.5 8.6 %collective-permute-start.20 = (bf16[192,768]{1,0:T(8,128)(2,1)S(1)}, bf16[192,768]{1,0:T(8,128)(2,1)S(1)}, u32[]{:S(2)}, u32[]{:S(2)}) collective-permute-start(bf16[192,768]{1,0:T(8,128)(2,1)S(1)} %concatenate.60), channel_id=1, source_target_pairs={{0,1},{1,0},{2,3},{3,2},{4,5},{5,4},{6,7},{7,6},{8,9},{9,8},{10,11... | collective-permute-start | bytes 884744 | tf_op jit(solution)/shard_map/ppermute | solution.py:151
  136.0 1.3 copy-start.16
  137.3 3.3 %copy-start.4 = (bf16[384,768]{1,0:T(8,128)(2,1)}, bf16[384,768]{1,0:T(8,128)(2,1)S(1)}, u32[]{:S(2)}) copy-start(bf16[384,768]{1,0:T(8,128)(2,1)S(1)} %concatenate.61) | copy-start | bytes 1769476
  137.3 1.7 copy-start.17
  155.7 1.4 copy-start.12
  156.6 5.2 %collective-permute-start.24 = (bf16[4,2,2,24,768]{4,3,2,1,0:T(8,128)(2,1)}, bf16[4,2,2,24,768]{4,3,2,1,0:T(8,128)(2,1)}, u32[]{:S(2)}, u32[]{:S(2)}) collective-permute-start(bf16[4,2,2,24,768]{4,3,2,1,0:T(8,128)(2,1)} %fusion.7), channel_id=1, source_target_pairs={{0,1},{1,0},{2,3},{3,2},{4,5},{5,4},{6,7},{7,6},{8,9},{9,8},{10,11... | collective-permute-start | bytes 1769480 | tf_op jit(solution)/shard_map/ppermute | solution.py:151
  157.1 1.1 copy-start.5
  157.1 1.2 copy-start.10
  159.1 1.4 copy-start.2
  161.4 3.2 %collective-permute-start.21 = (bf16[4,2,2,24,768]{4,3,0,2,1:T(8,128)(2,1)}, bf16[4,2,2,24,768]{4,3,0,2,1:T(8,128)(2,1)}, u32[]{:S(2)}, u32[]{:S(2)}) collective-permute-start(bf16[4,2,2,24,768]{4,3,0,2,1:T(8,128)(2,1)} %fusion.8), channel_id=1, source_target_pairs={{0,1},{1,0},{2,3},{3,2},{4,5},{5,4},{6,7},{7,6},{8,9},{9,8},{10,11... | collective-permute-start | bytes 1769480 | tf_op jit(solution)/shard_map/ppermute | solution.py:151
  161.8 2.8 %copy-start.3 = (f32[768,768]{1,0:T(8,128)S(1)}, f32[768,768]{1,0:T(8,128)}, u32[]{:S(2)}) copy-start(f32[768,768]{1,0:T(8,128)} %copy-done.2) | copy-start | bytes 7077892
  163.2 9.1 %collective-permute-start.25 = (bf16[4,2,24,768]{3,2,1,0:T(8,128)(2,1)S(1)}, bf16[4,2,24,768]{3,2,1,0:T(8,128)(2,1)S(1)}, u32[]{:S(2)}, u32[]{:S(2)}) collective-permute-start(bf16[4,2,24,768]{3,2,1,0:T(8,128)(2,1)S(1)} %fusion.18), channel_id=1, source_target_pairs={{0,16},{16,0},{1,17},{17,1},{2,18},{18,2},{3,19},{19,3},{4,20},{20... | collective-permute-start | bytes 884744 | tf_op jit(solution)/shard_map/ppermute | solution.py:160
  165.8 9.2 %collective-permute-start.22 = (bf16[4,2,24,768]{3,2,0,1:T(8,128)(2,1)S(1)}, bf16[4,2,24,768]{3,2,0,1:T(8,128)(2,1)S(1)}, u32[]{:S(2)}, u32[]{:S(2)}) collective-permute-start(bf16[4,2,24,768]{3,2,0,1:T(8,128)(2,1)S(1)} %fusion.17), channel_id=1, source_target_pairs={{0,2},{1,3},{2,0},{3,1},{4,6},{5,7},{6,4},{7,5},{8,10},{9,11},{10,... | collective-permute-start | bytes 884744 | tf_op jit(solution)/shard_map/ppermute | solution.py:151
  172.4 5.4 %collective-permute-start.26 = (bf16[4,24,768]{2,1,0:T(8,128)(2,1)S(1)}, bf16[4,24,768]{2,1,0:T(8,128)(2,1)S(1)}, u32[]{:S(2)}, u32[]{:S(2)}) collective-permute-start(bf16[4,24,768]{2,1,0:T(8,128)(2,1)S(1)} %fusion.23), channel_id=1, source_target_pairs={{0,2},{1,3},{2,0},{3,1},{4,6},{5,7},{6,4},{7,5},{8,10},{9,11},{10,... | collective-permute-start | bytes 442376 | tf_op jit(solution)/shard_map/ppermute | solution.py:151
  175.1 5.2 %collective-permute-start.23 = (bf16[4,24,768]{2,1,0:T(8,128)(2,1)S(1)}, bf16[4,24,768]{2,1,0:T(8,128)(2,1)S(1)}, u32[]{:S(2)}, u32[]{:S(2)}) collective-permute-start(bf16[4,24,768]{2,1,0:T(8,128)(2,1)S(1)} %fusion.22), channel_id=1, source_target_pairs={{0,16},{16,0},{1,17},{17,1},{2,18},{18,2},{3,19},{19,3},{4,20},{20... | collective-permute-start | bytes 442376 | tf_op jit(solution)/shard_map/ppermute | solution.py:160
  177.9 6.4 %copy-start.11 = (bf16[768,352]{1,0:T(8,128)(2,1)S(1)}, bf16[768,352]{1,0:T(8,128)(2,1)}, u32[]{:S(2)}) copy-start(bf16[768,352]{1,0:T(8,128)(2,1)} %get-tuple-element.14) | copy-start | bytes 1622020
  177.9 6.4 %copy-start.18 = (bf16[768,768]{1,0:T(8,128)(2,1)S(1)}, bf16[768,768]{1,0:T(8,128)(2,1)}, u32[]{:S(2)}) copy-start(bf16[768,768]{1,0:T(8,128)(2,1)} %param.20) | copy-start | bytes 3538948
  180.4 6.3 %collective-permute-start.27 = (bf16[24,1536]{1,0:T(8,128)(2,1)S(1)}, bf16[24,1536]{1,0:T(8,128)(2,1)S(1)}, u32[]{:S(2)}, u32[]{:S(2)}) collective-permute-start(bf16[24,1536]{1,0:T(8,128)(2,1)S(1)} %get-tuple-element.25), channel_id=1, source_target_pairs={{0,4},{1,5},{2,6},{3,7},{4,8},{5,9},{6,10},{7,11},{8,12},{9,13},{1... | collective-permute-start | bytes 221192 | tf_op jit(solution)/shard_map/ppermute | solution.py:167
  180.9 6.8 %collective-permute-start.28 = (bf16[24,1536]{1,0:T(8,128)(2,1)S(1)}, bf16[24,1536]{1,0:T(8,128)(2,1)S(1)}, u32[]{:S(2)}, u32[]{:S(2)}) collective-permute-start(bf16[24,1536]{1,0:T(8,128)(2,1)S(1)} %get-tuple-element.27), channel_id=1, source_target_pairs={{0,8},{1,9},{2,10},{3,11},{4,12},{5,13},{6,14},{7,15},{8,0},{9,1},... | collective-permute-start | bytes 221192 | tf_op jit(solution)/shard_map/ppermute | solution.py:167
  181.1 6.6 %collective-permute-start.29 = (bf16[24,1536]{1,0:T(8,128)(2,1)S(1)}, bf16[24,1536]{1,0:T(8,128)(2,1)S(1)}, u32[]{:S(2)}, u32[]{:S(2)}) collective-permute-start(bf16[24,1536]{1,0:T(8,128)(2,1)S(1)} %get-tuple-element.26), channel_id=1, source_target_pairs={{0,12},{1,13},{2,14},{3,15},{4,0},{5,1},{6,2},{7,3},{8,4},{9,5},{1... | collective-permute-start | bytes 221192 | tf_op jit(solution)/shard_map/ppermute | solution.py:167
  187.7 5.2 %copy-start.1 = (bf16[1536,768]{1,0:T(8,128)(2,1)S(1)}, bf16[1536,768]{1,0:T(8,128)(2,1)}, u32[]{:S(2)}) copy-start(bf16[1536,768]{1,0:T(8,128)(2,1)} %param.16) | copy-start | bytes 7077892
  187.8 4.4 %collective-permute-start.30 = (bf16[24,1536]{1,0:T(8,128)(2,1)S(1)}, bf16[24,1536]{1,0:T(8,128)(2,1)S(1)}, u32[]{:S(2)}, u32[]{:S(2)}) collective-permute-start(bf16[24,1536]{1,0:T(8,128)(2,1)S(1)} %fusion.29), channel_id=1, source_target_pairs={{0,16},{16,0},{1,17},{17,1},{2,18},{18,2},{3,19},{19,3},{4,20},{20... | collective-permute-start | bytes 221192 | tf_op jit(solution)/shard_map/ppermute | solution.py:160

commit v3 on v1

--- a/solution.py
+++ b/solution.py
@@ -3,7 +3,10 @@
 import jax
 import jax.numpy as jnp
 from jax import lax
+from jax.experimental import pallas as pl
+from jax.experimental.pallas import tpu as pltpu
 from jax.sharding import PartitionSpec as P
+
 
 HEADS = 16
 HEAD = 48
@@ -33,6 +36,120 @@
     return lax.dot_general(
         left, right, (((0,), (0,)), ((), ())), preferred_element_type=jnp.float32
     )
+
+
+def mm_tt(left, right):
+    return lax.dot_general(
+        left, right, (((0,), (1,)), ((), ())), preferred_element_type=jnp.float32
+    )
+
+
+def project_t(weight, rows):
+    return mm_tt(weight, rows).astype(jnp.bfloat16)
+
+
+HEADS_A_CALL = 8
+
+
+def own_body(rows_ref, wq_ref, wk_ref, wv_ref, bias_ref, q_ref, e_ref, m_ref, l_ref, o_ref):
+    bias = bias_ref[...]
+    rows = rows_ref[...]
+    q_ref[...] = project_t(wq_ref[...], rows)
+    keys, values = project_t(wk_ref[...], rows), project_t(wv_ref[...], rows)
+    for h in range(HEADS_A_CALL):
+        at = slice(h * HEAD, (h + 1) * HEAD)
+        scores = mm_tn(keys[at], q_ref[at]) * (1.0 / math.sqrt(HEAD)) + bias
+        top = jnp.max(scores, axis=0, keepdims=True)
+        exponent = jnp.exp(scores - top)
+        m_ref[h] = top
+        l_ref[h] = jnp.sum(exponent, axis=0, keepdims=True)
+        low = exponent.astype(jnp.bfloat16)
+        e_ref[h] = low
+        o_ref[at] = mm(values[at], low)
+
+
+def far_body(
+    rows_ref, wk_ref, wv_ref, bias_ref, g_ref, q_ref, e_ref, m_ref, l_ref, o_ref,
+    att_ref, own_ref, far_ref,
+):
+    bias = bias_ref[...]
+    rows = rows_ref[...]
+    keys, values = project_t(wk_ref[...], rows), project_t(wv_ref[...], rows)
+    for h in range(HEADS_A_CALL):
+        at = slice(h * HEAD, (h + 1) * HEAD)
+        scores = mm_tn(keys[at], q_ref[at]) * (1.0 / math.sqrt(HEAD)) + bias
+        top = jnp.maximum(jnp.max(scores, axis=0, keepdims=True), m_ref[h])
+        ratio = jnp.exp(m_ref[h] - top)
+        exponent = jnp.exp(scores - top)
+        norm = 1.0 / (l_ref[h] * ratio + jnp.sum(exponent, axis=0, keepdims=True))
+        low = exponent.astype(jnp.bfloat16)
+        att_ref[at] = ((o_ref[at] * ratio + mm(values[at], low)) * norm).astype(jnp.bfloat16)
+        grads = g_ref[at].astype(jnp.float32) * norm
+        far_ref[at] = mm_nt(grads.astype(jnp.bfloat16), low).astype(jnp.bfloat16)
+        own_ref[at] = mm_nt((grads * ratio).astype(jnp.bfloat16), e_ref[h]).astype(jnp.bfloat16)
+
+
+def whole_spec(array):
+    return pl.BlockSpec(array.shape, lambda i: (0,) * array.ndim)
+
+
+def weight_spec(array, part):
+    return pl.BlockSpec((array.shape[0], HEADS_A_CALL * HEAD), lambda i: (0, part))
+
+
+def feature_spec(array, part):
+    return pl.BlockSpec((HEADS_A_CALL * HEAD, array.shape[1]), lambda i: (part, 0))
+
+
+def attend_own(part, rows, w_query, w_key, w_value, bias):
+    count = rows.shape[0]
+    features = HEADS_A_CALL * HEAD
+    outs = [
+        jax.ShapeDtypeStruct((features, count), jnp.bfloat16),
+        jax.ShapeDtypeStruct((HEADS_A_CALL, count, count), jnp.bfloat16),
+        jax.ShapeDtypeStruct((HEADS_A_CALL, 1, count), jnp.float32),
+        jax.ShapeDtypeStruct((HEADS_A_CALL, 1, count), jnp.float32),
+        jax.ShapeDtypeStruct((features, count), jnp.float32),
+    ]
+    return pl.pallas_call(
+        own_body,
+        grid=(1,),
+        in_specs=[whole_spec(rows)]
+        + [weight_spec(w, part) for w in (w_query, w_key, w_value)]
+        + [whole_spec(bias)],
+        out_specs=[whole_spec(o) for o in outs],
+        out_shape=outs,
+        cost_estimate=pl.CostEstimate(
+            flops=40 * features * count * count,
+            transcendentals=HEADS_A_CALL * count * count,
+            bytes_accessed=2 * HEADS_A_CALL * count * count,
+        ),
+        name="attend_own",
+    )(rows, w_query, w_key, w_value, bias)
+
+
+def attend_far(part, rows, w_key, w_value, bias, grads, own):
+    count, features = grads.shape[1], HEADS_A_CALL * HEAD
+    outs = [
+        jax.ShapeDtypeStruct((features, count), jnp.bfloat16),
+        jax.ShapeDtypeStruct((features, count), jnp.bfloat16),
+        jax.ShapeDtypeStruct((features, rows.shape[0]), jnp.bfloat16),
+    ]
+    return pl.pallas_call(
+        far_body,
+        grid=(1,),
+        in_specs=[whole_spec(rows), weight_spec(w_key, part), weight_spec(w_value, part)]
+        + [whole_spec(bias), feature_spec(grads, part)]
+        + [whole_spec(o) for o in own],
+        out_specs=[whole_spec(o) for o in outs],
+        out_shape=outs,
+        cost_estimate=pl.CostEstimate(
+            flops=40 * features * count * count,
+            transcendentals=HEADS_A_CALL * count * count,
+            bytes_accessed=2 * HEADS_A_CALL * count * count,
+        ),
+        name="attend_far",
+    )(rows, w_key, w_value, bias, grads, *own)
 
 
 class Moves:
@@ -83,6 +200,71 @@
     return mm(active, down)
 
 
+def pack_body(gate_ref, up_ref, down_ref, out_ref):
+    width, hidden = gate_ref.shape
+    lanes = 2 * hidden
+    out_ref[:width] = jnp.concatenate([gate_ref[...], up_ref[...]], axis=1)
+    for tile in range(width // lanes):
+        block = down_ref[tile * lanes : (tile + 1) * lanes].astype(jnp.float32)
+        out_ref[width + tile * hidden : width + (tile + 1) * hidden] = block.T.astype(jnp.bfloat16)
+
+
+def pack_weights(w_gate, w_up, w_down_t):
+    width, hidden = w_gate.shape
+    return pl.pallas_call(
+        pack_body,
+        out_shape=jax.ShapeDtypeStruct((width + width // 2, 2 * hidden), jnp.bfloat16),
+        name="pack",
+    )(w_gate, w_up, w_down_t)
+
+
+def ffn_body(pieces, count, splits, *refs):
+    rows_refs, chunk_refs = refs[:pieces], refs[pieces : pieces + count]
+    at = pieces + count
+    starts = refs[at:-splits] if len(refs) - splits > at else None
+    outs = refs[-splits:]
+    rows = jnp.concatenate([r[...] for r in rows_refs], axis=0)
+    total = None if starts is None else jnp.concatenate([r[...] for r in starts], axis=0)
+    width = rows.shape[1]
+    lanes = chunk_refs[0].shape[1]
+    hidden = lanes // 2
+    is_low = lax.broadcasted_iota(jnp.int32, (rows.shape[0], lanes), 1) < hidden
+    actives, downs = [], []
+    for at in range(0, count, 2):
+        pair = chunk_refs[at : at + 2]
+        both = mm(rows, jnp.concatenate([c[:width] for c in pair], axis=1))
+        even, odd = both[:, :lanes], both[:, lanes:]
+        gate = jnp.where(is_low, even, pltpu.roll(odd, hidden, 1))
+        upward = jnp.where(is_low, pltpu.roll(even, hidden, 1), odd)
+        actives.append((gate / (1.0 + jnp.exp(-gate)) * upward).astype(jnp.bfloat16))
+        for c in pair:
+            tiles = [
+                c[width + tile * hidden : width + (tile + 1) * hidden]
+                for tile in range(width // lanes)
+            ]
+            downs.append(jnp.concatenate(tiles, axis=1))
+    term = mm(jnp.concatenate(actives, axis=1), jnp.concatenate(downs, axis=0))
+    total = term if total is None else total + term
+    share = total.shape[0] // splits
+    for i, out in enumerate(outs):
+        out[...] = total[i * share : (i + 1) * share].astype(out.dtype)
+
+
+def ffn_kernel(rows, chunks, starts, splits, dtype):
+    width = rows[0].shape[1]
+    height = sum(r.shape[0] for r in rows)
+    units = len(chunks) * chunks[0].shape[1] // 2
+    return pl.pallas_call(
+        lambda *refs: ffn_body(len(rows), len(chunks), splits, *refs),
+        out_shape=[jax.ShapeDtypeStruct((height // splits, width), dtype)] * splits,
+        cost_estimate=pl.CostEstimate(
+            flops=6 * height * width * units,
+            transcendentals=height * units,
+            bytes_accessed=2 * width * (height + 3 * units),
+        ),
+    )(*rows, *chunks, *(starts or []))
+
+
 def flip_blocks(rows):
     width = rows.shape[1]
     return rows.reshape(-1, BLOCK, width)[::-1].reshape(-1, width)
@@ -90,39 +272,59 @@
 
 def encode(moves, tile_rows, row_count, w_gate, w_up, w_down_t, w_embed):
     hidden = w_gate.shape[1]
+    packed = 2 * hidden == 128 and moves.ring > 1
     half = tile_rows.shape[0] // 2
+    part = half // 2
     spare = half - BLOCK
-    chunk = jnp.concatenate([w_gate.T, w_up.T, w_down_t.T], axis=0)
+    low = jnp.bfloat16
+    if packed:
+        chunk = pack_weights(w_gate, w_up, w_down_t)
+    else:
+        chunk = jnp.concatenate([w_gate.T, w_up.T, w_down_t.T], axis=0)
     ringed = [chunk]
-    for _ in range(moves.ring - 1):
+    for _ in range(1, moves.ring):
         ringed.append(moves.ring_next(ringed[-1]))
-    chunks = [[c, moves.core(c)] for c in ringed]
+    chunks = []
+    for c in ringed:
+        chunks.append([c, moves.core(c)])
     extra = moves.y(flip_blocks(tile_rows[half : half + spare]))
     own_blocks = (row_count + BLOCK - 1) // BLOCK
     kept = (1 + jnp.arange(spare) // BLOCK) < own_blocks
     level = jnp.concatenate(
         [tile_rows[:BLOCK], jnp.where(kept[:, None], tile_rows[BLOCK:half], extra)], axis=0
     )
-    normed = rms_rows(level).astype(jnp.bfloat16)
-    part = half // 2
+    normed = rms_rows(level).astype(low)
     first, second = normed[:part], normed[part:]
     first = jnp.concatenate([first, moves.x(first)], axis=0)
     second = jnp.concatenate([second, moves.y(second)], axis=0)
-    rows = jnp.concatenate([first, second, moves.y(first), moves.x(second)], axis=0)
+    first_y = moves.y(first)
+    second_x = moves.x(second)
     early = [c for pair in chunks[:-1] for c in pair]
-    mixed = ffn_term(rows, chunks[-1], hidden)
-    if early:
-        mixed = mixed + ffn_term(rows, early, hidden)
-    low = mixed.astype(jnp.bfloat16)
-    first = mixed[: 2 * part] + moves.y(low[4 * part : 6 * part]).astype(jnp.float32)
-    second = mixed[2 * part : 4 * part] + moves.x(low[6 * part :]).astype(jnp.float32)
-    first = first[:part] + moves.x(first[part:].astype(jnp.bfloat16)).astype(jnp.float32)
-    second = second[:part] + moves.y(second[part:].astype(jnp.bfloat16)).astype(jnp.float32)
+    if packed:
+        begun = ffn_kernel([first_y, second_x, first, second], early, None, 8, jnp.float32)
+        sent = ffn_kernel([first_y, second_x], chunks[-1], begun[:4], 4, low)
+        kept = ffn_kernel([first, second], chunks[-1], begun[4:], 4, jnp.float32)
+    else:
+        rows = jnp.concatenate([first_y, second_x, first, second], axis=0)
+        mixed = ffn_term(rows, [c for pair in chunks for c in pair], hidden)
+        pieces = [mixed[i * part : (i + 1) * part] for i in range(8)]
+        sent, kept = [p.astype(low) for p in pieces[:4]], pieces[4:]
+    first_on = moves.y(sent[1])
+    second_on = moves.x(sent[3])
+    first_own = moves.y(sent[0])
+    second_own = moves.x(sent[2])
+    first_end = moves.x((kept[1] + first_on.astype(jnp.float32)).astype(low))
+    second_end = moves.y((kept[3] + second_on.astype(jnp.float32)).astype(low))
+    first = kept[0] + first_own.astype(jnp.float32) + first_end.astype(jnp.float32)
+    second = kept[2] + second_own.astype(jnp.float32) + second_end.astype(jnp.float32)
     mixed = jnp.concatenate([first, second], axis=0)
-    embedded = rms_rows(level.astype(jnp.float32) + mixed).astype(jnp.bfloat16)
-    slide_part = mm(embedded, w_embed).astype(jnp.bfloat16)
+    embedded = rms_rows(level.astype(jnp.float32) + mixed).astype(low)
+    slide_part = mm(embedded, w_embed).astype(low)
+    normed_part = rms_rows(slide_part).astype(low)
+    far_back = moves.y(flip_blocks(normed_part[BLOCK:])[::RATE])
     back = moves.y(flip_blocks(slide_part[BLOCK:]))
-    return jnp.concatenate([slide_part, back], axis=0)
+    far = jnp.concatenate([normed_part[::RATE], far_back], axis=0)
+    return jnp.concatenate([slide_part, back], axis=0), far
 
 
 def reduce_grads(moves, part_value, part_out):
@@ -183,10 +385,11 @@
     live = seq_len - BLOCK
     is_valid = jnp.arange(live) < row_count
     grad_y = jnp.where(is_valid[:, None], cotangent[0, :live], jnp.zeros((), cotangent.dtype))
-    grad_att = mm_nt(grad_y, w_out).astype(jnp.bfloat16)
-
-    slide_tok = encode(moves, tile_rows, row_count, w_gate, w_up, w_down_t, w_embed)
-    score_scale = 1.0 / math.sqrt(HEAD)
+    grad_att = mm_nt(w_out, grad_y).astype(jnp.bfloat16)
+
+    slide_tok, own_far = encode(
+        moves, tile_rows, row_count, w_gate, w_up, w_down_t, w_embed
+    )
     slide_normed = rms_rows(slide_tok).astype(jnp.bfloat16)
     width = slide_normed.shape[1]
     dilated = seq_len // RATE
@@ -195,43 +398,31 @@
     far_rows = gather_far(
         moves,
         jnp.concatenate(
-            [
-                slide_normed.reshape(held, RATE, width)[:, 0],
-                jnp.full((dilated - held, width), far_count, jnp.bfloat16),
-            ],
-            axis=0,
+            [own_far, jnp.full((dilated - held, width), far_count, jnp.bfloat16)], axis=0
         ),
     )
     far_blocks = far_rows.reshape(moves.seqs, dilated, width)
     far_valid = (
         jnp.arange(dilated)[None, :] < far_blocks[:, dilated - 1, :1].astype(jnp.float32)
     ).reshape(-1)
-    queries = mm(slide_normed, w_query).astype(jnp.bfloat16)
-    all_rows = jnp.concatenate([slide_normed, far_rows], axis=0)
-    key_set = mm(all_rows, w_key).astype(jnp.bfloat16).reshape(-1, HEADS, HEAD)
-    value_set = mm(all_rows, w_value).astype(jnp.bfloat16).reshape(-1, HEADS, HEAD)
-    key_valid = jnp.concatenate([is_valid, far_valid])
-    query_heads = queries.reshape(live, HEADS, HEAD)
-    scores = (
-        jnp.einsum("phd,jhd->hpj", query_heads, key_set, preferred_element_type=jnp.float32)
-        * score_scale
-    )
-    scores = jnp.where(key_valid[None, None, :], scores, -1e30)
-    row_max = jnp.max(scores, axis=2, keepdims=True)
-    exponent = jnp.exp(scores - row_max)
-    weights = (exponent / jnp.sum(exponent, axis=2, keepdims=True)).astype(jnp.bfloat16)
-    attended = jnp.einsum("hpj,jhd->phd", weights, value_set, preferred_element_type=jnp.float32)
-    attended = attended.reshape(live, width).astype(jnp.bfloat16)
-    output = slide_tok.astype(jnp.float32) + mm(attended, w_out)
+    bias_own = jnp.where(is_valid, 0.0, -1e30).astype(jnp.float32)[:, None]
+    bias_far = jnp.where(far_valid, 0.0, -1e30).astype(jnp.float32)[:, None]
+    parts = range(HEADS // HEADS_A_CALL)
+    own = []
+    for part in parts:
+        own.append(attend_own(part, slide_normed, w_query, w_key, w_value, bias_own))
+    ends = [
+        attend_far(part, far_rows, w_key, w_value, bias_far, grad_att, own[part])
+        for part in parts
+    ]
+    attended, grads_own, grads_far = [
+        jnp.concatenate(pieces, axis=0) for pieces in zip(*ends)
+    ]
+    output = slide_tok.astype(jnp.float32) + mm_tn(attended, w_out)
     slide_out = jnp.where(is_valid[:, None], output, 0.0).astype(jnp.bfloat16)
     slide_out = jnp.concatenate([slide_out, jnp.zeros((BLOCK, width), jnp.bfloat16)], axis=0)
-    part_out = mm_tn(attended, grad_y)
-    grad_heads = grad_att.reshape(live, HEADS, HEAD)
-    grad_values = jnp.einsum(
-        "hpj,phd->jhd", weights, grad_heads, preferred_element_type=jnp.float32
-    )
-    grad_values = grad_values.reshape(-1, width).astype(jnp.bfloat16)
-    part_value = mm_tn(all_rows, grad_values)
+    part_out = mm(attended, grad_y)
+    part_value = mm_tt(slide_normed, grads_own) + mm_tt(far_rows, grads_far)
     grad_value, grad_out = reduce_grads(moves, part_value, part_out)
     return (slide_out[None], grad_value, grad_out)
 
@@ -250,6 +441,7 @@
         P(),
         P("group", "seq", None),
     )
+
     return jax.shard_map(
         shards,
         mesh=mesh,

time: 206 us -> 200 us (0.971)
  Pallas kernels: 0 us -> 51 us
  matrix products: 52.3 us -> 7.84 us
  waiting for transfers between devices: 82.1 us -> 72 us
  other arithmetic: 15.4 us -> 9.81 us
  local copies, waits for them, and re-layouts: 22.6 us -> 26.5 us
    pallas_call x0 -> x8, Pallas kernels: none -> 51 us  [the longest x3 18.5 us: ffn_kernel(): pl.pallas_call(lambda *refs: ffn_body(len(rows), len(chunks), splits, *re...]
    ppermute x9 -> x11, waiting for transfers between devices: 42.6 us -> 16.3 us  [y(): lax.ppermute(value, 'group', [(g, g ^ 1) for g in range(self.groups)])]
    dot_general x7 -> x2, matrix products: 25.3 us -> 2.72 us  [mm(): return jnp.dot(left, right, preferred_element_type=jnp.float32)]
    ppermute x3, waiting for transfers between devices: 15.5 us -> 34.4 us  [ring_next(): return lax.ppermute(value, BOTH, pairs)]
    sub x1 -> x0, matrix products: 10.8 us -> none  [shards(): exponent = jnp.exp(scores - row_max)]
    dot_general x3 -> x1, matrix products: 7.61 us -> 2.87 us  [mm_nt(): lax.dot_general(left, right, (((1,), (1,)), ((), ())), preferred_element_...]
    slice x6 -> x3, local copies, waits for them, and re-layouts: 5.22 us -> 0.72 us  [the longest x2 0.67 us: encode(): far_back = moves.y(flip_blocks(normed_part[BLOCK:])[::RATE])]
    concatenate x2 -> x3, local copies, waits for them, and re-layouts: 0.5 us -> 4.93 us  [gather_far(): block = jnp.concatenate([block, moves.seq_xor(block, bit)], axis=0)]
  transfers between devices with their start and end apart: 31 -> 34, of which waited for: 20 -> 18; matrix products, arithmetic and copies ran while one was open for 17% -> 12% of each run, Pallas kernels for 0% -> 15%
where the time goes in v3:
time: 200 us; the launch traced here: 199 us
  waiting for transfers between devices  72 us (36%)
  Pallas kernels  51 us (26%)
  starting transfers between devices  29.9 us (15%)
  local copies, waits for them, and re-layouts  26.5 us (13%)
  other arithmetic  9.81 us (5%)
  matrix products  7.84 us (4%)
    ppermute x3, waiting for transfers between devices, ring_next(): return lax.ppermute(value, BOTH, pairs)  34.4 us
    ppermute x17, waiting for transfers between devices, seq_xor(): return lax.ppermute(value, 'seq', [(s, s ^ bit) for s in range(self.seqs)])  18.6 us
    pallas_call x3, Pallas kernels, ffn_kernel(): pl.pallas_call(lambda *refs: ffn_body(len(rows), len(chunks), splits, *re...  18.5 us
    ppermute x11, waiting for transfers between devices, y(): lax.ppermute(value, 'group', [(g, g ^ 1) for g in range(self.groups)])  16.3 us
    pallas_call x2, Pallas kernels, attend_far(): pl.pallas_call(far_body, grid=(1,), in_specs=[whole_spec(rows), weight_sp...  16.3 us
    pallas_call x2, Pallas kernels, attend_own(): pl.pallas_call(own_body, grid=(1,), in_specs=[whole_spec(rows)] + [weight...  13.9 us
    ppermute x17, starting transfers between devices, seq_xor(): return lax.ppermute(value, 'seq', [(s, s ^ bit) for s in range(self.seqs)])  12.3 us
    ppermute x11, starting transfers between devices, y(): lax.ppermute(value, 'group', [(g, g ^ 1) for g in range(self.groups)])  12.1 us
  transfers between devices with their start and end apart: 34, of which 18 were waited for; matrix products, arithmetic and copies ran while one was open for 12% of the time, Pallas kernels for 15%

profile of v3, /device:TPU:0, one launch (start us, length us, event | category | flops | bytes accessed | tf_op | source)
XLA Modules:
  0.0 198.8 jit_solution(4617874983681958113)
XLA Ops:
  0.7 2.0 slice-done
  3.5 3.0 %collective-permute-start = (bf16[160,1536]{1,0:T(8,128)(2,1)}, bf16[160,1536]{1,0:T(8,128)(2,1)}, u32[]{:S(2)}, u32[]{:S(2)}) collective-permute-start(bf16[160,1536]{1,0:T(8,128)(2,1)} %bitcast.90), channel_id=1, source_target_pairs={{0,16},{16,0},{1,17},{17,1},{2,18},{18,2},{3,19},{19,3},{4,20},{20... | collective-permute-start | bytes 1474568 | tf_op jit(solution)/shard_map/ppermute | solution.py:171
  6.5 0.9 copy.30.gate_ref
  7.4 0.9 copy.31.up_ref
  8.3 0.9 copy.32.down_ref
  9.3 2.3 %pack.1.refs_4_ = bf16[2304,128]{1,0:T(8,128)(2,1)} custom-call(bf16[1536,64]{1,0:T(8,128)(2,1)} %copy.30.gate_ref, bf16[1536,64]{1,0:T(8,128)(2,1)} %copy.31.up_ref, bf16[1536,64]{1,0:T(8,128)(2,1)} %copy.32.down_ref), custom_call_target="tpu_custom_call" | custom-call | tf_op jit(solution)/shard_map/pack/pallas_call | solution.py:214
  11.6 1.6 collective-permute-start.3
  13.9 0.9 slice_bitcast_fusion
  14.8 3.2 %collective-permute-done = bf16[160,1536]{1,0:T(8,128)(2,1)} collective-permute-done((bf16[160,1536]{1,0:T(8,128)(2,1)}, bf16[160,1536]{1,0:T(8,128)(2,1)}, u32[]{:S(2)}, u32[]{:S(2)}) %collective-permute-start) | collective-permute-done | bytes 491552 | tf_op jit(solution)/shard_map/ppermute | solution.py:171
  18.0 1.3 bitcast_select_fusion.2
  19.7 8.9 %collective-permute-done.3.refs_6_ = bf16[2304,128]{1,0:T(8,128)(2,1)} collective-permute-done((bf16[2304,128]{1,0:T(8,128)(2,1)}, bf16[2304,128]{1,0:T(8,128)(2,1)}, u32[]{:S(2)}, u32[]{:S(2)}) %collective-permute-start.3) | collective-permute-done | bytes 589856 | tf_op jit(solution)/shard_map/ppermute | solution.py:188
  29.2 1.5 collective-permute-start.1
  30.9 13.7 %collective-permute-done.4.refs_8_ = bf16[2304,128]{1,0:T(8,128)(2,1)S(1)} collective-permute-done((bf16[2304,128]{1,0:T(8,128)(2,1)}, bf16[2304,128]{1,0:T(8,128)(2,1)S(1)}, u32[]{:S(2)}, u32[]{:S(2)}) %collective-permute-start.4) | collective-permute-done | bytes 589856 | tf_op jit(solution)/shard_map/ppermute | solution.py:188
  44.6 0.9 copy-done.6
  45.5 1.5 collective-permute-start.8
  47.7 11.9 %collective-permute-done.5.refs_2_ = bf16[2304,128]{1,0:T(8,128)(2,1)} collective-permute-done((bf16[2304,128]{1,0:T(8,128)(2,1)S(1)}, bf16[2304,128]{1,0:T(8,128)(2,1)}, u32[]{:S(2)}, u32[]{:S(2)}) %collective-permute-start.5) | collective-permute-done | bytes 589856 | tf_op jit(solution)/shard_map/ppermute | solution.py:188
  60.6 0.8 copy-done.11
  61.5 8.6 %shard_map.130 = (f32[96,1536]{1,0:T(8,128)}, f32[96,1536]{1,0:T(8,128)}, f32[96,1536]{1,0:T(8,128)}, f32[96,1536]{1,0:T(8,128)}, f32[96,1536]{1,0:T(8,128)}, /*...) custom-call(bf16[192,1536]{1,0:T(8,128)(2,1)} %copy-done.11, bf16[192,1536]{1,0:T(8,128)(2,1)} %copy-done.10, ...), custom_call_target="tpu_custom_call" | custom-call | flops 2717908992 | bytes 5898240 | tf_op jit(solution)/shard_map/pallas_call | solution.py:257
  70.1 4.8 %shard_map.132 = (bf16[96,1536]{1,0:T(8,128)(2,1)}, bf16[96,1536]{1,0:T(8,128)(2,1)}, bf16[96,1536]{1,0:T(8,128)(2,1)}, bf16[96,1536]{1,0:T(8,128)(2,1)}) custom-call(bf16[192,1536]{1,0:T(8,128)(2,1)} %copy-done.11, bf16[192,1536]{1,0:T(8,128)(2,1)} %copy-done.10, bf16[2304,128]{1,0:T(8,128)(2,1)} %collective-permute-done.5.refs_2_, ...), custom_call_target="tpu_custom_call" | custom-call | flops 452984832 | bytes 2359296 | tf_op jit(solution)/shard_map/pallas_call | solution.py:257
  74.9 0.9 collective-permute-start.13
  75.9 1.1 collective-permute-start.12
  76.9 1.5 collective-permute-start.16
  79.0 5.1 %shard_map.131 = (f32[96,1536]{1,0:T(8,128)}, f32[96,1536]{1,0:T(8,128)}, f32[96,1536]{1,0:T(8,128)}, f32[96,1536]{1,0:T(8,128)}) custom-call(bf16[192,1536]{1,0:T(8,128)(2,1)} %copy-done.7, bf16[192,1536]{1,0:T(8,128)(2,1)} %copy-done.6, bf16[2304,128]{1,0:T(8,128)(2,1)} %collective-permute-done.5.refs_2_, ...), custom_call_target="tpu_custom_call" | custom-call | flops 452984832 | bytes 2359296 | tf_op jit(solution)/shard_map/pallas_call | solution.py:257
  84.1 1.0 collective-permute-done.13
  85.1 1.3 add_convert_fusion.1
  86.4 1.6 collective-permute-start.14
  87.9 1.0 add_convert_fusion
  89.5 1.6 collective-permute-done.12
  91.2 7.5 %collective-permute-done.14 = bf16[96,1536]{1,0:T(8,128)(2,1)S(1)} collective-permute-done((bf16[96,1536]{1,0:T(8,128)(2,1)S(1)}, bf16[96,1536]{1,0:T(8,128)(2,1)S(1)}, u32[]{:S(2)}, u32[]{:S(2)}) %collective-permute-start.14) | collective-permute-done | bytes 294944 | tf_op jit(solution)/shard_map/ppermute | solution.py:162
  100.8 0.9 collective-permute-start.19
  101.7 2.9 %convolution_convert_fusion = bf16[352,768]{1,0:T(8,128)(2,1)} fusion(bf16[768,768]{1,0:T(8,128)(2,1)} %param.20, pred[352]{0:T(512)(128)(4,1)S(1)} %iota_compare_fusion.1, bf16[1,384,768]{2,1,0:T(8,128)(2,1)} %param.21), kind=kOutput, calls=%fused_computation.9 | convolution fusion | flops 415776768 | bytes 2261344 | tf_op jit(solution)/shard_map/dot_general | solution.py:30
  105.4 1.1 collective-permute-start.18
  107.3 2.1 %copy.34 = bf16[352,768]{0,1:T(8,128)(2,1)} copy(bf16[352,768]{1,0:T(8,128)(2,1)} %convolution_convert_fusion) | data formatting | bytes 1081344 | tf_op jit(solution)/shard_map/convert_element_type | solution.py:388
  109.5 2.0 collective-permute-done.20
  111.5 4.3 %collective-permute-done.21 = bf16[48,768]{1,0:T(8,128)(2,1)S(1)} collective-permute-done((bf16[48,768]{1,0:T(8,128)(2,1)S(1)}, bf16[48,768]{1,0:T(8,128)(2,1)S(1)}, u32[]{:S(2)}, u32[]{:S(2)}) %collective-permute-start.21) | collective-permute-done | bytes 73760 | tf_op jit(solution)/shard_map/ppermute | solution.py:162
  116.0 1.6 collective-permute-start.22
  117.8 1.0 fusion.5.rows_ref
  118.8 2.5 %collective-permute-done.22 = bf16[96,768]{1,0:T(8,128)(2,1)S(1)} collective-permute-done((bf16[96,768]{1,0:T(8,128)(2,1)S(1)}, bf16[96,768]{1,0:T(8,128)(2,1)S(1)}, u32[]{:S(2)}, u32[]{:S(2)}) %collective-permute-start.22) | collective-permute-done | bytes 147488 | tf_op jit(solution)/shard_map/ppermute | solution.py:162
  121.6 6.9 %attend_own.3 = (bf16[384,352]{1,0:T(8,128)(2,1)}, bf16[8,352,352]{2,1,0:T(8,128)(2,1)}, f32[8,1,352]{2,1,0:T(1,128)}, f32[8,1,352]{2,1,0:T(1,128)}, f32[384,352]{1,0:T(8,128)}) custom-call(bf16[352,768]{1,0:T(8,128)(2,1)} %fusion.5.rows_ref, bf16[768,768]{1,0:T(8,128)(2,1)} %wq_ref.3, bf16[768,768]{1,0:T(8,128)(2,1)} %wk_ref.7, bf16[768,768]{1,0:T(8,128)(2,1)} %wv_ref.7, ...), custom_call_target="tpu_custom_call" | custom-call | flops 1903165440 | bytes 1982464 | tf_op jit(solution)/shard_map/attend_own/pallas_call | solution.py:114
  128.5 6.9 %attend_own.2 = (bf16[384,352]{1,0:T(8,128)(2,1)}, bf16[8,352,352]{2,1,0:T(8,128)(2,1)}, f32[8,1,352]{2,1,0:T(1,128)}, f32[8,1,352]{2,1,0:T(1,128)}, f32[384,352]{1,0:T(8,128)}) custom-call(bf16[352,768]{1,0:T(8,128)(2,1)} %fusion.5.rows_ref, bf16[768,768]{1,0:T(8,128)(2,1)} %wq_ref.3, bf16[768,768]{1,0:T(8,128)(2,1)} %wk_ref.7, bf16[768,768]{1,0:T(8,128)(2,1)} %wv_ref.7, ...), custom_call_target="tpu_custom_call" | custom-call | flops 1903165440 | bytes 1982464 | tf_op jit(solution)/shard_map/attend_own/pallas_call | solution.py:114
  135.5 4.6 %concatenate.61.rows_ref = bf16[384,768]{1,0:T(8,128)(2,1)S(1)} concatenate(bf16[12,768]{1,0:T(8,128)(2,1)S(1)} %slice.54, bf16[10,768]{1,0:T(8,128)(2,1)S(1)} %collective-permute-done.19, bf16[2,768]{1,0:T(2,128)(2,1)S(1)} %broadcast_in_dim.69, bf16[24,768]{1,0:T(8,128)(2,1)} %copy-done.12, bf16[48,768]{1,0:T(8,128)(2,1)} %copy-done.9, bf16[96,768]{1,0:T(8,128)(2,1)} %copy-done.17, ...), dimensions={0} | concatenate | bytes 1179648 | tf_op jit(solution)/shard_map/concatenate | solution.py:373
  141.0 8.2 %attend_far.2 = (bf16[384,352]{1,0:T(8,128)(2,1)}, bf16[384,352]{1,0:T(8,128)(2,1)}, bf16[384,384]{1,0:T(8,128)(2,1)}) custom-call(bf16[384,768]{1,0:T(8,128)(2,1)} %copy-done.4, bf16[768,768]{1,0:T(8,128)(2,1)} %wk_ref.7, bf16[768,768]{1,0:T(8,128)(2,1)} %wv_ref.7, f32[384,1]{1,0:T(8,128)} %select_n.177.bias_ref, bf16[768,352]{1,0:T(8,128)(2,1)} %bitcast.88, ...), custom_call_target="tpu_custom_call" | custom-call | flops 1903165440 | bytes 1982464 | tf_op jit(solution)/shard_map/attend_far/pallas_call | solution.py:138
  149.2 1.0 constant_dynamic-update-slice_fusion.1
  150.2 8.1 %attend_far.3 = (bf16[384,352]{1,0:T(8,128)(2,1)}, bf16[384,352]{1,0:T(8,128)(2,1)}, bf16[384,384]{1,0:T(8,128)(2,1)}) custom-call(bf16[384,768]{1,0:T(8,128)(2,1)} %copy-done.4, bf16[768,768]{1,0:T(8,128)(2,1)} %wk_ref.7, bf16[768,768]{1,0:T(8,128)(2,1)} %wv_ref.7, f32[384,1]{1,0:T(8,128)} %select_n.177.bias_ref, bf16[768,352]{1,0:T(8,128)(2,1)} %bitcast.89, ...), custom_call_target="tpu_custom_call" | custom-call | flops 1903165440 | bytes 1982464 | tf_op jit(solution)/shard_map/attend_far/pallas_call | solution.py:138
  158.3 1.0 constant_dynamic-update-slice_fusion
  159.3 1.9 fusion.19
  161.3 0.9 fusion.9
  165.4 1.5 copy-done.2
  166.8 0.9 fusion.10
  168.2 1.7 bitcast_add_fusion
  170.0 1.0 collective-permute-start.28
  171.0 1.2 bitcast_add_fusion.1
  172.2 1.1 collective-permute-start.25
  173.3 5.6 %collective-permute-done.28 = bf16[4,2,24,768]{3,2,1,0:T(8,128)(2,1)S(1)} collective-permute-done((bf16[4,2,24,768]{3,2,1,0:T(8,128)(2,1)S(1)}, bf16[4,2,24,768]{3,2,1,0:T(8,128)(2,1)S(1)}, u32[]{:S(2)}, u32[]{:S(2)}) %collective-permute-start.28) | collective-permute-done | bytes 294944 | tf_op jit(solution)/shard_map/ppermute | solution.py:171
  179.1 1.6 collective-permute-start.29
  181.1 1.2 collective-permute-start.26
  182.3 1.9 collective-permute-done.29
  184.3 2.0 %collective-permute-done.26 = bf16[4,24,768]{2,1,0:T(8,128)(2,1)S(1)} collective-permute-done((bf16[4,24,768]{2,1,0:T(8,128)(2,1)S(1)}, bf16[4,24,768]{2,1,0:T(8,128)(2,1)S(1)}, u32[]{:S(2)}, u32[]{:S(2)}) %collective-permute-start.26) | collective-permute-done | bytes 147488 | tf_op jit(solution)/shard_map/ppermute | solution.py:171
  186.5 1.0 collective-permute-start.31
  187.5 2.8 %collective-permute-start.32 = (bf16[24,1536]{1,0:T(8,128)(2,1)S(1)}, bf16[24,1536]{1,0:T(8,128)(2,1)S(1)}, u32[]{:S(2)}, u32[]{:S(2)}) collective-permute-start(bf16[24,1536]{1,0:T(8,128)(2,1)S(1)} %get-tuple-element.72), channel_id=1, source_target_pairs={{0,12},{1,13},{2,14},{3,15},{4,0},{5,1},{6,2},{7,3},{8,4},{9,5},{1... | collective-permute-start | bytes 221192 | tf_op jit(solution)/shard_map/ppermute | solution.py:178
  191.0 1.8 collective-permute-done.30
  193.6 1.1 collective-permute-start.33
  194.7 0.9 pad_bitcast_fusion
  195.6 2.5 %collective-permute-done.33 = bf16[24,1536]{1,0:T(8,128)(2,1)S(1)} collective-permute-done((bf16[24,1536]{1,0:T(8,128)(2,1)S(1)}, bf16[24,1536]{1,0:T(8,128)(2,1)S(1)}, u32[]{:S(2)}, u32[]{:S(2)}) %collective-permute-start.33) | collective-permute-done | bytes 73760 | tf_op jit(solution)/shard_map/ppermute | solution.py:171
  (144 shorter events, 17.1 us)
Async XLA Ops:
  0.6 98.5 %copy-start = (bf16[1536,768]{1,0:T(8,128)(2,1)S(1)}, bf16[1536,768]{1,0:T(8,128)(2,1)}, u32[]{:S(2)}) copy-start(bf16[1536,768]{1,0:T(8,128)(2,1)} %param.16) | copy-start | bytes 7077892
  0.6 2.0 %slice-start = ((bf16[1,384,1536]{2,1,0:T(8,128)(2,1)}), bf16[1,160,1536]{2,1,0:T(8,128)(2,1)S(1)}, s32[]{:S(2)}) async-start(bf16[1,384,1536]{2,1,0:T(8,128)(2,1)} %param.11), calls=%async_computation | async-start | bytes 983040 | tf_op jit(solution)/shard_map/slice | solution.py:290
  0.7 5.8 %copy-start.22 = (bf16[1536,64]{0,1:T(8,128)(2,1)S(1)}, bf16[1536,64]{0,1:T(8,128)(2,1)}, u32[]{:S(2)}) copy-start(bf16[1536,64]{0,1:T(8,128)(2,1)} %param.13) | copy-start | bytes 589828
  0.7 6.7 %copy-start.23 = (bf16[1536,64]{0,1:T(8,128)(2,1)S(1)}, bf16[1536,64]{0,1:T(8,128)(2,1)}, u32[]{:S(2)}) copy-start(bf16[1536,64]{0,1:T(8,128)(2,1)} %param.14) | copy-start | bytes 589828
  0.7 7.7 %copy-start.24 = (bf16[1536,64]{0,1:T(8,128)(2,1)S(1)}, bf16[1536,64]{0,1:T(8,128)(2,1)}, u32[]{:S(2)}) copy-start(bf16[1536,64]{0,1:T(8,128)(2,1)} %param.15) | copy-start | bytes 589828
  3.5 14.5 %collective-permute-start = (bf16[160,1536]{1,0:T(8,128)(2,1)}, bf16[160,1536]{1,0:T(8,128)(2,1)}, u32[]{:S(2)}, u32[]{:S(2)}) collective-permute-start(bf16[160,1536]{1,0:T(8,128)(2,1)} %bitcast.90), channel_id=1, source_target_pairs={{0,16},{16,0},{1,17},{17,1},{2,18},{18,2},{3,19},{19,3},{4,20},{20... | collective-permute-start | bytes 1474568 | tf_op jit(solution)/shard_map/ppermute | solution.py:171
  11.6 17.0 %collective-permute-start.3 = (bf16[2304,128]{1,0:T(8,128)(2,1)}, bf16[2304,128]{1,0:T(8,128)(2,1)}, u32[]{:S(2)}, u32[]{:S(2)}) collective-permute-start(bf16[2304,128]{1,0:T(8,128)(2,1)} %pack.1.refs_4_), channel_id=1, source_target_pairs={{0,4},{1,5},{2,6},{3,7},{4,8},{5,9},{6,10},{7,11},{8,12},{9,13},{1... | collective-permute-start | bytes 1769480 | tf_op jit(solution)/shard_map/ppermute | solution.py:188
  19.5 9.7 %copy-start.13 = (bf16[2304,128]{1,0:T(8,128)(2,1)S(1)}, bf16[2304,128]{1,0:T(8,128)(2,1)}, u32[]{:S(2)}) copy-start(bf16[2304,128]{1,0:T(8,128)(2,1)} %pack.1.refs_4_) | copy-start | bytes 1769476
  28.6 16.0 %collective-permute-start.4 = (bf16[2304,128]{1,0:T(8,128)(2,1)}, bf16[2304,128]{1,0:T(8,128)(2,1)S(1)}, u32[]{:S(2)}, u32[]{:S(2)}) collective-permute-start(bf16[2304,128]{1,0:T(8,128)(2,1)} %collective-permute-done.3.refs_6_), channel_id=1, source_target_pairs={{0,4},{1,5},{2,6},{3,7},{4,8},{5,9},{6,10},{7,11},{8,12},{9,13},{1... | collective-permute-start | bytes 1769480 | tf_op jit(solution)/shard_map/ppermute | solution.py:188
  28.6 16.0 %collective-permute-start.2 = (bf16[96,1536]{1,0:T(8,128)(2,1)S(1)}, bf16[96,1536]{1,0:T(8,128)(2,1)S(1)}, u32[]{:S(2)}, u32[]{:S(2)}) collective-permute-start(bf16[96,1536]{1,0:T(8,128)(2,1)S(1)} %get-tuple-element.67), channel_id=1, source_target_pairs={{0,16},{16,0},{1,17},{17,1},{2,18},{18,2},{3,19},{19,3},{4,20},{20... | collective-permute-start | bytes 884744 | tf_op jit(solution)/shard_map/ppermute | solution.py:171
  29.2 18.5 %collective-permute-start.9 = (bf16[2304,128]{1,0:T(8,128)(2,1)S(1)}, bf16[2304,128]{1,0:T(8,128)(2,1)S(1)}, u32[]{:S(2)}, u32[]{:S(2)}) collective-permute-start(bf16[2304,128]{1,0:T(8,128)(2,1)S(1)} %copy-done.13), channel_id=1, source_target_pairs={{0,1},{1,0},{2,3},{3,2},{4,5},{5,4},{6,7},{7,6},{8,9},{9,8},{10,11... | collective-permute-start | bytes 1769480 | tf_op jit(solution)/shard_map/ppermute | solution.py:162
  29.2 17.8 %collective-permute-start.1 = (bf16[96,1536]{1,0:T(8,128)(2,1)S(1)}, bf16[96,1536]{1,0:T(8,128)(2,1)S(1)}, u32[]{:S(2)}, u32[]{:S(2)}) collective-permute-start(bf16[96,1536]{1,0:T(8,128)(2,1)S(1)} %get-tuple-element.68), channel_id=1, source_target_pairs={{0,2},{1,3},{2,0},{3,1},{4,6},{5,7},{6,4},{7,5},{8,10},{9,11},{10,... | collective-permute-start | bytes 884744 | tf_op jit(solution)/shard_map/ppermute | solution.py:162
  30.7 28.9 %collective-permute-start.10 = (bf16[2304,128]{1,0:T(8,128)(2,1)}, bf16[2304,128]{1,0:T(8,128)(2,1)S(1)}, u32[]{:S(2)}, u32[]{:S(2)}) collective-permute-start(bf16[2304,128]{1,0:T(8,128)(2,1)} %collective-permute-done.3.refs_6_), channel_id=1, source_target_pairs={{0,1},{1,0},{2,3},{3,2},{4,5},{5,4},{6,7},{7,6},{8,9},{9,8},{10,11... | collective-permute-start | bytes 1769480 | tf_op jit(solution)/shard_map/ppermute | solution.py:162
  44.6 3.1 %copy-start.26 = (bf16[2304,128]{1,0:T(8,128)(2,1)}, bf16[2304,128]{1,0:T(8,128)(2,1)S(1)}, u32[]{:S(2)}) copy-start(bf16[2304,128]{1,0:T(8,128)(2,1)S(1)} %collective-permute-done.4.refs_8_) | copy-start | bytes 1769476
  44.6 15.0 %collective-permute-start.5 = (bf16[2304,128]{1,0:T(8,128)(2,1)S(1)}, bf16[2304,128]{1,0:T(8,128)(2,1)}, u32[]{:S(2)}, u32[]{:S(2)}) collective-permute-start(bf16[2304,128]{1,0:T(8,128)(2,1)S(1)} %collective-permute-done.4.refs_8_), channel_id=1, source_target_pairs={{0,4},{1,5},{2,6},{3,7},{4,8},{5,9},{6,10},{7,11},{8,12},{9,13},{1... | collective-permute-start | bytes 1769480 | tf_op jit(solution)/shard_map/ppermute | solution.py:188
  44.6 0.9 copy-start.6
  45.5 14.1 %collective-permute-start.8 = (bf16[192,1536]{1,0:T(8,128)(2,1)S(1)}, bf16[192,1536]{1,0:T(8,128)(2,1)S(1)}, u32[]{:S(2)}, u32[]{:S(2)}) collective-permute-start(bf16[192,1536]{1,0:T(8,128)(2,1)S(1)} %pad_maximum_fusion.3.refs_3_.refs_1_), channel_id=1, source_target_pairs={{0,2},{1,3},{2,0},{3,1},{4,6},{5,7},{6,4},{7,5},{8,10},{9,11},{10,... | collective-permute-start | bytes 1769480 | tf_op jit(solution)/shard_map/ppermute | solution.py:162
  47.0 12.6 %copy-start.7 = (bf16[192,1536]{1,0:T(8,128)(2,1)}, bf16[192,1536]{1,0:T(8,128)(2,1)S(1)}, u32[]{:S(2)}) copy-start(bf16[192,1536]{1,0:T(8,128)(2,1)S(1)} %pad_maximum_fusion.2.refs_2_.refs_0_) | copy-start | bytes 1769476
  47.1 12.9 %collective-permute-start.7 = (bf16[192,1536]{1,0:T(8,128)(2,1)S(1)}, bf16[192,1536]{1,0:T(8,128)(2,1)S(1)}, u32[]{:S(2)}, u32[]{:S(2)}) collective-permute-start(bf16[192,1536]{1,0:T(8,128)(2,1)S(1)} %pad_maximum_fusion.2.refs_2_.refs_0_), channel_id=1, source_target_pairs={{0,16},{16,0},{1,17},{17,1},{2,18},{18,2},{3,19},{19,3},{4,20},{20... | collective-permute-start | bytes 1769480 | tf_op jit(solution)/shard_map/ppermute | solution.py:171
  47.6 12.3 %copy-start.27 = (bf16[2304,128]{1,0:T(8,128)(2,1)}, bf16[2304,128]{1,0:T(8,128)(2,1)S(1)}, u32[]{:S(2)}) copy-start(bf16[2304,128]{1,0:T(8,128)(2,1)S(1)} %collective-permute-done.9.refs_5_) | copy-start | bytes 1769476
  47.6 13.9 %collective-permute-start.11 = (bf16[2304,128]{1,0:T(8,128)(2,1)S(1)}, bf16[2304,128]{1,0:T(8,128)(2,1)}, u32[]{:S(2)}, u32[]{:S(2)}) collective-permute-start(bf16[2304,128]{1,0:T(8,128)(2,1)S(1)} %collective-permute-done.4.refs_8_), channel_id=1, source_target_pairs={{0,1},{1,0},{2,3},{3,2},{4,5},{5,4},{6,7},{7,6},{8,9},{9,8},{10,11... | collective-permute-start | bytes 1769480 | tf_op jit(solution)/shard_map/ppermute | solution.py:162
  59.6 10.5 %collective-permute-start.6 = (bf16[2304,128]{1,0:T(8,128)(2,1)}, bf16[2304,128]{1,0:T(8,128)(2,1)}, u32[]{:S(2)}, u32[]{:S(2)}) collective-permute-start(bf16[2304,128]{1,0:T(8,128)(2,1)} %collective-permute-done.5.refs_2_), channel_id=1, source_target_pairs={{0,1},{1,0},{2,3},{3,2},{4,5},{5,4},{6,7},{7,6},{8,9},{9,8},{10,11... | collective-permute-start | bytes 1769480 | tf_op jit(solution)/shard_map/ppermute | solution.py:162
  59.6 0.8 copy-start.28
  59.6 1.0 copy-start.10
  60.6 0.8 copy-start.11
  74.9 10.2 %collective-permute-start.13 = (bf16[96,1536]{1,0:T(8,128)(2,1)}, bf16[96,1536]{1,0:T(8,128)(2,1)}, u32[]{:S(2)}, u32[]{:S(2)}) collective-permute-start(bf16[96,1536]{1,0:T(8,128)(2,1)} %get-tuple-element.46), channel_id=1, source_target_pairs={{0,16},{16,0},{1,17},{17,1},{2,18},{18,2},{3,19},{19,3},{4,20},{20... | collective-permute-start | bytes 884744 | tf_op jit(solution)/shard_map/ppermute | solution.py:171
  75.9 15.3 %collective-permute-start.12 = (bf16[96,1536]{1,0:T(8,128)(2,1)}, bf16[96,1536]{1,0:T(8,128)(2,1)S(1)}, u32[]{:S(2)}, u32[]{:S(2)}) collective-permute-start(bf16[96,1536]{1,0:T(8,128)(2,1)} %get-tuple-element.44), channel_id=1, source_target_pairs={{0,16},{16,0},{1,17},{17,1},{2,18},{18,2},{3,19},{19,3},{4,20},{20... | collective-permute-start | bytes 884744 | tf_op jit(solution)/shard_map/ppermute | solution.py:171
  76.9 11.0 %collective-permute-start.16 = (bf16[96,1536]{1,0:T(8,128)(2,1)}, bf16[96,1536]{1,0:T(8,128)(2,1)}, u32[]{:S(2)}, u32[]{:S(2)}) collective-permute-start(bf16[96,1536]{1,0:T(8,128)(2,1)} %get-tuple-element.50), channel_id=1, source_target_pairs={{0,2},{1,3},{2,0},{3,1},{4,6},{5,7},{6,4},{7,5},{8,10},{9,11},{10,... | collective-permute-start | bytes 884744 | tf_op jit(solution)/shard_map/ppermute | solution.py:162
  78.4 20.3 %collective-permute-start.15 = (bf16[96,1536]{1,0:T(8,128)(2,1)}, bf16[96,1536]{1,0:T(8,128)(2,1)S(1)}, u32[]{:S(2)}, u32[]{:S(2)}) collective-permute-start(bf16[96,1536]{1,0:T(8,128)(2,1)} %get-tuple-element.48), channel_id=1, source_target_pairs={{0,2},{1,3},{2,0},{3,1},{4,6},{5,7},{6,4},{7,5},{8,10},{9,11},{10,... | collective-permute-start | bytes 884744 | tf_op jit(solution)/shard_map/ppermute | solution.py:162
  84.1 3.8 %copy-start.16 = (f32[96,1536]{1,0:T(8,128)S(1)}, f32[96,1536]{1,0:T(8,128)}, u32[]{:S(2)}) copy-start(f32[96,1536]{1,0:T(8,128)} %get-tuple-element.49) | copy-start | bytes 1769476
  85.1 13.5 %copy-start.15 = (f32[96,1536]{1,0:T(8,128)S(1)}, f32[96,1536]{1,0:T(8,128)}, u32[]{:S(2)}) copy-start(f32[96,1536]{1,0:T(8,128)} %get-tuple-element.39) | copy-start | bytes 1769476
  86.4 12.3 %collective-permute-start.14 = (bf16[96,1536]{1,0:T(8,128)(2,1)S(1)}, bf16[96,1536]{1,0:T(8,128)(2,1)S(1)}, u32[]{:S(2)}, u32[]{:S(2)}) collective-permute-start(bf16[96,1536]{1,0:T(8,128)(2,1)S(1)} %add_convert_fusion.1), channel_id=1, source_target_pairs={{0,2},{1,3},{2,0},{3,1},{4,6},{5,7},{6,4},{7,5},{8,10},{9,11},{10,... | collective-permute-start | bytes 884744 | tf_op jit(solution)/shard_map/ppermute | solution.py:162
  88.9 9.8 %copy-start.14 = (f32[96,1536]{1,0:T(8,128)S(1)}, f32[96,1536]{1,0:T(8,128)}, u32[]{:S(2)}) copy-start(f32[96,1536]{1,0:T(8,128)} %get-tuple-element.47) | copy-start | bytes 1769476
  89.0 9.8 %collective-permute-start.17 = (bf16[96,1536]{1,0:T(8,128)(2,1)S(1)}, bf16[96,1536]{1,0:T(8,128)(2,1)S(1)}, u32[]{:S(2)}, u32[]{:S(2)}) collective-permute-start(bf16[96,1536]{1,0:T(8,128)(2,1)S(1)} %add_convert_fusion), channel_id=1, source_target_pairs={{0,16},{16,0},{1,17},{17,1},{2,18},{18,2},{3,19},{19,3},{4,20},{20... | collective-permute-start | bytes 884744 | tf_op jit(solution)/shard_map/ppermute | solution.py:171
  100.8 5.7 %collective-permute-start.19 = (bf16[10,768]{1,0:T(8,128)(2,1)}, bf16[10,768]{1,0:T(8,128)(2,1)S(1)}, u32[]{:S(2)}, u32[]{:S(2)}) collective-permute-start(bf16[10,768]{1,0:T(8,128)(2,1)} %slice.56), channel_id=1, source_target_pairs={{0,16},{16,0},{1,17},{17,1},{2,18},{18,2},{3,19},{19,3},{4,20},{20... | collective-permute-start | bytes 46088 | tf_op jit(solution)/shard_map/ppermute | solution.py:171
  105.4 12.2 %collective-permute-start.18 = (bf16[160,768]{1,0:T(8,128)(2,1)}, bf16[160,768]{1,0:T(8,128)(2,1)S(1)}, u32[]{:S(2)}, u32[]{:S(2)}) collective-permute-start(bf16[160,768]{1,0:T(8,128)(2,1)} %bitcast.6), channel_id=1, source_target_pairs={{0,16},{16,0},{1,17},{17,1},{2,18},{18,2},{3,19},{19,3},{4,20},{20... | collective-permute-start | bytes 737288 | tf_op jit(solution)/shard_map/ppermute | solution.py:171
  106.5 4.9 %collective-permute-start.20 = (bf16[24,768]{1,0:T(8,128)(2,1)S(1)}, bf16[24,768]{1,0:T(8,128)(2,1)S(1)}, u32[]{:S(2)}, u32[]{:S(2)}) collective-permute-start(bf16[24,768]{1,0:T(8,128)(2,1)S(1)} %pad_maximum_fusion.6), channel_id=1, source_target_pairs={{0,8},{1,9},{2,10},{3,11},{4,12},{5,13},{6,14},{7,15},{8,0},{9,1},... | collective-permute-start | bytes 110600 | tf_op jit(solution)/shard_map/ppermute | solution.py:162
  111.4 10.1 %copy-start.12 = (bf16[24,768]{1,0:T(8,128)(2,1)}, bf16[24,768]{1,0:T(8,128)(2,1)S(1)}, u32[]{:S(2)}) copy-start(bf16[24,768]{1,0:T(8,128)(2,1)S(1)} %collective-permute-done.20) | copy-start | bytes 110596
  111.5 4.4 %collective-permute-start.21 = (bf16[48,768]{1,0:T(8,128)(2,1)S(1)}, bf16[48,768]{1,0:T(8,128)(2,1)S(1)}, u32[]{:S(2)}, u32[]{:S(2)}) collective-permute-start(bf16[48,768]{1,0:T(8,128)(2,1)S(1)} %pad_maximum_fusion.5), channel_id=1, source_target_pairs={{0,4},{1,5},{2,6},{3,7},{4,0},{5,1},{6,2},{7,3},{8,12},{9,13},{10,... | collective-permute-start | bytes 221192 | tf_op jit(solution)/shard_map/ppermute | solution.py:162
  115.9 5.6 %copy-start.9 = (bf16[48,768]{1,0:T(8,128)(2,1)}, bf16[48,768]{1,0:T(8,128)(2,1)S(1)}, u32[]{:S(2)}) copy-start(bf16[48,768]{1,0:T(8,128)(2,1)S(1)} %collective-permute-done.21) | copy-start | bytes 221188
  116.0 5.2 %collective-permute-start.22 = (bf16[96,768]{1,0:T(8,128)(2,1)S(1)}, bf16[96,768]{1,0:T(8,128)(2,1)S(1)}, u32[]{:S(2)}, u32[]{:S(2)}) collective-permute-start(bf16[96,768]{1,0:T(8,128)(2,1)S(1)} %concatenate.59), channel_id=1, source_target_pairs={{0,2},{1,3},{2,0},{3,1},{4,6},{5,7},{6,4},{7,5},{8,10},{9,11},{10,... | collective-permute-start | bytes 442376 | tf_op jit(solution)/shard_map/ppermute | solution.py:162
  121.2 7.3 %copy-start.17 = (bf16[96,768]{1,0:T(8,128)(2,1)}, bf16[96,768]{1,0:T(8,128)(2,1)S(1)}, u32[]{:S(2)}) copy-start(bf16[96,768]{1,0:T(8,128)(2,1)S(1)} %collective-permute-done.22) | copy-start | bytes 442372
  121.5 14.0 %collective-permute-start.23 = (bf16[192,768]{1,0:T(8,128)(2,1)S(1)}, bf16[192,768]{1,0:T(8,128)(2,1)}, u32[]{:S(2)}, u32[]{:S(2)}) collective-permute-start(bf16[192,768]{1,0:T(8,128)(2,1)S(1)} %concatenate.60), channel_id=1, source_target_pairs={{0,1},{1,0},{2,3},{3,2},{4,5},{5,4},{6,7},{7,6},{8,9},{9,8},{10,11... | collective-permute-start | bytes 884744 | tf_op jit(solution)/shard_map/ppermute | solution.py:162
  140.0 1.0 copy-start.4
  161.3 1.6 copy-start.1
  161.3 1.6 copy-start.8
  161.3 1.7 copy-start.20
  161.3 2.0 %copy-start.21 = (bf16[384,352]{1,0:T(8,128)(2,1)S(1)}, bf16[384,352]{1,0:T(8,128)(2,1)}, u32[]{:S(2)}) copy-start(bf16[384,352]{1,0:T(8,128)(2,1)} %get-tuple-element.64) | copy-start | bytes 811012
  162.2 6.0 %collective-permute-start.27 = (bf16[4,2,2,24,768]{4,3,2,1,0:T(8,128)(2,1)}, bf16[4,2,2,24,768]{4,3,2,1,0:T(8,128)(2,1)}, u32[]{:S(2)}, u32[]{:S(2)}) collective-permute-start(bf16[4,2,2,24,768]{4,3,2,1,0:T(8,128)(2,1)} %fusion.9), channel_id=1, source_target_pairs={{0,1},{1,0},{2,3},{3,2},{4,5},{5,4},{6,7},{7,6},{8,9},{9,8},{10,11... | collective-permute-start | bytes 1769480 | tf_op jit(solution)/shard_map/ppermute | solution.py:162
  163.3 1.1 copy-start.5
  163.3 1.1 copy-start.18
  163.3 1.2 copy-start.19
  165.3 1.5 copy-start.2
  167.7 3.3 %collective-permute-start.24 = (bf16[4,2,2,24,768]{4,3,0,2,1:T(8,128)(2,1)}, bf16[4,2,2,24,768]{4,3,0,2,1:T(8,128)(2,1)}, u32[]{:S(2)}, u32[]{:S(2)}) collective-permute-start(bf16[4,2,2,24,768]{4,3,0,2,1:T(8,128)(2,1)} %fusion.10), channel_id=1, source_target_pairs={{0,1},{1,0},{2,3},{3,2},{4,5},{5,4},{6,7},{7,6},{8,9},{9,8},{10,11... | collective-permute-start | bytes 1769480 | tf_op jit(solution)/shard_map/ppermute | solution.py:162
  168.2 2.8 %copy-start.3 = (f32[768,768]{1,0:T(8,128)S(1)}, f32[768,768]{1,0:T(8,128)}, u32[]{:S(2)}) copy-start(f32[768,768]{1,0:T(8,128)} %copy-done.2) | copy-start | bytes 7077892
  170.0 9.0 %collective-permute-start.28 = (bf16[4,2,24,768]{3,2,1,0:T(8,128)(2,1)S(1)}, bf16[4,2,24,768]{3,2,1,0:T(8,128)(2,1)S(1)}, u32[]{:S(2)}, u32[]{:S(2)}) collective-permute-start(bf16[4,2,24,768]{3,2,1,0:T(8,128)(2,1)S(1)} %fusion.27), channel_id=1, source_target_pairs={{0,16},{16,0},{1,17},{17,1},{2,18},{18,2},{3,19},{19,3},{4,20},{20... | collective-permute-start | bytes 884744 | tf_op jit(solution)/shard_map/ppermute | solution.py:171
  172.2 8.8 %collective-permute-start.25 = (bf16[4,2,24,768]{3,2,0,1:T(8,128)(2,1)S(1)}, bf16[4,2,24,768]{3,2,0,1:T(8,128)(2,1)S(1)}, u32[]{:S(2)}, u32[]{:S(2)}) collective-permute-start(bf16[4,2,24,768]{3,2,0,1:T(8,128)(2,1)S(1)} %fusion.26), channel_id=1, source_target_pairs={{0,2},{1,3},{2,0},{3,1},{4,6},{5,7},{6,4},{7,5},{8,10},{9,11},{10,... | collective-permute-start | bytes 884744 | tf_op jit(solution)/shard_map/ppermute | solution.py:162
  179.1 5.2 %collective-permute-start.29 = (bf16[4,24,768]{2,1,0:T(8,128)(2,1)S(1)}, bf16[4,24,768]{2,1,0:T(8,128)(2,1)S(1)}, u32[]{:S(2)}, u32[]{:S(2)}) collective-permute-start(bf16[4,24,768]{2,1,0:T(8,128)(2,1)S(1)} %fusion.32), channel_id=1, source_target_pairs={{0,2},{1,3},{2,0},{3,1},{4,6},{5,7},{6,4},{7,5},{8,10},{9,11},{10,... | collective-permute-start | bytes 442376 | tf_op jit(solution)/shard_map/ppermute | solution.py:162
  181.1 5.2 %collective-permute-start.26 = (bf16[4,24,768]{2,1,0:T(8,128)(2,1)S(1)}, bf16[4,24,768]{2,1,0:T(8,128)(2,1)S(1)}, u32[]{:S(2)}, u32[]{:S(2)}) collective-permute-start(bf16[4,24,768]{2,1,0:T(8,128)(2,1)S(1)} %fusion.31), channel_id=1, source_target_pairs={{0,16},{16,0},{1,17},{17,1},{2,18},{18,2},{3,19},{19,3},{4,20},{20... | collective-permute-start | bytes 442376 | tf_op jit(solution)/shard_map/ppermute | solution.py:171
  184.3 6.0 %copy-start.25 = (bf16[768,768]{1,0:T(8,128)(2,1)S(1)}, bf16[768,768]{1,0:T(8,128)(2,1)}, u32[]{:S(2)}) copy-start(bf16[768,768]{1,0:T(8,128)(2,1)} %param.20) | copy-start | bytes 3538948
  186.4 6.3 %collective-permute-start.30 = (bf16[24,1536]{1,0:T(8,128)(2,1)S(1)}, bf16[24,1536]{1,0:T(8,128)(2,1)S(1)}, u32[]{:S(2)}, u32[]{:S(2)}) collective-permute-start(bf16[24,1536]{1,0:T(8,128)(2,1)S(1)} %get-tuple-element.71), channel_id=1, source_target_pairs={{0,4},{1,5},{2,6},{3,7},{4,8},{5,9},{6,10},{7,11},{8,12},{9,13},{1... | collective-permute-start | bytes 221192 | tf_op jit(solution)/shard_map/ppermute | solution.py:178
  186.5 7.1 %collective-permute-start.31 = (bf16[24,1536]{1,0:T(8,128)(2,1)S(1)}, bf16[24,1536]{1,0:T(8,128)(2,1)S(1)}, u32[]{:S(2)}, u32[]{:S(2)}) collective-permute-start(bf16[24,1536]{1,0:T(8,128)(2,1)S(1)} %get-tuple-element.73), channel_id=1, source_target_pairs={{0,8},{1,9},{2,10},{3,11},{4,12},{5,13},{6,14},{7,15},{8,0},{9,1},... | collective-permute-start | bytes 221192 | tf_op jit(solution)/shard_map/ppermute | solution.py:178
  187.5 6.1 %collective-permute-start.32 = (bf16[24,1536]{1,0:T(8,128)(2,1)S(1)}, bf16[24,1536]{1,0:T(8,128)(2,1)S(1)}, u32[]{:S(2)}, u32[]{:S(2)}) collective-permute-start(bf16[24,1536]{1,0:T(8,128)(2,1)S(1)} %get-tuple-element.72), channel_id=1, source_target_pairs={{0,12},{1,13},{2,14},{3,15},{4,0},{5,1},{6,2},{7,3},{8,4},{9,5},{1... | collective-permute-start | bytes 221192 | tf_op jit(solution)/shard_map/ppermute | solution.py:178
  193.6 4.4 %collective-permute-start.33 = (bf16[24,1536]{1,0:T(8,128)(2,1)S(1)}, bf16[24,1536]{1,0:T(8,128)(2,1)S(1)}, u32[]{:S(2)}, u32[]{:S(2)}) collective-permute-start(bf16[24,1536]{1,0:T(8,128)(2,1)S(1)} %fusion.38), channel_id=1, source_target_pairs={{0,16},{16,0},{1,17},{17,1},{2,18},{18,2},{3,19},{19,3},{4,20},{20... | collective-permute-start | bytes 221192 | tf_op jit(solution)/shard_map/ppermute | solution.py:171

commit v4 on v3

--- a/solution.py
+++ b/solution.py
@@ -49,13 +49,67 @@
 
 
 HEADS_A_CALL = 8
-
-
-def own_body(rows_ref, wq_ref, wk_ref, wv_ref, bias_ref, q_ref, e_ref, m_ref, l_ref, o_ref):
-    bias = bias_ref[...]
+HEADS_A_STEP = 4
+
+
+def valid_column(count_ref, height):
+    return lax.broadcasted_iota(jnp.int32, (height, 1), 0) < count_ref[0, 0]
+
+
+def grads_in_body(count_ref, cotangent_ref, w_out_ref, grad_y_ref, grad_att_ref):
+    height = grad_y_ref.shape[0]
+    grad_y = cotangent_ref[:height].astype(jnp.float32)
+    grad_y = jnp.where(valid_column(count_ref, height), grad_y, 0.0).astype(jnp.bfloat16)
+    grad_y_ref[...] = grad_y
+    grad_att_ref[...] = mm_nt(w_out_ref[...], grad_y).astype(jnp.bfloat16)
+
+
+def grads_in(counts, cotangent, w_out, live):
+    width = w_out.shape[0]
+    return pl.pallas_call(
+        grads_in_body,
+        in_specs=[pl.BlockSpec(memory_space=pltpu.SMEM), NEAR, NEAR],
+        out_specs=[NEAR] * 2,
+        out_shape=[
+            pltpu.VMEM((live, width), jnp.bfloat16),
+            pltpu.VMEM((width, live), jnp.bfloat16),
+        ],
+        compiler_params=room(8),
+        name="grads_in",
+    )(counts, *near(cotangent, w_out))
+
+
+FAR_AWAY = pl.BlockSpec(memory_space=pltpu.HBM)
+
+
+def fetch(sources, targets, sems, first=0):
+    copies = []
+    for i, (source, target) in enumerate(zip(sources, targets)):
+        copies.append(pltpu.make_async_copy(source, target, sems.at[first + i]))
+        copies[-1].start()
+    return copies
+
+
+def own_body(
+    part, count_ref, rows_in, wq_in, wk_in, wv_in, q_out, e_out, m_out, l_out, o_out,
+    rows_ref, wq_ref, wk_ref, wv_ref, q_ref, e_ref, m_ref, l_ref, o_ref, sems,
+):
+    cut = pl.ds(part * HEADS_A_CALL * HEAD, HEADS_A_CALL * HEAD)
+    got = fetch(
+        (rows_in, wq_in.at[:, cut], wk_in.at[:, cut], wv_in.at[:, cut]),
+        (rows_ref, wq_ref, wk_ref, wv_ref),
+        sems,
+    )
+    got[0].wait()
     rows = rows_ref[...]
+    bias = jnp.where(valid_column(count_ref, rows.shape[0]), 0.0, -1e30)
+    got[1].wait()
     q_ref[...] = project_t(wq_ref[...], rows)
-    keys, values = project_t(wk_ref[...], rows), project_t(wv_ref[...], rows)
+    got[2].wait()
+    keys = project_t(wk_ref[...], rows)
+    got[3].wait()
+    values = project_t(wv_ref[...], rows)
+    sent = fetch([q_ref], [q_out], sems, 4)
     for h in range(HEADS_A_CALL):
         at = slice(h * HEAD, (h + 1) * HEAD)
         scores = mm_tn(keys[at], q_ref[at]) * (1.0 / math.sqrt(HEAD)) + bias
@@ -65,91 +119,157 @@
         l_ref[h] = jnp.sum(exponent, axis=0, keepdims=True)
         low = exponent.astype(jnp.bfloat16)
         e_ref[h] = low
+        sent += fetch([e_ref.at[h]], [e_out.at[h]], sems, 8 + h)
         o_ref[at] = mm(values[at], low)
-
-
-def far_body(
-    rows_ref, wk_ref, wv_ref, bias_ref, g_ref, q_ref, e_ref, m_ref, l_ref, o_ref,
-    att_ref, own_ref, far_ref,
-):
-    bias = bias_ref[...]
+    sent += fetch((m_ref, l_ref, o_ref), (m_out, l_out, o_out), sems, 5)
+    for copy in sent:
+        copy.wait()
+
+
+def far_body(dilated, *refs):
+    parts = HEADS // HEADS_A_CALL
+    count = 6 + 5 * parts
+    core_ref, ins, outs = refs[0], refs[1 : 1 + count], refs[1 + count : 6 + count]
+    held, sems = refs[6 + count : 6 + 2 * count], refs[-1]
+    keys_ref, values_ref, own_ref, far_ref, sum_ref = refs[-6:-1]
+    got = fetch(ins, held, sems)
+    rows_ref, wk_ref, wv_ref, g_ref = held[:4]
+    grad_y_ref, normed_ref = held[-2:]
+    att_ref = outs[0]
+    got[0].wait()
     rows = rows_ref[...]
-    keys, values = project_t(wk_ref[...], rows), project_t(wv_ref[...], rows)
-    for h in range(HEADS_A_CALL):
-        at = slice(h * HEAD, (h + 1) * HEAD)
-        scores = mm_tn(keys[at], q_ref[at]) * (1.0 / math.sqrt(HEAD)) + bias
-        top = jnp.maximum(jnp.max(scores, axis=0, keepdims=True), m_ref[h])
-        ratio = jnp.exp(m_ref[h] - top)
-        exponent = jnp.exp(scores - top)
-        norm = 1.0 / (l_ref[h] * ratio + jnp.sum(exponent, axis=0, keepdims=True))
-        low = exponent.astype(jnp.bfloat16)
-        att_ref[at] = ((o_ref[at] * ratio + mm(values[at], low)) * norm).astype(jnp.bfloat16)
-        grads = g_ref[at].astype(jnp.float32) * norm
-        far_ref[at] = mm_nt(grads.astype(jnp.bfloat16), low).astype(jnp.bfloat16)
-        own_ref[at] = mm_nt((grads * ratio).astype(jnp.bfloat16), e_ref[h]).astype(jnp.bfloat16)
-
-
-def whole_spec(array):
-    return pl.BlockSpec(array.shape, lambda i: (0,) * array.ndim)
-
-
-def weight_spec(array, part):
-    return pl.BlockSpec((array.shape[0], HEADS_A_CALL * HEAD), lambda i: (0, part))
-
-
-def feature_spec(array, part):
-    return pl.BlockSpec((HEADS_A_CALL * HEAD, array.shape[1]), lambda i: (part, 0))
-
-
-def attend_own(part, rows, w_query, w_key, w_value, bias):
+    place = lax.broadcasted_iota(jnp.int32, (dilated, 1), 0).astype(jnp.float32)
+    pieces = []
+    for end in range(dilated, rows.shape[0] + 1, dilated):
+        pieces.append(jnp.where(place < rows_ref[end - 1 : end, :1].astype(jnp.float32), 0.0, -1e30))
+    bias = jnp.concatenate(pieces, axis=0)
+    got[1].wait()
+    keys_ref[...] = project_t(wk_ref[...], rows)
+    got[2].wait()
+    values_ref[...] = project_t(wv_ref[...], rows)
+    got[3].wait()
+
+    for part in range(parts):
+        for copy in got[4 + part * 5 : 9 + part * 5]:
+            copy.wait()
+        q_ref, e_ref, m_ref, l_ref, o_ref = held[4 + part * 5 : 9 + part * 5]
+        first = part * HEADS_A_CALL * HEAD
+
+        def step(i, _):
+            for k in range(HEADS_A_STEP):
+                h = i * HEADS_A_STEP + k
+                here = pl.ds(pl.multiple_of(h * HEAD, HEAD), HEAD)
+                at = pl.ds(pl.multiple_of(first + h * HEAD, HEAD), HEAD)
+                scores = mm_tn(keys_ref[at], q_ref[here]) * (1.0 / math.sqrt(HEAD)) + bias
+                top = jnp.maximum(jnp.max(scores, axis=0, keepdims=True), m_ref[h])
+                ratio = jnp.exp(m_ref[h] - top)
+                exponent = jnp.exp(scores - top)
+                norm = 1.0 / (l_ref[h] * ratio + jnp.sum(exponent, axis=0, keepdims=True))
+                low = exponent.astype(jnp.bfloat16)
+                total = (o_ref[here] * ratio + mm(values_ref[at], low)) * norm
+                att_ref[at] = total.astype(jnp.bfloat16)
+                grads = g_ref[at].astype(jnp.float32) * norm
+                far_ref[at] = mm_nt(grads.astype(jnp.bfloat16), low).astype(jnp.bfloat16)
+                grads = (grads * ratio).astype(jnp.bfloat16)
+                own_ref[at] = mm_nt(grads, e_ref[h]).astype(jnp.bfloat16)
+            return 0
+
+        lax.fori_loop(0, HEADS_A_CALL // HEADS_A_STEP, step, 0)
+
+    def share_out(total, kept_ref, sent_ref):
+        sum_ref[...] = total
+        share = rows.shape[0] // dilated
+        share = sum_ref.shape[0] // share
+        for ref, bit in ((kept_ref, core_ref[0]), (sent_ref, 1 - core_ref[0])):
+            pieces = []
+            for first in range(0, sum_ref.shape[0], 2 * share):
+                start = pl.multiple_of(first + bit * share, 8)
+                pieces.append(sum_ref[pl.ds(start, share)])
+            ref[...] = jnp.concatenate(pieces, axis=0).astype(ref.dtype)
+
+    got[-2].wait()
+    share_out(mm(att_ref[...], grad_y_ref[...]), outs[1], outs[2])
+    got[-1].wait()
+    total = mm_tt(normed_ref[...], own_ref[...]) + mm_tt(rows, far_ref[...])
+    share_out(total, outs[3], outs[4])
+
+
+def attend_own(part, counts, rows, w_query, w_key, w_value):
     count = rows.shape[0]
     features = HEADS_A_CALL * HEAD
     outs = [
-        jax.ShapeDtypeStruct((features, count), jnp.bfloat16),
-        jax.ShapeDtypeStruct((HEADS_A_CALL, count, count), jnp.bfloat16),
-        jax.ShapeDtypeStruct((HEADS_A_CALL, 1, count), jnp.float32),
-        jax.ShapeDtypeStruct((HEADS_A_CALL, 1, count), jnp.float32),
-        jax.ShapeDtypeStruct((features, count), jnp.float32),
+        pltpu.HBM((features, count), jnp.bfloat16),
+        pltpu.HBM((HEADS_A_CALL, count, count), jnp.bfloat16),
+        pltpu.HBM((HEADS_A_CALL, 1, count), jnp.float32),
+        pltpu.HBM((HEADS_A_CALL, 1, count), jnp.float32),
+        pltpu.HBM((features, count), jnp.float32),
     ]
-    return pl.pallas_call(
-        own_body,
-        grid=(1,),
-        in_specs=[whole_spec(rows)]
-        + [weight_spec(w, part) for w in (w_query, w_key, w_value)]
-        + [whole_spec(bias)],
-        out_specs=[whole_spec(o) for o in outs],
+    cut = pltpu.VMEM((rows.shape[1], features), jnp.bfloat16)
+    return pl.pallas_call(
+        lambda *refs: own_body(part, *refs),
+        in_specs=[pl.BlockSpec(memory_space=pltpu.SMEM)] + [FAR_AWAY] * 4,
+        out_specs=[FAR_AWAY] * 5,
         out_shape=outs,
+        scratch_shapes=[
+            pltpu.VMEM(rows.shape, jnp.bfloat16),
+            cut,
+            cut,
+            cut,
+        ]
+        + [pltpu.VMEM(o.shape, o.dtype) for o in outs]
+        + [pltpu.SemaphoreType.DMA((8 + HEADS_A_CALL,))],
+        compiler_params=room(24),
         cost_estimate=pl.CostEstimate(
             flops=40 * features * count * count,
             transcendentals=HEADS_A_CALL * count * count,
             bytes_accessed=2 * HEADS_A_CALL * count * count,
         ),
         name="attend_own",
-    )(rows, w_query, w_key, w_value, bias)
-
-
-def attend_far(part, rows, w_key, w_value, bias, grads, own):
-    count, features = grads.shape[1], HEADS_A_CALL * HEAD
-    outs = [
-        jax.ShapeDtypeStruct((features, count), jnp.bfloat16),
-        jax.ShapeDtypeStruct((features, count), jnp.bfloat16),
-        jax.ShapeDtypeStruct((features, rows.shape[0]), jnp.bfloat16),
-    ]
-    return pl.pallas_call(
-        far_body,
-        grid=(1,),
-        in_specs=[whole_spec(rows), weight_spec(w_key, part), weight_spec(w_value, part)]
-        + [whole_spec(bias), feature_spec(grads, part)]
-        + [whole_spec(o) for o in own],
-        out_specs=[whole_spec(o) for o in outs],
-        out_shape=outs,
+    )(counts, *away(rows, w_query, w_key, w_value))
+
+
+def attend_far(dilated, core_bit, rows, w_key, w_value, grads, own, grad_y, normed):
+    width, count = grads.shape
+    args = [rows, w_key, w_value, grads]
+    args += [array for arrays in own for array in arrays] + [grad_y, normed]
+    low = jnp.bfloat16
+    cut = [pltpu.VMEM((width // 2, width), jnp.float32), pltpu.VMEM((width // 2, width), low)]
+    return pl.pallas_call(
+        lambda *refs: far_body(dilated, *refs),
+        in_specs=[pl.BlockSpec(memory_space=pltpu.SMEM)] + [FAR_AWAY] * len(args),
+        out_specs=[NEAR] * 5,
+        out_shape=[pltpu.VMEM((width, count), low)] + cut + cut,
+        scratch_shapes=[pltpu.VMEM(a.shape, a.dtype) for a in args]
+        + [pltpu.VMEM((width, rows.shape[0]), low)] * 2
+        + [
+            pltpu.VMEM((width, count), low),
+            pltpu.VMEM((width, rows.shape[0]), low),
+            pltpu.VMEM((width, width), jnp.float32),
+        ]
+        + [pltpu.SemaphoreType.DMA((len(args),))],
+        compiler_params=room(40),
         cost_estimate=pl.CostEstimate(
-            flops=40 * features * count * count,
-            transcendentals=HEADS_A_CALL * count * count,
-            bytes_accessed=2 * HEADS_A_CALL * count * count,
+            flops=40 * width * count * count,
+            transcendentals=HEADS * count * count,
+            bytes_accessed=2 * HEADS * count * count,
         ),
         name="attend_far",
-    )(rows, w_key, w_value, bias, grads, *own)
+    )(core_bit, *away(*args))
+
+
+def near(*arrays):
+    return tuple(pltpu.with_memory_space_constraint(a, pltpu.VMEM) for a in arrays)
+
+
+def room(mebibytes):
+    return pltpu.CompilerParams(vmem_limit_bytes=mebibytes << 20)
+
+
+def away(*arrays):
+    return tuple(pltpu.with_memory_space_constraint(a, pltpu.HBM) for a in arrays)
+
+
+NEAR = pl.BlockSpec(memory_space=pltpu.VMEM)
 
 
 class Moves:
@@ -201,21 +321,25 @@
 
 
 def pack_body(gate_ref, up_ref, down_ref, out_ref):
-    width, hidden = gate_ref.shape
+    hidden, width = gate_ref.shape
     lanes = 2 * hidden
-    out_ref[:width] = jnp.concatenate([gate_ref[...], up_ref[...]], axis=1)
     for tile in range(width // lanes):
-        block = down_ref[tile * lanes : (tile + 1) * lanes].astype(jnp.float32)
-        out_ref[width + tile * hidden : width + (tile + 1) * hidden] = block.T.astype(jnp.bfloat16)
+        at = slice(tile * lanes, (tile + 1) * lanes)
+        block = jnp.concatenate([gate_ref[:, at], up_ref[:, at]], axis=0)
+        out_ref[at] = block.T
+        out_ref[width + tile * hidden : width + (tile + 1) * hidden] = down_ref[:, at]
 
 
 def pack_weights(w_gate, w_up, w_down_t):
     width, hidden = w_gate.shape
     return pl.pallas_call(
         pack_body,
-        out_shape=jax.ShapeDtypeStruct((width + width // 2, 2 * hidden), jnp.bfloat16),
+        in_specs=[NEAR] * 3,
+        out_specs=NEAR,
+        out_shape=pltpu.VMEM((width + width // 2, 2 * hidden), jnp.bfloat16),
+        compiler_params=room(4),
         name="pack",
-    )(w_gate, w_up, w_down_t)
+    )(*near(w_gate.T, w_up.T, w_down_t.T))
 
 
 def ffn_body(pieces, count, splits, *refs):
@@ -256,13 +380,105 @@
     units = len(chunks) * chunks[0].shape[1] // 2
     return pl.pallas_call(
         lambda *refs: ffn_body(len(rows), len(chunks), splits, *refs),
-        out_shape=[jax.ShapeDtypeStruct((height // splits, width), dtype)] * splits,
+        in_specs=[NEAR] * (len(rows) + len(chunks) + len(starts or [])),
+        out_specs=[NEAR] * splits,
+        out_shape=[pltpu.VMEM((height // splits, width), dtype)] * splits,
         cost_estimate=pl.CostEstimate(
             flops=6 * height * width * units,
             transcendentals=height * units,
             bytes_accessed=2 * width * (height + 3 * units),
         ),
-    )(*rows, *chunks, *(starts or []))
+        compiler_params=room(24),
+    )(*near(*rows, *chunks, *(starts or [])))
+
+
+def norm_rows(values):
+    return values * lax.rsqrt(jnp.mean(values * values, axis=-1, keepdims=True) + epsilon)
+
+
+def join_body(first_ref, second_ref, out_ref):
+    height = first_ref.shape[0]
+    out_ref[:height] = first_ref[...]
+    out_ref[height:] = second_ref[...]
+
+
+def join(first, second):
+    height, width = first.shape
+    return pl.pallas_call(
+        join_body,
+        in_specs=[NEAR] * 2,
+        out_specs=NEAR,
+        out_shape=pltpu.VMEM((2 * height, width), first.dtype),
+        compiler_params=room(2),
+        name="join",
+    )(*near(first, second))
+
+
+def picked(rows, sources):
+    at = lax.broadcasted_iota(jnp.int32, (sources.shape[0], rows.shape[0]), 1)
+    return mm((at == sources).astype(jnp.bfloat16), rows)
+
+
+def finish_body(count_ref, level_ref, *refs):
+    sums, w_embed_ref = refs[:6], refs[6]
+    slide_ref, back_ref, far_ref, far_send_ref = refs[7:]
+    low = jnp.bfloat16
+    mixed = []
+    for kept, own, end in (sums[:3], sums[3:]):
+        mixed.append(kept[...] + own[...].astype(jnp.float32) + end[...].astype(jnp.float32))
+    encoded = level_ref[...].astype(jnp.float32) + jnp.concatenate(mixed, axis=0)
+    slide = mm(norm_rows(encoded).astype(low), w_embed_ref[...]).astype(low)
+    slide_ref[...] = slide
+    half, blocks = slide.shape[0], back_ref.shape[0] // BLOCK
+    for block in range(blocks):
+        source = (blocks - block) * BLOCK
+        back_ref[block * BLOCK : (block + 1) * BLOCK] = slide[source : source + BLOCK]
+    normed = norm_rows(slide.astype(jnp.float32)).astype(low)
+    place = lax.broadcasted_iota(jnp.int32, (far_ref.shape[0], 1), 0)
+    own_far, sent_far = half // RATE, blocks * BLOCK // RATE
+    far = picked(normed, jnp.where(place < own_far, place * RATE, -1))
+    far_count = ((count_ref[0, 0] + RATE - 1) // RATE).astype(jnp.float32)
+    far_ref[...] = jnp.where(place < own_far + sent_far, far, far_count).astype(low)
+    step = (place - own_far) * RATE
+    source = (blocks - step // BLOCK) * BLOCK + step % BLOCK
+    is_sent = (place >= own_far) & (place < own_far + sent_far)
+    far_send_ref[...] = picked(normed, jnp.where(is_sent, source, -1)).astype(low)
+
+
+def finish(counts, level, sums, w_embed, dilated):
+    half, width = level.shape[0], w_embed.shape[1]
+    low = jnp.bfloat16
+    return pl.pallas_call(
+        finish_body,
+        in_specs=[pl.BlockSpec(memory_space=pltpu.SMEM)] + [NEAR] * 8,
+        out_specs=[NEAR] * 4,
+        out_shape=[
+            pltpu.VMEM((half, width), low),
+            pltpu.VMEM((half - BLOCK, width), low),
+            pltpu.VMEM((dilated, width), low),
+            pltpu.VMEM((dilated, width), low),
+        ],
+        compiler_params=room(12),
+        name="finish",
+    )(counts, *near(level, *sums, w_embed))
+
+
+def tokens_body(part_ref, back_ref, slide_ref, normed_ref):
+    slide = jnp.concatenate([part_ref[...], back_ref[...]], axis=0)
+    slide_ref[...] = slide
+    normed_ref[...] = norm_rows(slide.astype(jnp.float32)).astype(jnp.bfloat16)
+
+
+def tokens(part, back):
+    shape = (part.shape[0] + back.shape[0], part.shape[1])
+    return pl.pallas_call(
+        tokens_body,
+        in_specs=[NEAR] * 2,
+        out_specs=[NEAR] * 2,
+        out_shape=[pltpu.HBM(shape, jnp.bfloat16)] * 2,
+        compiler_params=room(6),
+        name="tokens",
+    )(*near(part, back))
 
 
 def flip_blocks(rows):
@@ -270,7 +486,7 @@
     return rows.reshape(-1, BLOCK, width)[::-1].reshape(-1, width)
 
 
-def encode(moves, tile_rows, row_count, w_gate, w_up, w_down_t, w_embed):
+def encode(moves, counts, tile_rows, row_count, w_gate, w_up, w_down_t, w_embed):
     hidden = w_gate.shape[1]
     packed = 2 * hidden == 128 and moves.ring > 1
     half = tile_rows.shape[0] // 2
@@ -315,23 +531,21 @@
     second_own = moves.x(sent[2])
     first_end = moves.x((kept[1] + first_on.astype(jnp.float32)).astype(low))
     second_end = moves.y((kept[3] + second_on.astype(jnp.float32)).astype(low))
-    first = kept[0] + first_own.astype(jnp.float32) + first_end.astype(jnp.float32)
-    second = kept[2] + second_own.astype(jnp.float32) + second_end.astype(jnp.float32)
-    mixed = jnp.concatenate([first, second], axis=0)
-    embedded = rms_rows(level.astype(jnp.float32) + mixed).astype(low)
-    slide_part = mm(embedded, w_embed).astype(low)
-    normed_part = rms_rows(slide_part).astype(low)
-    far_back = moves.y(flip_blocks(normed_part[BLOCK:])[::RATE])
-    back = moves.y(flip_blocks(slide_part[BLOCK:]))
-    far = jnp.concatenate([normed_part[::RATE], far_back], axis=0)
-    return jnp.concatenate([slide_part, back], axis=0), far
-
-
-def reduce_grads(moves, part_value, part_out):
+    dilated = tile_rows.shape[0] // RATE
+    sums = (kept[0], first_own, first_end, kept[2], second_own, second_end)
+    slide_part, to_back, far_own, far_send = finish(counts, level, sums, w_embed, dilated)
+    far_got = moves.y(far_send)
+    back = moves.y(to_back)
+    place = jnp.arange(dilated)[:, None]
+    is_got = (place >= half // RATE) & (place < (half + spare) // RATE)
+    return tokens(slide_part, back), jnp.where(is_got, far_got, far_own)
+
+
+def reduce_grads(moves, out_kept, out_sent, value_kept, value_sent):
     seqs = moves.seqs
-    features, width = part_value.shape
+    features, width = 2 * out_kept.shape[0], out_kept.shape[1]
     seq_index, group_index = lax.axis_index("seq"), lax.axis_index("group")
-    core_bit, x_bit, rest = seq_index % 2, (seq_index // 2) % 2, seq_index // 4
+    x_bit, rest = (seq_index // 2) % 2, seq_index // 4
     y_bit = group_index % 2
     share = features // seqs // 2
     low = jnp.bfloat16
@@ -340,11 +554,12 @@
         kept = take(array, bit, axis).astype(jnp.float32)
         return kept + move(take(array, 1 - bit, axis).astype(low)).astype(jnp.float32)
 
-    def split(array):
-        return array.reshape(moves.rests, 2, 2, 2, share, width)
-
-    value = halve(split(part_value), core_bit, 2, moves.core)
-    out = halve(split(part_out), core_bit, 2, moves.core)
+    def with_core(kept, sent):
+        total = kept + moves.core(sent).astype(jnp.float32)
+        return total.reshape(moves.rests, 2, 2, share, width)
+
+    out = with_core(out_kept, out_sent)
+    value = with_core(value_kept, value_sent)
     value = halve(value, x_bit, 1, moves.x)
     out = halve(out, y_bit, 2, moves.y)
     value = halve(value, y_bit, 1, moves.y)
@@ -370,7 +585,7 @@
 def gather_far(moves, block):
     bit = moves.seqs // 2
     while bit >= 1:
-        block = jnp.concatenate([block, moves.seq_xor(block, bit)], axis=0)
+        block = join(block, moves.seq_xor(block, bit))
         bit //= 2
     return block
 
@@ -384,46 +599,24 @@
     seq_len = tile_rows.shape[0]
     live = seq_len - BLOCK
     is_valid = jnp.arange(live) < row_count
-    grad_y = jnp.where(is_valid[:, None], cotangent[0, :live], jnp.zeros((), cotangent.dtype))
-    grad_att = mm_nt(w_out, grad_y).astype(jnp.bfloat16)
-
-    slide_tok, own_far = encode(
-        moves, tile_rows, row_count, w_gate, w_up, w_down_t, w_embed
-    )
-    slide_normed = rms_rows(slide_tok).astype(jnp.bfloat16)
-    width = slide_normed.shape[1]
+    grad_y, grad_att = grads_in(tile_counts, cotangent[0], w_out, live)
+    (slide_tok, slide_normed), far_block = encode(
+        moves, tile_counts, tile_rows, row_count, w_gate, w_up, w_down_t, w_embed
+    )
+    width = slide_tok.shape[1]
     dilated = seq_len // RATE
-    held = live // RATE
-    far_count = ((row_count + RATE - 1) // RATE).astype(jnp.bfloat16)
-    far_rows = gather_far(
-        moves,
-        jnp.concatenate(
-            [own_far, jnp.full((dilated - held, width), far_count, jnp.bfloat16)], axis=0
-        ),
-    )
-    far_blocks = far_rows.reshape(moves.seqs, dilated, width)
-    far_valid = (
-        jnp.arange(dilated)[None, :] < far_blocks[:, dilated - 1, :1].astype(jnp.float32)
-    ).reshape(-1)
-    bias_own = jnp.where(is_valid, 0.0, -1e30).astype(jnp.float32)[:, None]
-    bias_far = jnp.where(far_valid, 0.0, -1e30).astype(jnp.float32)[:, None]
-    parts = range(HEADS // HEADS_A_CALL)
+    far_rows = gather_far(moves, far_block)
     own = []
-    for part in parts:
-        own.append(attend_own(part, slide_normed, w_query, w_key, w_value, bias_own))
-    ends = [
-        attend_far(part, far_rows, w_key, w_value, bias_far, grad_att, own[part])
-        for part in parts
-    ]
-    attended, grads_own, grads_far = [
-        jnp.concatenate(pieces, axis=0) for pieces in zip(*ends)
-    ]
+    for part in range(HEADS // HEADS_A_CALL):
+        own.append(attend_own(part, tile_counts, slide_normed, w_query, w_key, w_value))
+    core_bit = (lax.axis_index("seq") % 2).astype(jnp.int32)[None]
+    attended, *parts = attend_far(
+        dilated, core_bit, far_rows, w_key, w_value, grad_att, own, grad_y, slide_normed
+    )
     output = slide_tok.astype(jnp.float32) + mm_tn(attended, w_out)
     slide_out = jnp.where(is_valid[:, None], output, 0.0).astype(jnp.bfloat16)
     slide_out = jnp.concatenate([slide_out, jnp.zeros((BLOCK, width), jnp.bfloat16)], axis=0)
-    part_out = mm(attended, grad_y)
-    part_value = mm_tt(slide_normed, grads_own) + mm_tt(far_rows, grads_far)
-    grad_value, grad_out = reduce_grads(moves, part_value, part_out)
+    grad_value, grad_out = reduce_grads(moves, *parts)
     return (slide_out[None], grad_value, grad_out)
 
 

time: 200 us -> 170 us (0.85)
  local copies, waits for them, and re-layouts: 26.5 us -> 4.47 us
  waiting for transfers between devices: 72 us -> 92.7 us
  Pallas kernels: 51 us -> 40 us
  matrix products: 7.84 us -> 0.62 us
  other arithmetic: 9.81 us -> 3.41 us
  starting transfers between devices: 29.9 us -> 26.5 us
    ppermute x17, waiting for transfers between devices: 18.6 us -> 30.8 us  [seq_xor(): return lax.ppermute(value, 'seq', [(s, s ^ bit) for s in range(self.seqs)])]
    pallas_call x3, Pallas kernels: 18.5 us -> 6.78 us  [ffn_kernel(): pl.pallas_call(lambda *refs: ffn_body(len(rows), len(chunks), splits, *re...]
    ppermute x11, waiting for transfers between devices: 16.3 us -> 25.5 us  [y(): lax.ppermute(value, 'group', [(g, g ^ 1) for g in range(self.groups)])]
    dot_general x5 -> x0, matrix products: 7.22 us -> none  [the longest x1 2.87 us: mm_nt(): lax.dot_general(left, right, (((1,), (1,)), ((), ())), preferred_element_...]
    unnamed x63 -> x26, local copies, waits for them, and re-layouts: 8.81 us -> 1.67 us
    concatenate x4 -> x0, local copies, waits for them, and re-layouts: 5.94 us -> none  [the longest x3 4.93 us: gather_far(): block = jnp.concatenate([block, moves.seq_xor(block, bit)], axis=0)]
    ppermute x3, waiting for transfers between devices: 34.4 us -> 31.3 us  [ring_next(): return lax.ppermute(value, BOTH, pairs)]
    add x6 -> x4, other arithmetic: 3.08 us -> 0.17 us  [halve(): kept + move(take(array, 1 - bit, axis).astype(low)).astype(jnp.float32)]
  transfers between devices with their start and end apart: 34 -> 34, of which waited for: 18 -> 20; matrix products, arithmetic and copies ran while one was open for 12% -> 3% of each run, Pallas kernels for 15% -> 12%
where the time goes in v4:
time: 170 us; the launch traced here: 169 us
  waiting for transfers between devices  92.7 us (55%)
  Pallas kernels  40 us (24%)
  starting transfers between devices  26.5 us (16%)
  local copies, waits for them, and re-layouts  4.47 us (3%)
  other arithmetic  3.41 us (2%)
  between operations  1.76 us (1%)
    ppermute x3, waiting for transfers between devices, ring_next(): return lax.ppermute(value, BOTH, pairs)  31.3 us
    ppermute x17, waiting for transfers between devices, seq_xor(): return lax.ppermute(value, 'seq', [(s, s ^ bit) for s in range(self.seqs)])  30.8 us
    ppermute x11, waiting for transfers between devices, y(): lax.ppermute(value, 'group', [(g, g ^ 1) for g in range(self.groups)])  25.5 us
    pallas_call x1, Pallas kernels, attend_far(): pl.pallas_call(lambda *refs: far_body(dilated, *refs), in_specs=[pl.Block...  16.4 us
    pallas_call x2, Pallas kernels, attend_own(): pl.pallas_call(lambda *refs: own_body(part, *refs), in_specs=[pl.BlockSpe...  13 us
    ppermute x11, starting transfers between devices, y(): lax.ppermute(value, 'group', [(g, g ^ 1) for g in range(self.groups)])  11.5 us
    ppermute x17, starting transfers between devices, seq_xor(): return lax.ppermute(value, 'seq', [(s, s ^ bit) for s in range(self.seqs)])  10.8 us
    pallas_call x3, Pallas kernels, ffn_kernel(): pl.pallas_call(lambda *refs: ffn_body(len(rows), len(chunks), splits, *re...  6.78 us
  transfers between devices with their start and end apart: 34, of which 20 were waited for; matrix products, arithmetic and copies ran while one was open for 3% of the time, Pallas kernels for 12%

profile of v4, /device:TPU:0, one launch (start us, length us, event | category | flops | bytes accessed | tf_op | source)
XLA Modules:
  0.0 169.5 jit_solution(11635620800461458134)
XLA Ops:
  0.7 1.0 slice-done
  1.7 3.1 %collective-permute-start = (bf16[160,1536]{1,0:T(8,128)(2,1)S(1)}, bf16[160,1536]{1,0:T(8,128)(2,1)S(1)}, u32[]{:S(2)}, u32[]{:S(2)}) collective-permute-start(bf16[160,1536]{1,0:T(8,128)(2,1)S(1)} %bitcast.61), channel_id=1, source_target_pairs={{0,16},{16,0},{1,17},{17,1},{2,18},{18,2},{3,19},{19,3},{4,20},{20... | collective-permute-start | bytes 1474568 | tf_op jit(solution)/shard_map/ppermute | solution.py:291
  4.8 0.2 pack.1.refs_4_
  4.9 1.6 collective-permute-start.3
  7.3 8.7 %collective-permute-done = bf16[160,1536]{1,0:T(8,128)(2,1)S(1)} collective-permute-done((bf16[160,1536]{1,0:T(8,128)(2,1)S(1)}, bf16[160,1536]{1,0:T(8,128)(2,1)S(1)}, u32[]{:S(2)}, u32[]{:S(2)}) %collective-permute-start) | collective-permute-done | bytes 491552 | tf_op jit(solution)/shard_map/ppermute | solution.py:291
  16.1 0.2 fusion
  16.3 0.2 fusion.1
  16.5 5.1 %collective-permute-done.3.refs_6_ = bf16[2304,128]{1,0:T(8,128)(2,1)S(1)} collective-permute-done((bf16[2304,128]{1,0:T(8,128)(2,1)S(1)}, bf16[2304,128]{1,0:T(8,128)(2,1)S(1)}, u32[]{:S(2)}, u32[]{:S(2)}) %collective-permute-start.3) | collective-permute-done | bytes 589856 | tf_op jit(solution)/shard_map/ppermute | solution.py:308
  21.7 1.6 collective-permute-start.1
  23.2 0.5 collective-permute-start.2
  23.7 0.2 collective-permute-start.10
  24.0 13.5 %collective-permute-done.4.refs_8_ = bf16[2304,128]{1,0:T(8,128)(2,1)S(1)} collective-permute-done((bf16[2304,128]{1,0:T(8,128)(2,1)S(1)}, bf16[2304,128]{1,0:T(8,128)(2,1)S(1)}, u32[]{:S(2)}, u32[]{:S(2)}) %collective-permute-start.4) | collective-permute-done | bytes 589856 | tf_op jit(solution)/shard_map/ppermute | solution.py:308
  37.5 0.8 collective-permute-start.7
  38.3 1.3 collective-permute-start.8
  39.7 12.7 %collective-permute-done.5.refs_2_ = bf16[2304,128]{1,0:T(8,128)(2,1)S(1)} collective-permute-done((bf16[2304,128]{1,0:T(8,128)(2,1)S(1)}, bf16[2304,128]{1,0:T(8,128)(2,1)S(1)}, u32[]{:S(2)}, u32[]{:S(2)}) %collective-permute-start.5) | collective-permute-done | bytes 589856 | tf_op jit(solution)/shard_map/ppermute | solution.py:308
  52.4 3.8 %shard_map.130 = (f32[96,1536]{1,0:T(8,128)S(1)}, f32[96,1536]{1,0:T(8,128)S(1)}, f32[96,1536]{1,0:T(8,128)S(1)}, f32[96,1536]{1,0:T(8,128)S(1)}, f32[96,1536]{1...) custom-call(bf16[192,1536]{1,0:T(8,128)(2,1)S(1)} %collective-permute-done.7.refs_0_, ...), custom_call_target="tpu_custom_call" | custom-call | flops 2717908992 | bytes 5898240 | tf_op jit(solution)/shard_map/pallas_call | solution.py:381
  56.2 1.5 shard_map.132
  57.7 1.0 collective-permute-start.13
  58.7 1.1 collective-permute-start.12
  59.8 1.5 collective-permute-start.15
  61.3 0.5 collective-permute-start.16
  61.8 1.5 shard_map.131
  63.3 4.3 %collective-permute-done.13 = bf16[96,1536]{1,0:T(8,128)(2,1)S(1)} collective-permute-done((bf16[96,1536]{1,0:T(8,128)(2,1)S(1)}, bf16[96,1536]{1,0:T(8,128)(2,1)S(1)}, u32[]{:S(2)}, u32[]{:S(2)}) %collective-permute-start.13) | collective-permute-done | bytes 294944 | tf_op jit(solution)/shard_map/ppermute | solution.py:291
  67.7 1.6 collective-permute-start.14
  69.3 6.7 %collective-permute-done.16 = bf16[96,1536]{1,0:T(8,128)(2,1)S(1)} collective-permute-done((bf16[96,1536]{1,0:T(8,128)(2,1)S(1)}, bf16[96,1536]{1,0:T(8,128)(2,1)S(1)}, u32[]{:S(2)}, u32[]{:S(2)}) %collective-permute-start.16) | collective-permute-done | bytes 294944 | tf_op jit(solution)/shard_map/ppermute | solution.py:282
  76.1 1.0 collective-permute-start.17
  77.1 4.2 %collective-permute-done.14.refs_2_ = bf16[96,1536]{1,0:T(8,128)(2,1)S(1)} collective-permute-done((bf16[96,1536]{1,0:T(8,128)(2,1)S(1)}, bf16[96,1536]{1,0:T(8,128)(2,1)S(1)}, u32[]{:S(2)}, u32[]{:S(2)}) %collective-permute-start.14) | collective-permute-done | bytes 294944 | tf_op jit(solution)/shard_map/ppermute | solution.py:282
  81.3 1.8 %collective-permute-done.17.refs_5_ = bf16[96,1536]{1,0:T(8,128)(2,1)S(1)} collective-permute-done((bf16[96,1536]{1,0:T(8,128)(2,1)S(1)}, bf16[96,1536]{1,0:T(8,128)(2,1)S(1)}, u32[]{:S(2)}, u32[]{:S(2)}) %collective-permute-start.17) | collective-permute-done | bytes 294944 | tf_op jit(solution)/shard_map/ppermute | solution.py:291
  83.1 1.4 finish.1
  84.5 1.0 collective-permute-start.19
  85.5 3.4 %collective-permute-done.19 = bf16[24,768]{1,0:T(8,128)(2,1)S(1)} collective-permute-done((bf16[24,768]{1,0:T(8,128)(2,1)S(1)}, bf16[24,768]{1,0:T(8,128)(2,1)S(1)}, u32[]{:S(2)}, u32[]{:S(2)}) %collective-permute-start.19) | collective-permute-done | bytes 36896 | tf_op jit(solution)/shard_map/ppermute | solution.py:291
  89.0 1.0 collective-permute-start.18
  90.0 3.8 %collective-permute-done.20.second_ref = bf16[24,768]{1,0:T(8,128)(2,1)S(1)} collective-permute-done((bf16[24,768]{1,0:T(8,128)(2,1)S(1)}, bf16[24,768]{1,0:T(8,128)(2,1)S(1)}, u32[]{:S(2)}, u32[]{:S(2)}) %collective-permute-start.20) | collective-permute-done | bytes 36896 | tf_op jit(solution)/shard_map/ppermute | solution.py:282
  93.9 4.3 %collective-permute-done.21.second_ref = bf16[48,768]{1,0:T(8,128)(2,1)S(1)} collective-permute-done((bf16[48,768]{1,0:T(8,128)(2,1)S(1)}, bf16[48,768]{1,0:T(8,128)(2,1)S(1)}, u32[]{:S(2)}, u32[]{:S(2)}) %collective-permute-start.21) | collective-permute-done | bytes 73760 | tf_op jit(solution)/shard_map/ppermute | solution.py:282
  98.2 1.6 collective-permute-start.22
  99.8 0.8 grads_in.1
  100.7 1.4 tokens.1
  102.0 1.4 collective-permute-done.22.second_ref
  103.6 6.6 %attend_own.2 = (bf16[384,352]{1,0:T(8,128)(2,1)}, bf16[8,352,352]{2,1,0:T(8,128)(2,1)}, f32[8,1,352]{2,1,0:T(1,128)}, f32[8,1,352]{2,1,0:T(1,128)}, f32[384,352]{1,0:T(8,128)}) custom-call(s32[1,1]{1,0:T(1,128)} %copy.21.count_ref.refs_0_, bf16[352,768]{1,0:T(8,128)(2,1)} %get-tuple-element.64.refs_1_.refs_16_, bf16[768,768]{1,0:T(8,128)(2,1)} %refs_2_.4, ...), custom_call_target="tpu_custom_call" | custom-call | flops 1903165440 | bytes 1982464 | tf_op jit(solution)/shard_map/attend_own/pallas_call | solution.py:208
  110.2 6.4 %attend_own.3 = (bf16[384,352]{1,0:T(8,128)(2,1)}, bf16[8,352,352]{2,1,0:T(8,128)(2,1)}, f32[8,1,352]{2,1,0:T(1,128)}, f32[8,1,352]{2,1,0:T(1,128)}, f32[384,352]{1,0:T(8,128)}) custom-call(s32[1,1]{1,0:T(1,128)} %copy.21.count_ref.refs_0_, bf16[352,768]{1,0:T(8,128)(2,1)} %get-tuple-element.64.refs_1_.refs_16_, bf16[768,768]{1,0:T(8,128)(2,1)} %refs_2_.4, ...), custom_call_target="tpu_custom_call" | custom-call | flops 1903165440 | bytes 1982464 | tf_op jit(solution)/shard_map/attend_own/pallas_call | solution.py:208
  116.7 0.8 copy-done.2
  117.5 16.4 %attend_far.1 = (bf16[768,352]{1,0:T(8,128)(2,1)S(1)}, f32[384,768]{1,0:T(8,128)S(1)}, bf16[384,768]{1,0:T(8,128)(2,1)}, f32[384,768]{1,0:T(8,128)S(1)}, bf16[384,768]{1,0:T(8,128)(2,1)}) custom-call(s32[1]{0:T(128)} %bitcast.8.refs_0_, bf16[384,768]{1,0:T(8,128)(2,1)} %copy-done.2, bf16[768,768]{1,0:T(8,128)(2,1)} %refs_2_.5, bf16[768,768]{1,0:T(8,128)(2,1)} %refs_3_.5, ...), custom_call_target="tpu_custom_call" | custom-call | flops 3806330880 | bytes 3964928 | tf_op jit(solution)/shard_map/attend_far/pallas_call | solution.py:237
  133.9 0.8 copy-done.9
  134.7 0.5 collective-permute-start.24
  135.2 1.9 %collective-permute-done.24 = bf16[384,768]{1,0:T(8,128)(2,1)} collective-permute-done((bf16[384,768]{1,0:T(8,128)(2,1)}, bf16[384,768]{1,0:T(8,128)(2,1)}, u32[]{:S(2)}, u32[]{:S(2)}) %collective-permute-start.24) | collective-permute-done | bytes 589856 | tf_op jit(solution)/shard_map/ppermute | solution.py:282
  137.1 1.2 convert_add_fusion.1
  138.4 1.6 collective-permute-start.25
  139.9 1.2 convert_add_fusion
  141.1 0.6 collective-permute-start.28
  141.7 6.0 %collective-permute-done.25 = bf16[4,2,24,768]{3,2,1,0:T(8,128)(2,1)S(1)} collective-permute-done((bf16[4,2,24,768]{3,2,1,0:T(8,128)(2,1)S(1)}, bf16[4,2,24,768]{3,2,1,0:T(8,128)(2,1)S(1)}, u32[]{:S(2)}, u32[]{:S(2)}) %collective-permute-start.25) | collective-permute-done | bytes 294944 | tf_op jit(solution)/shard_map/ppermute | solution.py:282
  147.8 1.0 collective-permute-start.26
  148.8 1.6 collective-permute-done.28
  150.6 0.3 collective-permute-start.29
  150.9 2.5 %collective-permute-done.26 = bf16[4,24,768]{2,1,0:T(8,128)(2,1)S(1)} collective-permute-done((bf16[4,24,768]{2,1,0:T(8,128)(2,1)S(1)}, bf16[4,24,768]{2,1,0:T(8,128)(2,1)S(1)}, u32[]{:S(2)}, u32[]{:S(2)}) %collective-permute-start.26) | collective-permute-done | bytes 147488 | tf_op jit(solution)/shard_map/ppermute | solution.py:291
  153.4 2.3 %collective-permute-done.29 = bf16[4,24,768]{2,1,0:T(8,128)(2,1)S(1)} collective-permute-done((bf16[4,24,768]{2,1,0:T(8,128)(2,1)S(1)}, bf16[4,24,768]{2,1,0:T(8,128)(2,1)S(1)}, u32[]{:S(2)}, u32[]{:S(2)}) %collective-permute-start.29) | collective-permute-done | bytes 147488 | tf_op jit(solution)/shard_map/ppermute | solution.py:282
  155.9 2.0 %collective-permute-start.32 = (bf16[24,1536]{1,0:T(8,128)(2,1)S(1)}, bf16[24,1536]{1,0:T(8,128)(2,1)S(1)}, u32[]{:S(2)}, u32[]{:S(2)}) collective-permute-start(bf16[24,1536]{1,0:T(8,128)(2,1)S(1)} %get-tuple-element.86), channel_id=1, source_target_pairs={{0,12},{1,13},{2,14},{3,15},{4,0},{5,1},{6,2},{7,3},{8,4},{9,5},{1... | collective-permute-start | bytes 221192 | tf_op jit(solution)/shard_map/ppermute | solution.py:298
  157.8 0.6 collective-permute-start.30
  158.5 0.6 select_convert_fusion
  159.1 2.6 %collective-permute-done.32 = bf16[24,1536]{1,0:T(8,128)(2,1)S(1)} collective-permute-done((bf16[24,1536]{1,0:T(8,128)(2,1)S(1)}, bf16[24,1536]{1,0:T(8,128)(2,1)S(1)}, u32[]{:S(2)}, u32[]{:S(2)}) %collective-permute-start.32) | collective-permute-done | bytes 73760 | tf_op jit(solution)/shard_map/ppermute | solution.py:298
  161.7 2.5 %collective-permute-done.31 = bf16[24,1536]{1,0:T(8,128)(2,1)S(1)} collective-permute-done((bf16[24,1536]{1,0:T(8,128)(2,1)S(1)}, bf16[24,1536]{1,0:T(8,128)(2,1)S(1)}, u32[]{:S(2)}, u32[]{:S(2)}) %collective-permute-start.31) | collective-permute-done | bytes 73760 | tf_op jit(solution)/shard_map/ppermute | solution.py:298
  164.3 0.4 collective-permute-start.33
  164.7 0.9 pad_bitcast_fusion
  165.5 3.2 %collective-permute-done.33 = bf16[24,1536]{1,0:T(8,128)(2,1)S(1)} collective-permute-done((bf16[24,1536]{1,0:T(8,128)(2,1)S(1)}, bf16[24,1536]{1,0:T(8,128)(2,1)S(1)}, u32[]{:S(2)}, u32[]{:S(2)}) %collective-permute-start.33) | collective-permute-done | bytes 73760 | tf_op jit(solution)/shard_map/ppermute | solution.py:291
  168.7 0.7 fusion.16
  (80 shorter events, 1.3 us)
Async XLA Ops:
  0.6 1.0 slice-start
  0.6 4.1 %copy-start.4 = (bf16[1536,64]{0,1:T(8,128)(2,1)S(1)}, bf16[1536,64]{0,1:T(8,128)(2,1)}, u32[]{:S(2)}) copy-start(bf16[1536,64]{0,1:T(8,128)(2,1)} %param.13) | copy-start | bytes 589828
  0.7 4.1 %copy-start.5 = (bf16[1536,64]{0,1:T(8,128)(2,1)S(1)}, bf16[1536,64]{0,1:T(8,128)(2,1)}, u32[]{:S(2)}) copy-start(bf16[1536,64]{0,1:T(8,128)(2,1)} %param.14) | copy-start | bytes 589828
  0.7 4.1 %copy-start.6 = (bf16[1536,64]{0,1:T(8,128)(2,1)S(1)}, bf16[1536,64]{0,1:T(8,128)(2,1)}, u32[]{:S(2)}) copy-start(bf16[1536,64]{0,1:T(8,128)(2,1)} %param.15) | copy-start | bytes 589828
  0.7 6.6 %copy-start.11 = (bf16[1,384,1536]{2,1,0:T(8,128)(2,1)S(1)}, bf16[1,384,1536]{2,1,0:T(8,128)(2,1)}, u32[]{:S(2)}) copy-start(bf16[1,384,1536]{2,1,0:T(8,128)(2,1)} %param.11) | copy-start | bytes 3538948
  1.7 14.3 %collective-permute-start = (bf16[160,1536]{1,0:T(8,128)(2,1)S(1)}, bf16[160,1536]{1,0:T(8,128)(2,1)S(1)}, u32[]{:S(2)}, u32[]{:S(2)}) collective-permute-start(bf16[160,1536]{1,0:T(8,128)(2,1)S(1)} %bitcast.61), channel_id=1, source_target_pairs={{0,16},{16,0},{1,17},{17,1},{2,18},{18,2},{3,19},{19,3},{4,20},{20... | collective-permute-start | bytes 1474568 | tf_op jit(solution)/shard_map/ppermute | solution.py:291
  4.9 16.7 %collective-permute-start.3 = (bf16[2304,128]{1,0:T(8,128)(2,1)S(1)}, bf16[2304,128]{1,0:T(8,128)(2,1)S(1)}, u32[]{:S(2)}, u32[]{:S(2)}) collective-permute-start(bf16[2304,128]{1,0:T(8,128)(2,1)S(1)} %pack.1.refs_4_), channel_id=1, source_target_pairs={{0,4},{1,5},{2,6},{3,7},{4,8},{5,9},{6,10},{7,11},{8,12},{9,13},{1... | collective-permute-start | bytes 1769480 | tf_op jit(solution)/shard_map/ppermute | solution.py:308
  21.6 15.8 %collective-permute-start.4 = (bf16[2304,128]{1,0:T(8,128)(2,1)S(1)}, bf16[2304,128]{1,0:T(8,128)(2,1)S(1)}, u32[]{:S(2)}, u32[]{:S(2)}) collective-permute-start(bf16[2304,128]{1,0:T(8,128)(2,1)S(1)} %collective-permute-done.3.refs_6_), channel_id=1, source_target_pairs={{0,4},{1,5},{2,6},{3,7},{4,8},{5,9},{6,10},{7,11},{8,12},{9,13},{1... | collective-permute-start | bytes 1769480 | tf_op jit(solution)/shard_map/ppermute | solution.py:308
  21.7 15.8 %collective-permute-start.1 = (bf16[96,1536]{1,0:T(8,128)(2,1)S(1)}, bf16[96,1536]{1,0:T(8,128)(2,1)S(1)}, u32[]{:S(2)}, u32[]{:S(2)}) collective-permute-start(bf16[96,1536]{1,0:T(8,128)(2,1)S(1)} %get-tuple-element.82), channel_id=1, source_target_pairs={{0,2},{1,3},{2,0},{3,1},{4,6},{5,7},{6,4},{7,5},{8,10},{9,11},{10,... | collective-permute-start | bytes 884744 | tf_op jit(solution)/shard_map/ppermute | solution.py:282
  23.2 16.4 %collective-permute-start.9 = (bf16[2304,128]{1,0:T(8,128)(2,1)S(1)}, bf16[2304,128]{1,0:T(8,128)(2,1)S(1)}, u32[]{:S(2)}, u32[]{:S(2)}) collective-permute-start(bf16[2304,128]{1,0:T(8,128)(2,1)S(1)} %pack.1.refs_4_), channel_id=1, source_target_pairs={{0,1},{1,0},{2,3},{3,2},{4,5},{5,4},{6,7},{7,6},{8,9},{9,8},{10,11... | collective-permute-start | bytes 1769480 | tf_op jit(solution)/shard_map/ppermute | solution.py:282
  23.2 15.0 %collective-permute-start.2 = (bf16[96,1536]{1,0:T(8,128)(2,1)S(1)}, bf16[96,1536]{1,0:T(8,128)(2,1)S(1)}, u32[]{:S(2)}, u32[]{:S(2)}) collective-permute-start(bf16[96,1536]{1,0:T(8,128)(2,1)S(1)} %get-tuple-element.81), channel_id=1, source_target_pairs={{0,16},{16,0},{1,17},{17,1},{2,18},{18,2},{3,19},{19,3},{4,20},{20... | collective-permute-start | bytes 884744 | tf_op jit(solution)/shard_map/ppermute | solution.py:291
  23.7 28.6 %collective-permute-start.10 = (bf16[2304,128]{1,0:T(8,128)(2,1)S(1)}, bf16[2304,128]{1,0:T(8,128)(2,1)S(1)}, u32[]{:S(2)}, u32[]{:S(2)}) collective-permute-start(bf16[2304,128]{1,0:T(8,128)(2,1)S(1)} %collective-permute-done.3.refs_6_), channel_id=1, source_target_pairs={{0,1},{1,0},{2,3},{3,2},{4,5},{5,4},{6,7},{7,6},{8,9},{9,8},{10,11... | collective-permute-start | bytes 1769480 | tf_op jit(solution)/shard_map/ppermute | solution.py:282
  37.4 14.9 %collective-permute-start.5 = (bf16[2304,128]{1,0:T(8,128)(2,1)S(1)}, bf16[2304,128]{1,0:T(8,128)(2,1)S(1)}, u32[]{:S(2)}, u32[]{:S(2)}) collective-permute-start(bf16[2304,128]{1,0:T(8,128)(2,1)S(1)} %collective-permute-done.4.refs_8_), channel_id=1, source_target_pairs={{0,4},{1,5},{2,6},{3,7},{4,8},{5,9},{6,10},{7,11},{8,12},{9,13},{1... | collective-permute-start | bytes 1769480 | tf_op jit(solution)/shard_map/ppermute | solution.py:308
  37.5 14.9 %collective-permute-start.7 = (bf16[192,1536]{1,0:T(8,128)(2,1)S(1)}, bf16[192,1536]{1,0:T(8,128)(2,1)S(1)}, u32[]{:S(2)}, u32[]{:S(2)}) collective-permute-start(bf16[192,1536]{1,0:T(8,128)(2,1)S(1)} %pad_maximum_fusion.2.refs_2_.refs_0_), channel_id=1, source_target_pairs={{0,16},{16,0},{1,17},{17,1},{2,18},{18,2},{3,19},{19,3},{4,20},{20... | collective-permute-start | bytes 1769480 | tf_op jit(solution)/shard_map/ppermute | solution.py:291
  38.3 14.1 %collective-permute-start.8 = (bf16[192,1536]{1,0:T(8,128)(2,1)S(1)}, bf16[192,1536]{1,0:T(8,128)(2,1)S(1)}, u32[]{:S(2)}, u32[]{:S(2)}) collective-permute-start(bf16[192,1536]{1,0:T(8,128)(2,1)S(1)} %pad_maximum_fusion.3.refs_3_.refs_1_), channel_id=1, source_target_pairs={{0,2},{1,3},{2,0},{3,1},{4,6},{5,7},{6,4},{7,5},{8,10},{9,11},{10,... | collective-permute-start | bytes 1769480 | tf_op jit(solution)/shard_map/ppermute | solution.py:282
  39.7 12.7 %collective-permute-start.11 = (bf16[2304,128]{1,0:T(8,128)(2,1)S(1)}, bf16[2304,128]{1,0:T(8,128)(2,1)S(1)}, u32[]{:S(2)}, u32[]{:S(2)}) collective-permute-start(bf16[2304,128]{1,0:T(8,128)(2,1)S(1)} %collective-permute-done.4.refs_8_), channel_id=1, source_target_pairs={{0,1},{1,0},{2,3},{3,2},{4,5},{5,4},{6,7},{7,6},{8,9},{9,8},{10,11... | collective-permute-start | bytes 1769480 | tf_op jit(solution)/shard_map/ppermute | solution.py:282
  52.4 3.9 %collective-permute-start.6 = (bf16[2304,128]{1,0:T(8,128)(2,1)S(1)}, bf16[2304,128]{1,0:T(8,128)(2,1)S(1)}, u32[]{:S(2)}, u32[]{:S(2)}) collective-permute-start(bf16[2304,128]{1,0:T(8,128)(2,1)S(1)} %collective-permute-done.5.refs_2_), channel_id=1, source_target_pairs={{0,1},{1,0},{2,3},{3,2},{4,5},{5,4},{6,7},{7,6},{8,9},{9,8},{10,11... | collective-permute-start | bytes 1769480 | tf_op jit(solution)/shard_map/ppermute | solution.py:282
  57.7 9.9 %collective-permute-start.13 = (bf16[96,1536]{1,0:T(8,128)(2,1)S(1)}, bf16[96,1536]{1,0:T(8,128)(2,1)S(1)}, u32[]{:S(2)}, u32[]{:S(2)}) collective-permute-start(bf16[96,1536]{1,0:T(8,128)(2,1)S(1)} %get-tuple-element.53), channel_id=1, source_target_pairs={{0,16},{16,0},{1,17},{17,1},{2,18},{18,2},{3,19},{19,3},{4,20},{20... | collective-permute-start | bytes 884744 | tf_op jit(solution)/shard_map/ppermute | solution.py:291
  58.7 18.4 %collective-permute-start.12 = (bf16[96,1536]{1,0:T(8,128)(2,1)S(1)}, bf16[96,1536]{1,0:T(8,128)(2,1)S(1)}, u32[]{:S(2)}, u32[]{:S(2)}) collective-permute-start(bf16[96,1536]{1,0:T(8,128)(2,1)S(1)} %get-tuple-element.51), channel_id=1, source_target_pairs={{0,16},{16,0},{1,17},{17,1},{2,18},{18,2},{3,19},{19,3},{4,20},{20... | collective-permute-start | bytes 884744 | tf_op jit(solution)/shard_map/ppermute | solution.py:291
  59.8 17.3 %collective-permute-start.15 = (bf16[96,1536]{1,0:T(8,128)(2,1)S(1)}, bf16[96,1536]{1,0:T(8,128)(2,1)S(1)}, u32[]{:S(2)}, u32[]{:S(2)}) collective-permute-start(bf16[96,1536]{1,0:T(8,128)(2,1)S(1)} %get-tuple-element.55), channel_id=1, source_target_pairs={{0,2},{1,3},{2,0},{3,1},{4,6},{5,7},{6,4},{7,5},{8,10},{9,11},{10,... | collective-permute-start | bytes 884744 | tf_op jit(solution)/shard_map/ppermute | solution.py:282
  61.3 14.7 %collective-permute-start.16 = (bf16[96,1536]{1,0:T(8,128)(2,1)S(1)}, bf16[96,1536]{1,0:T(8,128)(2,1)S(1)}, u32[]{:S(2)}, u32[]{:S(2)}) collective-permute-start(bf16[96,1536]{1,0:T(8,128)(2,1)S(1)} %get-tuple-element.57), channel_id=1, source_target_pairs={{0,2},{1,3},{2,0},{3,1},{4,6},{5,7},{6,4},{7,5},{8,10},{9,11},{10,... | collective-permute-start | bytes 884744 | tf_op jit(solution)/shard_map/ppermute | solution.py:282
  67.7 13.6 %collective-permute-start.14 = (bf16[96,1536]{1,0:T(8,128)(2,1)S(1)}, bf16[96,1536]{1,0:T(8,128)(2,1)S(1)}, u32[]{:S(2)}, u32[]{:S(2)}) collective-permute-start(bf16[96,1536]{1,0:T(8,128)(2,1)S(1)} %add_convert_fusion.1), channel_id=1, source_target_pairs={{0,2},{1,3},{2,0},{3,1},{4,6},{5,7},{6,4},{7,5},{8,10},{9,11},{10,... | collective-permute-start | bytes 884744 | tf_op jit(solution)/shard_map/ppermute | solution.py:282
  76.0 7.1 %copy-start = (bf16[1536,768]{1,0:T(8,128)(2,1)S(1)}, bf16[1536,768]{1,0:T(8,128)(2,1)}, u32[]{:S(2)}) copy-start(bf16[1536,768]{1,0:T(8,128)(2,1)} %refs_6_.1) | copy-start | bytes 7077892
  76.1 7.0 %collective-permute-start.17 = (bf16[96,1536]{1,0:T(8,128)(2,1)S(1)}, bf16[96,1536]{1,0:T(8,128)(2,1)S(1)}, u32[]{:S(2)}, u32[]{:S(2)}) collective-permute-start(bf16[96,1536]{1,0:T(8,128)(2,1)S(1)} %add_convert_fusion), channel_id=1, source_target_pairs={{0,16},{16,0},{1,17},{17,1},{2,18},{18,2},{3,19},{19,3},{4,20},{20... | collective-permute-start | bytes 884744 | tf_op jit(solution)/shard_map/ppermute | solution.py:291
  83.1 16.7 %copy-start.1 = (bf16[768,768]{1,0:T(8,128)(2,1)S(1)}, bf16[768,768]{1,0:T(8,128)(2,1)}, u32[]{:S(2)}) copy-start(bf16[768,768]{1,0:T(8,128)(2,1)} %w_out_ref.1) | copy-start | bytes 3538948
  83.1 16.7 %copy-start.3 = (bf16[1,384,768]{2,1,0:T(8,128)(2,1)S(1)}, bf16[1,384,768]{2,1,0:T(8,128)(2,1)}, u32[]{:S(2)}) copy-start(bf16[1,384,768]{2,1,0:T(8,128)(2,1)} %param.21) | copy-start | bytes 1769476
  84.5 4.4 %collective-permute-start.19 = (bf16[24,768]{1,0:T(8,128)(2,1)S(1)}, bf16[24,768]{1,0:T(8,128)(2,1)S(1)}, u32[]{:S(2)}, u32[]{:S(2)}) collective-permute-start(bf16[24,768]{1,0:T(8,128)(2,1)S(1)} %get-tuple-element.61), channel_id=1, source_target_pairs={{0,16},{16,0},{1,17},{17,1},{2,18},{18,2},{3,19},{19,3},{4,20},{20... | collective-permute-start | bytes 110600 | tf_op jit(solution)/shard_map/ppermute | solution.py:291
  89.0 4.9 %collective-permute-start.20 = (bf16[24,768]{1,0:T(8,128)(2,1)S(1)}, bf16[24,768]{1,0:T(8,128)(2,1)S(1)}, u32[]{:S(2)}, u32[]{:S(2)}) collective-permute-start(bf16[24,768]{1,0:T(8,128)(2,1)S(1)} %broadcast_select_fusion.2.first_ref), channel_id=1, source_target_pairs={{0,8},{1,9},{2,10},{3,11},{4,12},{5,13},{6,14},{7,15},{8,0},{9,1},... | collective-permute-start | bytes 110600 | tf_op jit(solution)/shard_map/ppermute | solution.py:282
  89.0 11.6 %collective-permute-start.18 = (bf16[160,768]{1,0:T(8,128)(2,1)S(1)}, bf16[160,768]{1,0:T(8,128)(2,1)S(1)}, u32[]{:S(2)}, u32[]{:S(2)}) collective-permute-start(bf16[160,768]{1,0:T(8,128)(2,1)S(1)} %get-tuple-element.59), channel_id=1, source_target_pairs={{0,16},{16,0},{1,17},{17,1},{2,18},{18,2},{3,19},{19,3},{4,20},{20... | collective-permute-start | bytes 737288 | tf_op jit(solution)/shard_map/ppermute | solution.py:291
  93.9 4.4 %collective-permute-start.21 = (bf16[48,768]{1,0:T(8,128)(2,1)S(1)}, bf16[48,768]{1,0:T(8,128)(2,1)S(1)}, u32[]{:S(2)}, u32[]{:S(2)}) collective-permute-start(bf16[48,768]{1,0:T(8,128)(2,1)S(1)} %join.4.first_ref), channel_id=1, source_target_pairs={{0,4},{1,5},{2,6},{3,7},{4,0},{5,1},{6,2},{7,3},{8,12},{9,13},{10,... | collective-permute-start | bytes 221192 | tf_op jit(solution)/shard_map/ppermute | solution.py:282
  98.2 5.2 %collective-permute-start.22 = (bf16[96,768]{1,0:T(8,128)(2,1)S(1)}, bf16[96,768]{1,0:T(8,128)(2,1)S(1)}, u32[]{:S(2)}, u32[]{:S(2)}) collective-permute-start(bf16[96,768]{1,0:T(8,128)(2,1)S(1)} %join.5.first_ref), channel_id=1, source_target_pairs={{0,2},{1,3},{2,0},{3,1},{4,6},{5,7},{6,4},{7,5},{8,10},{9,11},{10,... | collective-permute-start | bytes 442376 | tf_op jit(solution)/shard_map/ppermute | solution.py:282
  100.6 2.9 %copy-start.7 = (bf16[768,352]{1,0:T(8,128)(2,1)}, bf16[768,352]{1,0:T(8,128)(2,1)S(1)}, u32[]{:S(2)}) copy-start(bf16[768,352]{1,0:T(8,128)(2,1)S(1)} %get-tuple-element.63.refs_4_) | copy-start | bytes 1622020
  100.6 2.9 %copy-start.8 = (bf16[352,768]{1,0:T(8,128)(2,1)}, bf16[352,768]{1,0:T(8,128)(2,1)S(1)}, u32[]{:S(2)}) copy-start(bf16[352,768]{1,0:T(8,128)(2,1)S(1)} %get-tuple-element.75.refs_15_) | copy-start | bytes 1622020
  103.5 13.1 %collective-permute-start.23 = (bf16[192,768]{1,0:T(8,128)(2,1)S(1)}, bf16[192,768]{1,0:T(8,128)(2,1)S(1)}, u32[]{:S(2)}, u32[]{:S(2)}) collective-permute-start(bf16[192,768]{1,0:T(8,128)(2,1)S(1)} %join.6.first_ref), channel_id=1, source_target_pairs={{0,1},{1,0},{2,3},{3,2},{4,5},{5,4},{6,7},{7,6},{8,9},{9,8},{10,11... | collective-permute-start | bytes 884744 | tf_op jit(solution)/shard_map/ppermute | solution.py:282
  116.6 0.8 copy-start.2
  133.9 0.8 copy-start.9
  134.7 2.5 %collective-permute-start.24 = (bf16[384,768]{1,0:T(8,128)(2,1)}, bf16[384,768]{1,0:T(8,128)(2,1)}, u32[]{:S(2)}, u32[]{:S(2)}) collective-permute-start(bf16[384,768]{1,0:T(8,128)(2,1)} %get-tuple-element.78), channel_id=1, source_target_pairs={{0,1},{1,0},{2,3},{3,2},{4,5},{5,4},{6,7},{7,6},{8,9},{9,8},{10,11... | collective-permute-start | bytes 1769480 | tf_op jit(solution)/shard_map/ppermute | solution.py:282
  135.2 4.8 %collective-permute-start.27 = (bf16[384,768]{1,0:T(8,128)(2,1)}, bf16[384,768]{1,0:T(8,128)(2,1)}, u32[]{:S(2)}, u32[]{:S(2)}) collective-permute-start(bf16[384,768]{1,0:T(8,128)(2,1)} %get-tuple-element.80), channel_id=1, source_target_pairs={{0,1},{1,0},{2,3},{3,2},{4,5},{5,4},{6,7},{7,6},{8,9},{9,8},{10,11... | collective-permute-start | bytes 1769480 | tf_op jit(solution)/shard_map/ppermute | solution.py:282
  138.4 9.4 %collective-permute-start.25 = (bf16[4,2,24,768]{3,2,1,0:T(8,128)(2,1)S(1)}, bf16[4,2,24,768]{3,2,1,0:T(8,128)(2,1)S(1)}, u32[]{:S(2)}, u32[]{:S(2)}) collective-permute-start(bf16[4,2,24,768]{3,2,1,0:T(8,128)(2,1)S(1)} %fusion.3), channel_id=1, source_target_pairs={{0,2},{1,3},{2,0},{3,1},{4,6},{5,7},{6,4},{7,5},{8,10},{9,11},{10,... | collective-permute-start | bytes 884744 | tf_op jit(solution)/shard_map/ppermute | solution.py:282
  141.1 9.3 %collective-permute-start.28 = (bf16[4,2,24,768]{3,2,0,1:T(8,128)(2,1)S(1)}, bf16[4,2,24,768]{3,2,0,1:T(8,128)(2,1)S(1)}, u32[]{:S(2)}, u32[]{:S(2)}) collective-permute-start(bf16[4,2,24,768]{3,2,0,1:T(8,128)(2,1)S(1)} %fusion.4), channel_id=1, source_target_pairs={{0,16},{16,0},{1,17},{17,1},{2,18},{18,2},{3,19},{19,3},{4,20},{20... | collective-permute-start | bytes 884744 | tf_op jit(solution)/shard_map/ppermute | solution.py:291
  147.8 5.6 %collective-permute-start.26 = (bf16[4,24,768]{2,1,0:T(8,128)(2,1)S(1)}, bf16[4,24,768]{2,1,0:T(8,128)(2,1)S(1)}, u32[]{:S(2)}, u32[]{:S(2)}) collective-permute-start(bf16[4,24,768]{2,1,0:T(8,128)(2,1)S(1)} %fusion.5), channel_id=1, source_target_pairs={{0,16},{16,0},{1,17},{17,1},{2,18},{18,2},{3,19},{19,3},{4,20},{20... | collective-permute-start | bytes 442376 | tf_op jit(solution)/shard_map/ppermute | solution.py:291
  150.6 5.2 %collective-permute-start.29 = (bf16[4,24,768]{2,1,0:T(8,128)(2,1)S(1)}, bf16[4,24,768]{2,1,0:T(8,128)(2,1)S(1)}, u32[]{:S(2)}, u32[]{:S(2)}) collective-permute-start(bf16[4,24,768]{2,1,0:T(8,128)(2,1)S(1)} %fusion.6), channel_id=1, source_target_pairs={{0,2},{1,3},{2,0},{3,1},{4,6},{5,7},{6,4},{7,5},{8,10},{9,11},{10,... | collective-permute-start | bytes 442376 | tf_op jit(solution)/shard_map/ppermute | solution.py:282
  153.4 5.1 %copy-start.10 = (bf16[768,352]{1,0:T(8,128)(2,1)S(1)}, bf16[768,352]{1,0:T(8,128)(2,1)}, u32[]{:S(2)}) copy-start(bf16[768,352]{1,0:T(8,128)(2,1)} %copy-done.9) | copy-start | bytes 1622020
  153.4 5.1 %copy-start.12 = (bf16[352,768]{1,0:T(8,128)(2,1)S(1)}, bf16[352,768]{1,0:T(8,128)(2,1)}, u32[]{:S(2)}) copy-start(bf16[352,768]{1,0:T(8,128)(2,1)} %get-tuple-element.60) | copy-start | bytes 1622020
  155.9 5.9 %collective-permute-start.32 = (bf16[24,1536]{1,0:T(8,128)(2,1)S(1)}, bf16[24,1536]{1,0:T(8,128)(2,1)S(1)}, u32[]{:S(2)}, u32[]{:S(2)}) collective-permute-start(bf16[24,1536]{1,0:T(8,128)(2,1)S(1)} %get-tuple-element.86), channel_id=1, source_target_pairs={{0,12},{1,13},{2,14},{3,15},{4,0},{5,1},{6,2},{7,3},{8,4},{9,5},{1... | collective-permute-start | bytes 221192 | tf_op jit(solution)/shard_map/ppermute | solution.py:298
  157.8 6.4 %collective-permute-start.31 = (bf16[24,1536]{1,0:T(8,128)(2,1)S(1)}, bf16[24,1536]{1,0:T(8,128)(2,1)S(1)}, u32[]{:S(2)}, u32[]{:S(2)}) collective-permute-start(bf16[24,1536]{1,0:T(8,128)(2,1)S(1)} %get-tuple-element.87), channel_id=1, source_target_pairs={{0,8},{1,9},{2,10},{3,11},{4,12},{5,13},{6,14},{7,15},{8,0},{9,1},... | collective-permute-start | bytes 221192 | tf_op jit(solution)/shard_map/ppermute | solution.py:298
  157.8 6.4 %collective-permute-start.30 = (bf16[24,1536]{1,0:T(8,128)(2,1)S(1)}, bf16[24,1536]{1,0:T(8,128)(2,1)S(1)}, u32[]{:S(2)}, u32[]{:S(2)}) collective-permute-start(bf16[24,1536]{1,0:T(8,128)(2,1)S(1)} %get-tuple-element.85), channel_id=1, source_target_pairs={{0,4},{1,5},{2,6},{3,7},{4,8},{5,9},{6,10},{7,11},{8,12},{9,13},{1... | collective-permute-start | bytes 221192 | tf_op jit(solution)/shard_map/ppermute | solution.py:298
  164.3 4.4 %collective-permute-start.33 = (bf16[24,1536]{1,0:T(8,128)(2,1)S(1)}, bf16[24,1536]{1,0:T(8,128)(2,1)S(1)}, u32[]{:S(2)}, u32[]{:S(2)}) collective-permute-start(bf16[24,1536]{1,0:T(8,128)(2,1)S(1)} %fusion.12), channel_id=1, source_target_pairs={{0,16},{16,0},{1,17},{17,1},{2,18},{18,2},{3,19},{19,3},{4,20},{20... | collective-permute-start | bytes 221192 | tf_op jit(solution)/shard_map/ppermute | solution.py:291

commit v5 on v4

--- a/solution.py
+++ b/solution.py
@@ -38,14 +38,8 @@
     )
 
 
-def mm_tt(left, right):
-    return lax.dot_general(
-        left, right, (((0,), (1,)), ((), ())), preferred_element_type=jnp.float32
-    )
-
-
-def project_t(weight, rows):
-    return mm_tt(weight, rows).astype(jnp.bfloat16)
+def project_t(weight_t, rows):
+    return mm_nt(weight_t, rows).astype(jnp.bfloat16)
 
 
 HEADS_A_CALL = 8
@@ -90,13 +84,41 @@
     return copies
 
 
+def turn_body(count, *refs):
+    ins, outs = refs[:count], refs[count : 2 * count]
+    held, turned, sems = refs[2 * count : 3 * count], refs[3 * count : 4 * count], refs[-1]
+    got = fetch(ins, held, sems)
+    sent = []
+    for i in range(count):
+        got[i].wait()
+        turned[i][...] = held[i][...].T
+        sent += fetch([turned[i]], [outs[i]], sems, count + i)
+    for copy in sent:
+        copy.wait()
+
+
+def turn(*weights):
+    flat = [(w.shape[1], w.shape[0]) for w in weights]
+    return pl.pallas_call(
+        lambda *refs: turn_body(len(weights), *refs),
+        in_specs=[FAR_AWAY] * len(weights),
+        out_specs=[FAR_AWAY] * len(weights),
+        out_shape=[pltpu.HBM(shape, jnp.bfloat16) for shape in flat],
+        scratch_shapes=[pltpu.VMEM(w.shape, jnp.bfloat16) for w in weights]
+        + [pltpu.VMEM(shape, jnp.bfloat16) for shape in flat]
+        + [pltpu.SemaphoreType.DMA((2 * len(weights),))],
+        compiler_params=room(16),
+        name="turn",
+    )(*away(*weights))
+
+
 def own_body(
     part, count_ref, rows_in, wq_in, wk_in, wv_in, q_out, e_out, m_out, l_out, o_out,
     rows_ref, wq_ref, wk_ref, wv_ref, q_ref, e_ref, m_ref, l_ref, o_ref, sems,
 ):
     cut = pl.ds(part * HEADS_A_CALL * HEAD, HEADS_A_CALL * HEAD)
     got = fetch(
-        (rows_in, wq_in.at[:, cut], wk_in.at[:, cut], wv_in.at[:, cut]),
+        (rows_in, wq_in.at[cut], wk_in.at[cut], wv_in.at[cut]),
         (rows_ref, wq_ref, wk_ref, wv_ref),
         sems,
     )
@@ -104,7 +126,8 @@
     rows = rows_ref[...]
     bias = jnp.where(valid_column(count_ref, rows.shape[0]), 0.0, -1e30)
     got[1].wait()
-    q_ref[...] = project_t(wq_ref[...], rows)
+    scale = 1.0 / (math.sqrt(HEAD) * math.log(2.0))
+    q_ref[...] = (mm_nt(wq_ref[...], rows) * scale).astype(jnp.bfloat16)
     got[2].wait()
     keys = project_t(wk_ref[...], rows)
     got[3].wait()
@@ -112,9 +135,9 @@
     sent = fetch([q_ref], [q_out], sems, 4)
     for h in range(HEADS_A_CALL):
         at = slice(h * HEAD, (h + 1) * HEAD)
-        scores = mm_tn(keys[at], q_ref[at]) * (1.0 / math.sqrt(HEAD)) + bias
+        scores = mm_tn(keys[at], q_ref[at]) + bias
         top = jnp.max(scores, axis=0, keepdims=True)
-        exponent = jnp.exp(scores - top)
+        exponent = jnp.exp2(scores - top)
         m_ref[h] = top
         l_ref[h] = jnp.sum(exponent, axis=0, keepdims=True)
         low = exponent.astype(jnp.bfloat16)
@@ -131,7 +154,7 @@
     count = 6 + 5 * parts
     core_ref, ins, outs = refs[0], refs[1 : 1 + count], refs[1 + count : 6 + count]
     held, sems = refs[6 + count : 6 + 2 * count], refs[-1]
-    keys_ref, values_ref, own_ref, far_ref, sum_ref = refs[-6:-1]
+    keys_ref, values_ref, own_ref, far_ref, turned_ref, turned_far_ref = refs[-7:-1]
     got = fetch(ins, held, sems)
     rows_ref, wk_ref, wv_ref, g_ref = held[:4]
     grad_y_ref, normed_ref = held[-2:]
@@ -160,10 +183,10 @@
                 h = i * HEADS_A_STEP + k
                 here = pl.ds(pl.multiple_of(h * HEAD, HEAD), HEAD)
                 at = pl.ds(pl.multiple_of(first + h * HEAD, HEAD), HEAD)
-                scores = mm_tn(keys_ref[at], q_ref[here]) * (1.0 / math.sqrt(HEAD)) + bias
+                scores = mm_tn(keys_ref[at], q_ref[here]) + bias
                 top = jnp.maximum(jnp.max(scores, axis=0, keepdims=True), m_ref[h])
-                ratio = jnp.exp(m_ref[h] - top)
-                exponent = jnp.exp(scores - top)
+                ratio = jnp.exp2(m_ref[h] - top)
+                exponent = jnp.exp2(scores - top)
                 norm = 1.0 / (l_ref[h] * ratio + jnp.sum(exponent, axis=0, keepdims=True))
                 low = exponent.astype(jnp.bfloat16)
                 total = (o_ref[here] * ratio + mm(values_ref[at], low)) * norm
@@ -176,22 +199,26 @@
 
         lax.fori_loop(0, HEADS_A_CALL // HEADS_A_STEP, step, 0)
 
-    def share_out(total, kept_ref, sent_ref):
-        sum_ref[...] = total
-        share = rows.shape[0] // dilated
-        share = sum_ref.shape[0] // share
-        for ref, bit in ((kept_ref, core_ref[0]), (sent_ref, 1 - core_ref[0])):
+    share = turned_ref.shape[0] * dilated // rows.shape[0]
+
+    def halves(ref):
+        for bit in (core_ref[0], 1 - core_ref[0]):
             pieces = []
-            for first in range(0, sum_ref.shape[0], 2 * share):
-                start = pl.multiple_of(first + bit * share, 8)
-                pieces.append(sum_ref[pl.ds(start, share)])
-            ref[...] = jnp.concatenate(pieces, axis=0).astype(ref.dtype)
+            for first in range(0, ref.shape[0], 2 * share):
+                start = pl.multiple_of(first + bit * share, share)
+                pieces.append(ref[pl.ds(start, share)])
+            yield jnp.concatenate(pieces, axis=0)
 
     got[-2].wait()
-    share_out(mm(att_ref[...], grad_y_ref[...]), outs[1], outs[2])
     got[-1].wait()
-    total = mm_tt(normed_ref[...], own_ref[...]) + mm_tt(rows, far_ref[...])
-    share_out(total, outs[3], outs[4])
+    for half, out in zip(halves(att_ref), outs[1:3]):
+        out[...] = mm(half, grad_y_ref[...]).astype(out.dtype)
+    own_count = normed_ref.shape[0]
+    turned_ref[:, :own_count] = normed_ref[...].T
+    turned_far_ref[...] = rows.T
+    for half, far, out in zip(halves(turned_ref), halves(turned_far_ref), outs[3:5]):
+        total = mm_nt(half[:, :own_count], own_ref[...]) + mm_nt(far, far_ref[...])
+        out[...] = total.astype(out.dtype)
 
 
 def attend_own(part, counts, rows, w_query, w_key, w_value):
@@ -204,7 +231,7 @@
         pltpu.HBM((HEADS_A_CALL, 1, count), jnp.float32),
         pltpu.HBM((features, count), jnp.float32),
     ]
-    cut = pltpu.VMEM((rows.shape[1], features), jnp.bfloat16)
+    cut = pltpu.VMEM((features, rows.shape[1]), jnp.bfloat16)
     return pl.pallas_call(
         lambda *refs: own_body(part, *refs),
         in_specs=[pl.BlockSpec(memory_space=pltpu.SMEM)] + [FAR_AWAY] * 4,
@@ -244,7 +271,8 @@
         + [
             pltpu.VMEM((width, count), low),
             pltpu.VMEM((width, rows.shape[0]), low),
-            pltpu.VMEM((width, width), jnp.float32),
+            pltpu.VMEM((width, count), low),
+            pltpu.VMEM((width, rows.shape[0]), low),
         ]
         + [pltpu.SemaphoreType.DMA((len(args),))],
         compiler_params=room(40),
@@ -320,7 +348,10 @@
     return mm(active, down)
 
 
-def pack_body(gate_ref, up_ref, down_ref, out_ref):
+def pack_body(gate_in, up_in, down_in, out_ref, gate_ref, up_ref, down_ref, sems):
+    got = fetch((gate_in, up_in, down_in), (gate_ref, up_ref, down_ref), sems)
+    for copy in got:
+        copy.wait()
     hidden, width = gate_ref.shape
     lanes = 2 * hidden
     for tile in range(width // lanes):
@@ -334,12 +365,14 @@
     width, hidden = w_gate.shape
     return pl.pallas_call(
         pack_body,
-        in_specs=[NEAR] * 3,
+        in_specs=[FAR_AWAY] * 3,
         out_specs=NEAR,
         out_shape=pltpu.VMEM((width + width // 2, 2 * hidden), jnp.bfloat16),
+        scratch_shapes=[pltpu.VMEM((hidden, width), jnp.bfloat16)] * 3
+        + [pltpu.SemaphoreType.DMA((3,))],
         compiler_params=room(4),
         name="pack",
-    )(*near(w_gate.T, w_up.T, w_down_t.T))
+    )(*away(w_gate.T, w_up.T, w_down_t.T))
 
 
 def ffn_body(pieces, count, splits, *refs):
@@ -503,7 +536,7 @@
     chunks = []
     for c in ringed:
         chunks.append([c, moves.core(c)])
-    extra = moves.y(flip_blocks(tile_rows[half : half + spare]))
+    extra = flip_blocks(moves.y(tile_rows[half : half + spare]))
     own_blocks = (row_count + BLOCK - 1) // BLOCK
     kept = (1 + jnp.arange(spare) // BLOCK) < own_blocks
     level = jnp.concatenate(
@@ -606,12 +639,13 @@
     width = slide_tok.shape[1]
     dilated = seq_len // RATE
     far_rows = gather_far(moves, far_block)
+    wq_t, wk_t, wv_t = turn(w_query, w_key, w_value)
     own = []
     for part in range(HEADS // HEADS_A_CALL):
-        own.append(attend_own(part, tile_counts, slide_normed, w_query, w_key, w_value))
+        own.append(attend_own(part, tile_counts, slide_normed, wq_t, wk_t, wv_t))
     core_bit = (lax.axis_index("seq") % 2).astype(jnp.int32)[None]
     attended, *parts = attend_far(
-        dilated, core_bit, far_rows, w_key, w_value, grad_att, own, grad_y, slide_normed
+        dilated, core_bit, far_rows, wk_t, wv_t, grad_att, own, grad_y, slide_normed
     )
     output = slide_tok.astype(jnp.float32) + mm_tn(attended, w_out)
     slide_out = jnp.where(is_valid[:, None], output, 0.0).astype(jnp.bfloat16)

time: 170 us -> 172 us (1.012)
  waiting for transfers between devices: 92.7 us -> 89.5 us
  Pallas kernels: 40 us -> 42.7 us
  local copies, waits for them, and re-layouts: 4.47 us -> 6.31 us
    pallas_call x1 -> x2, Pallas kernels: 0.15 us -> 4.82 us  [the longest x1 3.49 us: turn(): pl.pallas_call(lambda *refs: turn_body(len(weights), *refs), in_specs=[FA...]
    ppermute x11, waiting for transfers between devices: 25.5 us -> 22.6 us  [y(): lax.ppermute(value, 'group', [(g, g ^ 1) for g in range(self.groups)])]
    ppermute x17, waiting for transfers between devices: 30.8 us -> 28.9 us  [seq_xor(): return lax.ppermute(value, 'seq', [(s, s ^ bit) for s in range(self.seqs)])]
  transfers between devices with their start and end apart: 34 -> 34, of which waited for: 20 -> 19; matrix products, arithmetic and copies ran while one was open for 3% -> 3% of each run, Pallas kernels for 12% -> 14%
where the time goes in v5:
time: 172 us
  waiting for transfers between devices  89.5 us (52%)
  Pallas kernels  42.7 us (25%)
  starting transfers between devices  27.2 us (16%)
  local copies, waits for them, and re-layouts  6.31 us (4%)
  other arithmetic  3.45 us (2%)
    ppermute x3, waiting for transfers between devices, ring_next(): return lax.ppermute(value, BOTH, pairs)  32.4 us
    ppermute x17, waiting for transfers between devices, seq_xor(): return lax.ppermute(value, 'seq', [(s, s ^ bit) for s in range(self.seqs)])  28.9 us
    ppermute x11, waiting for transfers between devices, y(): lax.ppermute(value, 'group', [(g, g ^ 1) for g in range(self.groups)])  22.6 us
    pallas_call x1, Pallas kernels, attend_far(): pl.pallas_call(lambda *refs: far_body(dilated, *refs), in_specs=[pl.Block...  15 us
    pallas_call x2, Pallas kernels, attend_own(): pl.pallas_call(lambda *refs: own_body(part, *refs), in_specs=[pl.BlockSpe...  12.7 us
    ppermute x11, starting transfers between devices, y(): lax.ppermute(value, 'group', [(g, g ^ 1) for g in range(self.groups)])  12 us
    ppermute x17, starting transfers between devices, seq_xor(): return lax.ppermute(value, 'seq', [(s, s ^ bit) for s in range(self.seqs)])  11.2 us
    pallas_call x3, Pallas kernels, ffn_kernel(): pl.pallas_call(lambda *refs: ffn_body(len(rows), len(chunks), splits, *re...  6.78 us
  transfers between devices with their start and end apart: 34, of which 19 were waited for; matrix products, arithmetic and copies ran while one was open for 3% of the time, Pallas kernels for 14%

profile of v5, /device:TPU:0, one launch (start us, length us, event | category | flops | bytes accessed | tf_op | source)
XLA Modules:
  0.0 171.5 jit_solution(16811351550541459223)
XLA Ops:
  0.6 1.2 slice_bitcast_fusion
  1.8 3.1 %collective-permute-start = (bf16[160,1536]{1,0:T(8,128)(2,1)S(1)}, bf16[160,1536]{1,0:T(8,128)(2,1)S(1)}, u32[]{:S(2)}, u32[]{:S(2)}) collective-permute-start(bf16[160,1536]{1,0:T(8,128)(2,1)S(1)} %slice_bitcast_fusion), channel_id=1, source_target_pairs={{0,16},{16,0},{1,17},{17,1},{2,18},{18,2},{3,19},{19,3},{4,20},{20... | collective-permute-start | bytes 1474568 | tf_op jit(solution)/shard_map/ppermute | solution.py:319
  4.9 1.3 pack.1.refs_4_
  6.2 1.6 collective-permute-start.3
  8.5 7.5 %collective-permute-done = bf16[160,1536]{1,0:T(8,128)(2,1)S(1)} collective-permute-done((bf16[160,1536]{1,0:T(8,128)(2,1)S(1)}, bf16[160,1536]{1,0:T(8,128)(2,1)S(1)}, u32[]{:S(2)}, u32[]{:S(2)}) %collective-permute-start) | collective-permute-done | bytes 491552 | tf_op jit(solution)/shard_map/ppermute | solution.py:319
  16.7 6.2 %collective-permute-done.3.refs_6_ = bf16[2304,128]{1,0:T(8,128)(2,1)S(1)} collective-permute-done((bf16[2304,128]{1,0:T(8,128)(2,1)S(1)}, bf16[2304,128]{1,0:T(8,128)(2,1)S(1)}, u32[]{:S(2)}, u32[]{:S(2)}) %collective-permute-start.3) | collective-permute-done | bytes 589856 | tf_op jit(solution)/shard_map/ppermute | solution.py:336
  22.9 1.6 collective-permute-start.1
  24.5 0.5 collective-permute-start.2
  25.0 0.2 collective-permute-start.10
  25.2 13.5 %collective-permute-done.4.refs_8_ = bf16[2304,128]{1,0:T(8,128)(2,1)S(1)} collective-permute-done((bf16[2304,128]{1,0:T(8,128)(2,1)S(1)}, bf16[2304,128]{1,0:T(8,128)(2,1)S(1)}, u32[]{:S(2)}, u32[]{:S(2)}) %collective-permute-start.4) | collective-permute-done | bytes 589856 | tf_op jit(solution)/shard_map/ppermute | solution.py:336
  38.7 0.8 collective-permute-start.7
  39.6 1.3 collective-permute-start.8
  40.9 12.7 %collective-permute-done.5.refs_2_ = bf16[2304,128]{1,0:T(8,128)(2,1)S(1)} collective-permute-done((bf16[2304,128]{1,0:T(8,128)(2,1)S(1)}, bf16[2304,128]{1,0:T(8,128)(2,1)S(1)}, u32[]{:S(2)}, u32[]{:S(2)}) %collective-permute-start.5) | collective-permute-done | bytes 589856 | tf_op jit(solution)/shard_map/ppermute | solution.py:336
  53.7 3.8 %shard_map.130 = (f32[96,1536]{1,0:T(8,128)S(1)}, f32[96,1536]{1,0:T(8,128)S(1)}, f32[96,1536]{1,0:T(8,128)S(1)}, f32[96,1536]{1,0:T(8,128)S(1)}, f32[96,1536]{1...) custom-call(bf16[192,1536]{1,0:T(8,128)(2,1)S(1)} %collective-permute-done.7.refs_0_, ...), custom_call_target="tpu_custom_call" | custom-call | flops 2717908992 | bytes 5898240 | tf_op jit(solution)/shard_map/pallas_call | solution.py:414
  57.5 1.5 shard_map.132
  59.0 1.0 collective-permute-start.13
  60.0 1.1 collective-permute-start.12
  61.1 1.5 collective-permute-start.15
  62.6 0.5 collective-permute-start.16
  63.1 1.5 shard_map.131
  64.6 4.4 %collective-permute-done.13 = bf16[96,1536]{1,0:T(8,128)(2,1)S(1)} collective-permute-done((bf16[96,1536]{1,0:T(8,128)(2,1)S(1)}, bf16[96,1536]{1,0:T(8,128)(2,1)S(1)}, u32[]{:S(2)}, u32[]{:S(2)}) %collective-permute-start.13) | collective-permute-done | bytes 294944 | tf_op jit(solution)/shard_map/ppermute | solution.py:319
  69.0 1.6 collective-permute-start.14
  70.5 6.7 %collective-permute-done.16 = bf16[96,1536]{1,0:T(8,128)(2,1)S(1)} collective-permute-done((bf16[96,1536]{1,0:T(8,128)(2,1)S(1)}, bf16[96,1536]{1,0:T(8,128)(2,1)S(1)}, u32[]{:S(2)}, u32[]{:S(2)}) %collective-permute-start.16) | collective-permute-done | bytes 294944 | tf_op jit(solution)/shard_map/ppermute | solution.py:310
  77.3 1.0 collective-permute-start.17
  78.4 4.2 %collective-permute-done.14.refs_2_ = bf16[96,1536]{1,0:T(8,128)(2,1)S(1)} collective-permute-done((bf16[96,1536]{1,0:T(8,128)(2,1)S(1)}, bf16[96,1536]{1,0:T(8,128)(2,1)S(1)}, u32[]{:S(2)}, u32[]{:S(2)}) %collective-permute-start.14) | collective-permute-done | bytes 294944 | tf_op jit(solution)/shard_map/ppermute | solution.py:310
  82.6 1.8 %collective-permute-done.17.refs_5_ = bf16[96,1536]{1,0:T(8,128)(2,1)S(1)} collective-permute-done((bf16[96,1536]{1,0:T(8,128)(2,1)S(1)}, bf16[96,1536]{1,0:T(8,128)(2,1)S(1)}, u32[]{:S(2)}, u32[]{:S(2)}) %collective-permute-start.17) | collective-permute-done | bytes 294944 | tf_op jit(solution)/shard_map/ppermute | solution.py:319
  84.4 1.4 finish.1
  85.8 1.0 collective-permute-start.19
  86.8 3.4 %collective-permute-done.19 = bf16[24,768]{1,0:T(8,128)(2,1)S(1)} collective-permute-done((bf16[24,768]{1,0:T(8,128)(2,1)S(1)}, bf16[24,768]{1,0:T(8,128)(2,1)S(1)}, u32[]{:S(2)}, u32[]{:S(2)}) %collective-permute-start.19) | collective-permute-done | bytes 36896 | tf_op jit(solution)/shard_map/ppermute | solution.py:319
  90.3 1.0 collective-permute-start.18
  91.3 3.8 %collective-permute-done.20.second_ref = bf16[24,768]{1,0:T(8,128)(2,1)S(1)} collective-permute-done((bf16[24,768]{1,0:T(8,128)(2,1)S(1)}, bf16[24,768]{1,0:T(8,128)(2,1)S(1)}, u32[]{:S(2)}, u32[]{:S(2)}) %collective-permute-start.20) | collective-permute-done | bytes 36896 | tf_op jit(solution)/shard_map/ppermute | solution.py:310
  95.1 4.3 %collective-permute-done.21.second_ref = bf16[48,768]{1,0:T(8,128)(2,1)S(1)} collective-permute-done((bf16[48,768]{1,0:T(8,128)(2,1)S(1)}, bf16[48,768]{1,0:T(8,128)(2,1)S(1)}, u32[]{:S(2)}, u32[]{:S(2)}) %collective-permute-start.21) | collective-permute-done | bytes 73760 | tf_op jit(solution)/shard_map/ppermute | solution.py:310
  99.5 1.6 collective-permute-start.22
  101.1 0.8 grads_in.1
  101.9 0.9 copy-done.4
  102.8 0.8 copy-done.5
  103.6 3.5 %turn.1 = (bf16[768,768]{1,0:T(8,128)(2,1)}, bf16[768,768]{1,0:T(8,128)(2,1)}, bf16[768,768]{1,0:T(8,128)(2,1)}) custom-call(bf16[768,768]{1,0:T(8,128)(2,1)} %refs_0_.3, bf16[768,768]{1,0:T(8,128)(2,1)} %refs_1_.1, bf16[768,768]{1,0:T(8,128)(2,1)} %refs_2_.1), custom_call_target="tpu_custom_call" | custom-call | tf_op jit(solution)/shard_map/turn/pallas_call | solution.py:102
  107.1 1.0 tokens.1
  108.2 6.5 %attend_own.2 = (bf16[384,352]{1,0:T(8,128)(2,1)}, bf16[8,352,352]{2,1,0:T(8,128)(2,1)}, f32[8,1,352]{2,1,0:T(1,128)}, f32[8,1,352]{2,1,0:T(1,128)}, f32[384,352]{1,0:T(8,128)}) custom-call(s32[1,1]{1,0:T(1,128)} %copy.21.count_ref.refs_0_, bf16[352,768]{1,0:T(8,128)(2,1)} %get-tuple-element.69.refs_1_.refs_16_, bf16[768,768]{1,0:T(8,128)(2,1)} %get-tuple-element.70.refs_2_, ...), custom_call_target="tpu_custom_call" | custom-call | flops 1903165440 | bytes 1982464 | tf_op jit(solution)/shard_map/attend_own/pallas_call | solution.py:235
  114.7 6.3 %attend_own.3 = (bf16[384,352]{1,0:T(8,128)(2,1)}, bf16[8,352,352]{2,1,0:T(8,128)(2,1)}, f32[8,1,352]{2,1,0:T(1,128)}, f32[8,1,352]{2,1,0:T(1,128)}, f32[384,352]{1,0:T(8,128)}) custom-call(s32[1,1]{1,0:T(1,128)} %copy.21.count_ref.refs_0_, bf16[352,768]{1,0:T(8,128)(2,1)} %get-tuple-element.69.refs_1_.refs_16_, bf16[768,768]{1,0:T(8,128)(2,1)} %get-tuple-element.70.refs_2_, ...), custom_call_target="tpu_custom_call" | custom-call | flops 1903165440 | bytes 1982464 | tf_op jit(solution)/shard_map/attend_own/pallas_call | solution.py:235
  121.1 0.8 copy-done.2
  121.9 15.0 %attend_far.1 = (bf16[768,352]{1,0:T(8,128)(2,1)S(1)}, f32[384,768]{1,0:T(8,128)S(1)}, bf16[384,768]{1,0:T(8,128)(2,1)}, f32[384,768]{1,0:T(8,128)S(1)}, bf16[384,768]{1,0:T(8,128)(2,1)}) custom-call(s32[1]{0:T(128)} %bitcast.9.refs_0_, bf16[384,768]{1,0:T(8,128)(2,1)} %copy-done.2, bf16[768,768]{1,0:T(8,128)(2,1)} %get-tuple-element.66.refs_3_.refs_2_, ...), custom_call_target="tpu_custom_call" | custom-call | flops 3806330880 | bytes 3964928 | tf_op jit(solution)/shard_map/attend_far/pallas_call | solution.py:264
  136.9 0.8 copy-done.6
  137.7 0.5 collective-permute-start.24
  138.2 1.9 %collective-permute-done.24 = bf16[384,768]{1,0:T(8,128)(2,1)} collective-permute-done((bf16[384,768]{1,0:T(8,128)(2,1)}, bf16[384,768]{1,0:T(8,128)(2,1)}, u32[]{:S(2)}, u32[]{:S(2)}) %collective-permute-start.24) | collective-permute-done | bytes 589856 | tf_op jit(solution)/shard_map/ppermute | solution.py:310
  140.2 1.2 convert_add_fusion.1
  141.4 0.6 collective-permute-start.25
  142.0 1.2 convert_add_fusion
  143.2 1.0 collective-permute-start.28
  144.2 6.5 %collective-permute-done.25 = bf16[4,2,24,768]{3,2,1,0:T(8,128)(2,1)S(1)} collective-permute-done((bf16[4,2,24,768]{3,2,1,0:T(8,128)(2,1)S(1)}, bf16[4,2,24,768]{3,2,1,0:T(8,128)(2,1)S(1)}, u32[]{:S(2)}, u32[]{:S(2)}) %collective-permute-start.25) | collective-permute-done | bytes 294944 | tf_op jit(solution)/shard_map/ppermute | solution.py:310
  150.8 0.6 collective-permute-start.26
  151.4 0.9 collective-permute-done.28
  152.4 1.8 %collective-permute-start.29 = (bf16[4,24,768]{2,1,0:T(8,128)(2,1)S(1)}, bf16[4,24,768]{2,1,0:T(8,128)(2,1)S(1)}, u32[]{:S(2)}, u32[]{:S(2)}) collective-permute-start(bf16[4,24,768]{2,1,0:T(8,128)(2,1)S(1)} %fusion.6), channel_id=1, source_target_pairs={{0,2},{1,3},{2,0},{3,1},{4,6},{5,7},{6,4},{7,5},{8,10},{9,11},{10,... | collective-permute-start | bytes 442376 | tf_op jit(solution)/shard_map/ppermute | solution.py:310
  154.2 2.0 %collective-permute-done.26 = bf16[4,24,768]{2,1,0:T(8,128)(2,1)S(1)} collective-permute-done((bf16[4,24,768]{2,1,0:T(8,128)(2,1)S(1)}, bf16[4,24,768]{2,1,0:T(8,128)(2,1)S(1)}, u32[]{:S(2)}, u32[]{:S(2)}) %collective-permute-start.26) | collective-permute-done | bytes 147488 | tf_op jit(solution)/shard_map/ppermute | solution.py:319
  156.2 1.4 collective-permute-done.29
  157.7 1.7 collective-permute-start.32
  159.4 0.6 collective-permute-start.30
  160.0 0.6 select_convert_fusion
  160.7 1.7 collective-permute-done.32
  162.4 3.9 %collective-permute-done.31 = bf16[24,1536]{1,0:T(8,128)(2,1)S(1)} collective-permute-done((bf16[24,1536]{1,0:T(8,128)(2,1)S(1)}, bf16[24,1536]{1,0:T(8,128)(2,1)S(1)}, u32[]{:S(2)}, u32[]{:S(2)}) %collective-permute-start.31) | collective-permute-done | bytes 73760 | tf_op jit(solution)/shard_map/ppermute | solution.py:326
  166.3 0.9 collective-permute-start.33
  167.3 0.9 pad_bitcast_fusion
  168.1 2.6 %collective-permute-done.33 = bf16[24,1536]{1,0:T(8,128)(2,1)S(1)} collective-permute-done((bf16[24,1536]{1,0:T(8,128)(2,1)S(1)}, bf16[24,1536]{1,0:T(8,128)(2,1)S(1)}, u32[]{:S(2)}, u32[]{:S(2)}) %collective-permute-start.33) | collective-permute-done | bytes 73760 | tf_op jit(solution)/shard_map/ppermute | solution.py:319
  170.8 0.7 fusion.16
  (74 shorter events, 1.6 us)
Async XLA Ops:
  0.6 7.9 %copy-start.8 = (bf16[1,384,1536]{2,1,0:T(8,128)(2,1)S(1)}, bf16[1,384,1536]{2,1,0:T(8,128)(2,1)}, u32[]{:S(2)}) copy-start(bf16[1,384,1536]{2,1,0:T(8,128)(2,1)} %param.11) | copy-start | bytes 3538948
  1.8 14.3 %collective-permute-start = (bf16[160,1536]{1,0:T(8,128)(2,1)S(1)}, bf16[160,1536]{1,0:T(8,128)(2,1)S(1)}, u32[]{:S(2)}, u32[]{:S(2)}) collective-permute-start(bf16[160,1536]{1,0:T(8,128)(2,1)S(1)} %slice_bitcast_fusion), channel_id=1, source_target_pairs={{0,16},{16,0},{1,17},{17,1},{2,18},{18,2},{3,19},{19,3},{4,20},{20... | collective-permute-start | bytes 1474568 | tf_op jit(solution)/shard_map/ppermute | solution.py:319
  6.2 16.7 %collective-permute-start.3 = (bf16[2304,128]{1,0:T(8,128)(2,1)S(1)}, bf16[2304,128]{1,0:T(8,128)(2,1)S(1)}, u32[]{:S(2)}, u32[]{:S(2)}) collective-permute-start(bf16[2304,128]{1,0:T(8,128)(2,1)S(1)} %pack.1.refs_4_), channel_id=1, source_target_pairs={{0,4},{1,5},{2,6},{3,7},{4,8},{5,9},{6,10},{7,11},{8,12},{9,13},{1... | collective-permute-start | bytes 1769480 | tf_op jit(solution)/shard_map/ppermute | solution.py:336
  22.9 15.8 %collective-permute-start.4 = (bf16[2304,128]{1,0:T(8,128)(2,1)S(1)}, bf16[2304,128]{1,0:T(8,128)(2,1)S(1)}, u32[]{:S(2)}, u32[]{:S(2)}) collective-permute-start(bf16[2304,128]{1,0:T(8,128)(2,1)S(1)} %collective-permute-done.3.refs_6_), channel_id=1, source_target_pairs={{0,4},{1,5},{2,6},{3,7},{4,8},{5,9},{6,10},{7,11},{8,12},{9,13},{1... | collective-permute-start | bytes 1769480 | tf_op jit(solution)/shard_map/ppermute | solution.py:336
  22.9 15.8 %collective-permute-start.1 = (bf16[96,1536]{1,0:T(8,128)(2,1)S(1)}, bf16[96,1536]{1,0:T(8,128)(2,1)S(1)}, u32[]{:S(2)}, u32[]{:S(2)}) collective-permute-start(bf16[96,1536]{1,0:T(8,128)(2,1)S(1)} %get-tuple-element.88), channel_id=1, source_target_pairs={{0,2},{1,3},{2,0},{3,1},{4,6},{5,7},{6,4},{7,5},{8,10},{9,11},{10,... | collective-permute-start | bytes 884744 | tf_op jit(solution)/shard_map/ppermute | solution.py:310
  24.5 16.4 %collective-permute-start.9 = (bf16[2304,128]{1,0:T(8,128)(2,1)S(1)}, bf16[2304,128]{1,0:T(8,128)(2,1)S(1)}, u32[]{:S(2)}, u32[]{:S(2)}) collective-permute-start(bf16[2304,128]{1,0:T(8,128)(2,1)S(1)} %pack.1.refs_4_), channel_id=1, source_target_pairs={{0,1},{1,0},{2,3},{3,2},{4,5},{5,4},{6,7},{7,6},{8,9},{9,8},{10,11... | collective-permute-start | bytes 1769480 | tf_op jit(solution)/shard_map/ppermute | solution.py:310
  24.5 15.0 %collective-permute-start.2 = (bf16[96,1536]{1,0:T(8,128)(2,1)S(1)}, bf16[96,1536]{1,0:T(8,128)(2,1)S(1)}, u32[]{:S(2)}, u32[]{:S(2)}) collective-permute-start(bf16[96,1536]{1,0:T(8,128)(2,1)S(1)} %get-tuple-element.87), channel_id=1, source_target_pairs={{0,16},{16,0},{1,17},{17,1},{2,18},{18,2},{3,19},{19,3},{4,20},{20... | collective-permute-start | bytes 884744 | tf_op jit(solution)/shard_map/ppermute | solution.py:319
  25.0 28.6 %collective-permute-start.10 = (bf16[2304,128]{1,0:T(8,128)(2,1)S(1)}, bf16[2304,128]{1,0:T(8,128)(2,1)S(1)}, u32[]{:S(2)}, u32[]{:S(2)}) collective-permute-start(bf16[2304,128]{1,0:T(8,128)(2,1)S(1)} %collective-permute-done.3.refs_6_), channel_id=1, source_target_pairs={{0,1},{1,0},{2,3},{3,2},{4,5},{5,4},{6,7},{7,6},{8,9},{9,8},{10,11... | collective-permute-start | bytes 1769480 | tf_op jit(solution)/shard_map/ppermute | solution.py:310
  38.7 14.9 %collective-permute-start.5 = (bf16[2304,128]{1,0:T(8,128)(2,1)S(1)}, bf16[2304,128]{1,0:T(8,128)(2,1)S(1)}, u32[]{:S(2)}, u32[]{:S(2)}) collective-permute-start(bf16[2304,128]{1,0:T(8,128)(2,1)S(1)} %collective-permute-done.4.refs_8_), channel_id=1, source_target_pairs={{0,4},{1,5},{2,6},{3,7},{4,8},{5,9},{6,10},{7,11},{8,12},{9,13},{1... | collective-permute-start | bytes 1769480 | tf_op jit(solution)/shard_map/ppermute | solution.py:336
  38.7 14.9 %collective-permute-start.7 = (bf16[192,1536]{1,0:T(8,128)(2,1)S(1)}, bf16[192,1536]{1,0:T(8,128)(2,1)S(1)}, u32[]{:S(2)}, u32[]{:S(2)}) collective-permute-start(bf16[192,1536]{1,0:T(8,128)(2,1)S(1)} %pad_maximum_fusion.2.refs_2_.refs_0_), channel_id=1, source_target_pairs={{0,16},{16,0},{1,17},{17,1},{2,18},{18,2},{3,19},{19,3},{4,20},{20... | collective-permute-start | bytes 1769480 | tf_op jit(solution)/shard_map/ppermute | solution.py:319
  39.6 14.1 %collective-permute-start.8 = (bf16[192,1536]{1,0:T(8,128)(2,1)S(1)}, bf16[192,1536]{1,0:T(8,128)(2,1)S(1)}, u32[]{:S(2)}, u32[]{:S(2)}) collective-permute-start(bf16[192,1536]{1,0:T(8,128)(2,1)S(1)} %pad_maximum_fusion.3.refs_3_.refs_1_), channel_id=1, source_target_pairs={{0,2},{1,3},{2,0},{3,1},{4,6},{5,7},{6,4},{7,5},{8,10},{9,11},{10,... | collective-permute-start | bytes 1769480 | tf_op jit(solution)/shard_map/ppermute | solution.py:310
  40.9 12.7 %collective-permute-start.11 = (bf16[2304,128]{1,0:T(8,128)(2,1)S(1)}, bf16[2304,128]{1,0:T(8,128)(2,1)S(1)}, u32[]{:S(2)}, u32[]{:S(2)}) collective-permute-start(bf16[2304,128]{1,0:T(8,128)(2,1)S(1)} %collective-permute-done.4.refs_8_), channel_id=1, source_target_pairs={{0,1},{1,0},{2,3},{3,2},{4,5},{5,4},{6,7},{7,6},{8,9},{9,8},{10,11... | collective-permute-start | bytes 1769480 | tf_op jit(solution)/shard_map/ppermute | solution.py:310
  53.6 3.9 %collective-permute-start.6 = (bf16[2304,128]{1,0:T(8,128)(2,1)S(1)}, bf16[2304,128]{1,0:T(8,128)(2,1)S(1)}, u32[]{:S(2)}, u32[]{:S(2)}) collective-permute-start(bf16[2304,128]{1,0:T(8,128)(2,1)S(1)} %collective-permute-done.5.refs_2_), channel_id=1, source_target_pairs={{0,1},{1,0},{2,3},{3,2},{4,5},{5,4},{6,7},{7,6},{8,9},{9,8},{10,11... | collective-permute-start | bytes 1769480 | tf_op jit(solution)/shard_map/ppermute | solution.py:310
  59.0 9.9 %collective-permute-start.13 = (bf16[96,1536]{1,0:T(8,128)(2,1)S(1)}, bf16[96,1536]{1,0:T(8,128)(2,1)S(1)}, u32[]{:S(2)}, u32[]{:S(2)}) collective-permute-start(bf16[96,1536]{1,0:T(8,128)(2,1)S(1)} %get-tuple-element.56), channel_id=1, source_target_pairs={{0,16},{16,0},{1,17},{17,1},{2,18},{18,2},{3,19},{19,3},{4,20},{20... | collective-permute-start | bytes 884744 | tf_op jit(solution)/shard_map/ppermute | solution.py:319
  60.0 18.4 %collective-permute-start.12 = (bf16[96,1536]{1,0:T(8,128)(2,1)S(1)}, bf16[96,1536]{1,0:T(8,128)(2,1)S(1)}, u32[]{:S(2)}, u32[]{:S(2)}) collective-permute-start(bf16[96,1536]{1,0:T(8,128)(2,1)S(1)} %get-tuple-element.54), channel_id=1, source_target_pairs={{0,16},{16,0},{1,17},{17,1},{2,18},{18,2},{3,19},{19,3},{4,20},{20... | collective-permute-start | bytes 884744 | tf_op jit(solution)/shard_map/ppermute | solution.py:319
  61.1 17.3 %collective-permute-start.15 = (bf16[96,1536]{1,0:T(8,128)(2,1)S(1)}, bf16[96,1536]{1,0:T(8,128)(2,1)S(1)}, u32[]{:S(2)}, u32[]{:S(2)}) collective-permute-start(bf16[96,1536]{1,0:T(8,128)(2,1)S(1)} %get-tuple-element.58), channel_id=1, source_target_pairs={{0,2},{1,3},{2,0},{3,1},{4,6},{5,7},{6,4},{7,5},{8,10},{9,11},{10,... | collective-permute-start | bytes 884744 | tf_op jit(solution)/shard_map/ppermute | solution.py:310
  62.6 14.7 %collective-permute-start.16 = (bf16[96,1536]{1,0:T(8,128)(2,1)S(1)}, bf16[96,1536]{1,0:T(8,128)(2,1)S(1)}, u32[]{:S(2)}, u32[]{:S(2)}) collective-permute-start(bf16[96,1536]{1,0:T(8,128)(2,1)S(1)} %get-tuple-element.60), channel_id=1, source_target_pairs={{0,2},{1,3},{2,0},{3,1},{4,6},{5,7},{6,4},{7,5},{8,10},{9,11},{10,... | collective-permute-start | bytes 884744 | tf_op jit(solution)/shard_map/ppermute | solution.py:310
  69.0 13.6 %collective-permute-start.14 = (bf16[96,1536]{1,0:T(8,128)(2,1)S(1)}, bf16[96,1536]{1,0:T(8,128)(2,1)S(1)}, u32[]{:S(2)}, u32[]{:S(2)}) collective-permute-start(bf16[96,1536]{1,0:T(8,128)(2,1)S(1)} %add_convert_fusion.1), channel_id=1, source_target_pairs={{0,2},{1,3},{2,0},{3,1},{4,6},{5,7},{6,4},{7,5},{8,10},{9,11},{10,... | collective-permute-start | bytes 884744 | tf_op jit(solution)/shard_map/ppermute | solution.py:310
  77.3 7.1 %copy-start = (bf16[1536,768]{1,0:T(8,128)(2,1)S(1)}, bf16[1536,768]{1,0:T(8,128)(2,1)}, u32[]{:S(2)}) copy-start(bf16[1536,768]{1,0:T(8,128)(2,1)} %refs_6_.1) | copy-start | bytes 7077892
  77.3 7.0 %collective-permute-start.17 = (bf16[96,1536]{1,0:T(8,128)(2,1)S(1)}, bf16[96,1536]{1,0:T(8,128)(2,1)S(1)}, u32[]{:S(2)}, u32[]{:S(2)}) collective-permute-start(bf16[96,1536]{1,0:T(8,128)(2,1)S(1)} %add_convert_fusion), channel_id=1, source_target_pairs={{0,16},{16,0},{1,17},{17,1},{2,18},{18,2},{3,19},{19,3},{4,20},{20... | collective-permute-start | bytes 884744 | tf_op jit(solution)/shard_map/ppermute | solution.py:319
  84.4 16.7 %copy-start.1 = (bf16[768,768]{1,0:T(8,128)(2,1)S(1)}, bf16[768,768]{1,0:T(8,128)(2,1)}, u32[]{:S(2)}) copy-start(bf16[768,768]{1,0:T(8,128)(2,1)} %w_out_ref.1) | copy-start | bytes 3538948
  84.4 16.7 %copy-start.3 = (bf16[1,384,768]{2,1,0:T(8,128)(2,1)S(1)}, bf16[1,384,768]{2,1,0:T(8,128)(2,1)}, u32[]{:S(2)}) copy-start(bf16[1,384,768]{2,1,0:T(8,128)(2,1)} %param.21) | copy-start | bytes 1769476
  85.8 4.4 %collective-permute-start.19 = (bf16[24,768]{1,0:T(8,128)(2,1)S(1)}, bf16[24,768]{1,0:T(8,128)(2,1)S(1)}, u32[]{:S(2)}, u32[]{:S(2)}) collective-permute-start(bf16[24,768]{1,0:T(8,128)(2,1)S(1)} %get-tuple-element.64), channel_id=1, source_target_pairs={{0,16},{16,0},{1,17},{17,1},{2,18},{18,2},{3,19},{19,3},{4,20},{20... | collective-permute-start | bytes 110600 | tf_op jit(solution)/shard_map/ppermute | solution.py:319
  90.3 4.9 %collective-permute-start.20 = (bf16[24,768]{1,0:T(8,128)(2,1)S(1)}, bf16[24,768]{1,0:T(8,128)(2,1)S(1)}, u32[]{:S(2)}, u32[]{:S(2)}) collective-permute-start(bf16[24,768]{1,0:T(8,128)(2,1)S(1)} %broadcast_select_fusion.2.first_ref), channel_id=1, source_target_pairs={{0,8},{1,9},{2,10},{3,11},{4,12},{5,13},{6,14},{7,15},{8,0},{9,1},... | collective-permute-start | bytes 110600 | tf_op jit(solution)/shard_map/ppermute | solution.py:310
  90.3 16.8 %collective-permute-start.18 = (bf16[160,768]{1,0:T(8,128)(2,1)S(1)}, bf16[160,768]{1,0:T(8,128)(2,1)S(1)}, u32[]{:S(2)}, u32[]{:S(2)}) collective-permute-start(bf16[160,768]{1,0:T(8,128)(2,1)S(1)} %get-tuple-element.62), channel_id=1, source_target_pairs={{0,16},{16,0},{1,17},{17,1},{2,18},{18,2},{3,19},{19,3},{4,20},{20... | collective-permute-start | bytes 737288 | tf_op jit(solution)/shard_map/ppermute | solution.py:319
  95.1 4.4 %collective-permute-start.21 = (bf16[48,768]{1,0:T(8,128)(2,1)S(1)}, bf16[48,768]{1,0:T(8,128)(2,1)S(1)}, u32[]{:S(2)}, u32[]{:S(2)}) collective-permute-start(bf16[48,768]{1,0:T(8,128)(2,1)S(1)} %join.4.first_ref), channel_id=1, source_target_pairs={{0,4},{1,5},{2,6},{3,7},{4,0},{5,1},{6,2},{7,3},{8,12},{9,13},{10,... | collective-permute-start | bytes 221192 | tf_op jit(solution)/shard_map/ppermute | solution.py:310
  99.5 8.6 %collective-permute-start.22 = (bf16[96,768]{1,0:T(8,128)(2,1)S(1)}, bf16[96,768]{1,0:T(8,128)(2,1)S(1)}, u32[]{:S(2)}, u32[]{:S(2)}) collective-permute-start(bf16[96,768]{1,0:T(8,128)(2,1)S(1)} %join.5.first_ref), channel_id=1, source_target_pairs={{0,2},{1,3},{2,0},{3,1},{4,6},{5,7},{6,4},{7,5},{8,10},{9,11},{10,... | collective-permute-start | bytes 442376 | tf_op jit(solution)/shard_map/ppermute | solution.py:310
  101.9 0.9 copy-start.4
  102.8 0.8 copy-start.5
  108.2 12.8 %collective-permute-start.23 = (bf16[192,768]{1,0:T(8,128)(2,1)S(1)}, bf16[192,768]{1,0:T(8,128)(2,1)S(1)}, u32[]{:S(2)}, u32[]{:S(2)}) collective-permute-start(bf16[192,768]{1,0:T(8,128)(2,1)S(1)} %join.6.first_ref), channel_id=1, source_target_pairs={{0,1},{1,0},{2,3},{3,2},{4,5},{5,4},{6,7},{7,6},{8,9},{9,8},{10,11... | collective-permute-start | bytes 884744 | tf_op jit(solution)/shard_map/ppermute | solution.py:310
  121.1 0.8 copy-start.2
  136.9 0.8 copy-start.6
  137.7 2.5 %collective-permute-start.24 = (bf16[384,768]{1,0:T(8,128)(2,1)}, bf16[384,768]{1,0:T(8,128)(2,1)}, u32[]{:S(2)}, u32[]{:S(2)}) collective-permute-start(bf16[384,768]{1,0:T(8,128)(2,1)} %get-tuple-element.84), channel_id=1, source_target_pairs={{0,1},{1,0},{2,3},{3,2},{4,5},{5,4},{6,7},{7,6},{8,9},{9,8},{10,11... | collective-permute-start | bytes 1769480 | tf_op jit(solution)/shard_map/ppermute | solution.py:310
  138.2 3.8 %collective-permute-start.27 = (bf16[384,768]{1,0:T(8,128)(2,1)}, bf16[384,768]{1,0:T(8,128)(2,1)}, u32[]{:S(2)}, u32[]{:S(2)}) collective-permute-start(bf16[384,768]{1,0:T(8,128)(2,1)} %get-tuple-element.86), channel_id=1, source_target_pairs={{0,1},{1,0},{2,3},{3,2},{4,5},{5,4},{6,7},{7,6},{8,9},{9,8},{10,11... | collective-permute-start | bytes 1769480 | tf_op jit(solution)/shard_map/ppermute | solution.py:310
  141.4 9.4 %collective-permute-start.25 = (bf16[4,2,24,768]{3,2,1,0:T(8,128)(2,1)S(1)}, bf16[4,2,24,768]{3,2,1,0:T(8,128)(2,1)S(1)}, u32[]{:S(2)}, u32[]{:S(2)}) collective-permute-start(bf16[4,2,24,768]{3,2,1,0:T(8,128)(2,1)S(1)} %fusion.3), channel_id=1, source_target_pairs={{0,2},{1,3},{2,0},{3,1},{4,6},{5,7},{6,4},{7,5},{8,10},{9,11},{10,... | collective-permute-start | bytes 884744 | tf_op jit(solution)/shard_map/ppermute | solution.py:310
  143.2 9.1 %collective-permute-start.28 = (bf16[4,2,24,768]{3,2,0,1:T(8,128)(2,1)S(1)}, bf16[4,2,24,768]{3,2,0,1:T(8,128)(2,1)S(1)}, u32[]{:S(2)}, u32[]{:S(2)}) collective-permute-start(bf16[4,2,24,768]{3,2,0,1:T(8,128)(2,1)S(1)} %fusion.4), channel_id=1, source_target_pairs={{0,16},{16,0},{1,17},{17,1},{2,18},{18,2},{3,19},{19,3},{4,20},{20... | collective-permute-start | bytes 884744 | tf_op jit(solution)/shard_map/ppermute | solution.py:319
  150.8 5.3 %collective-permute-start.26 = (bf16[4,24,768]{2,1,0:T(8,128)(2,1)S(1)}, bf16[4,24,768]{2,1,0:T(8,128)(2,1)S(1)}, u32[]{:S(2)}, u32[]{:S(2)}) collective-permute-start(bf16[4,24,768]{2,1,0:T(8,128)(2,1)S(1)} %fusion.5), channel_id=1, source_target_pairs={{0,16},{16,0},{1,17},{17,1},{2,18},{18,2},{3,19},{19,3},{4,20},{20... | collective-permute-start | bytes 442376 | tf_op jit(solution)/shard_map/ppermute | solution.py:319
  152.4 5.2 %collective-permute-start.29 = (bf16[4,24,768]{2,1,0:T(8,128)(2,1)S(1)}, bf16[4,24,768]{2,1,0:T(8,128)(2,1)S(1)}, u32[]{:S(2)}, u32[]{:S(2)}) collective-permute-start(bf16[4,24,768]{2,1,0:T(8,128)(2,1)S(1)} %fusion.6), channel_id=1, source_target_pairs={{0,2},{1,3},{2,0},{3,1},{4,6},{5,7},{6,4},{7,5},{8,10},{9,11},{10,... | collective-permute-start | bytes 442376 | tf_op jit(solution)/shard_map/ppermute | solution.py:310
  156.2 3.8 %copy-start.7 = (bf16[768,352]{1,0:T(8,128)(2,1)S(1)}, bf16[768,352]{1,0:T(8,128)(2,1)}, u32[]{:S(2)}) copy-start(bf16[768,352]{1,0:T(8,128)(2,1)} %copy-done.6) | copy-start | bytes 1622020
  156.2 3.8 %copy-start.9 = (bf16[352,768]{1,0:T(8,128)(2,1)S(1)}, bf16[352,768]{1,0:T(8,128)(2,1)}, u32[]{:S(2)}) copy-start(bf16[352,768]{1,0:T(8,128)(2,1)} %get-tuple-element.63) | copy-start | bytes 1622020
  157.7 4.6 %collective-permute-start.32 = (bf16[24,1536]{1,0:T(8,128)(2,1)S(1)}, bf16[24,1536]{1,0:T(8,128)(2,1)S(1)}, u32[]{:S(2)}, u32[]{:S(2)}) collective-permute-start(bf16[24,1536]{1,0:T(8,128)(2,1)S(1)} %get-tuple-element.92), channel_id=1, source_target_pairs={{0,12},{1,13},{2,14},{3,15},{4,0},{5,1},{6,2},{7,3},{8,4},{9,5},{1... | collective-permute-start | bytes 221192 | tf_op jit(solution)/shard_map/ppermute | solution.py:326
  159.4 6.9 %collective-permute-start.31 = (bf16[24,1536]{1,0:T(8,128)(2,1)S(1)}, bf16[24,1536]{1,0:T(8,128)(2,1)S(1)}, u32[]{:S(2)}, u32[]{:S(2)}) collective-permute-start(bf16[24,1536]{1,0:T(8,128)(2,1)S(1)} %get-tuple-element.93), channel_id=1, source_target_pairs={{0,8},{1,9},{2,10},{3,11},{4,12},{5,13},{6,14},{7,15},{8,0},{9,1},... | collective-permute-start | bytes 221192 | tf_op jit(solution)/shard_map/ppermute | solution.py:326
  159.4 6.9 %collective-permute-start.30 = (bf16[24,1536]{1,0:T(8,128)(2,1)S(1)}, bf16[24,1536]{1,0:T(8,128)(2,1)S(1)}, u32[]{:S(2)}, u32[]{:S(2)}) collective-permute-start(bf16[24,1536]{1,0:T(8,128)(2,1)S(1)} %get-tuple-element.91), channel_id=1, source_target_pairs={{0,4},{1,5},{2,6},{3,7},{4,8},{5,9},{6,10},{7,11},{8,12},{9,13},{1... | collective-permute-start | bytes 221192 | tf_op jit(solution)/shard_map/ppermute | solution.py:326
  166.3 4.4 %collective-permute-start.33 = (bf16[24,1536]{1,0:T(8,128)(2,1)S(1)}, bf16[24,1536]{1,0:T(8,128)(2,1)S(1)}, u32[]{:S(2)}, u32[]{:S(2)}) collective-permute-start(bf16[24,1536]{1,0:T(8,128)(2,1)S(1)} %fusion.12), channel_id=1, source_target_pairs={{0,16},{16,0},{1,17},{17,1},{2,18},{18,2},{3,19},{19,3},{4,20},{20... | collective-permute-start | bytes 221192 | tf_op jit(solution)/shard_map/ppermute | solution.py:319

commit v6 on v5

--- a/solution.py
+++ b/solution.py
@@ -113,24 +113,21 @@
 
 
 def own_body(
-    part, count_ref, rows_in, wq_in, wk_in, wv_in, q_out, e_out, m_out, l_out, o_out,
-    rows_ref, wq_ref, wk_ref, wv_ref, q_ref, e_ref, m_ref, l_ref, o_ref, sems,
+    part, count_ref, rows_ref, wq_in, wk_in, wv_in, q_out, e_out, m_out, l_out, o_out,
+    wq_ref, wk_ref, wv_ref, q_ref, e_ref, m_ref, l_ref, o_ref, sems,
 ):
     cut = pl.ds(part * HEADS_A_CALL * HEAD, HEADS_A_CALL * HEAD)
     got = fetch(
-        (rows_in, wq_in.at[cut], wk_in.at[cut], wv_in.at[cut]),
-        (rows_ref, wq_ref, wk_ref, wv_ref),
-        sems,
-    )
-    got[0].wait()
+        (wq_in.at[cut], wk_in.at[cut], wv_in.at[cut]), (wq_ref, wk_ref, wv_ref), sems
+    )
     rows = rows_ref[...]
     bias = jnp.where(valid_column(count_ref, rows.shape[0]), 0.0, -1e30)
-    got[1].wait()
+    got[0].wait()
     scale = 1.0 / (math.sqrt(HEAD) * math.log(2.0))
     q_ref[...] = (mm_nt(wq_ref[...], rows) * scale).astype(jnp.bfloat16)
+    got[1].wait()
+    keys = project_t(wk_ref[...], rows)
     got[2].wait()
-    keys = project_t(wk_ref[...], rows)
-    got[3].wait()
     values = project_t(wv_ref[...], rows)
     sent = fetch([q_ref], [q_out], sems, 4)
     for h in range(HEADS_A_CALL):
@@ -144,38 +141,47 @@
         e_ref[h] = low
         sent += fetch([e_ref.at[h]], [e_out.at[h]], sems, 8 + h)
         o_ref[at] = mm(values[at], low)
-    sent += fetch((m_ref, l_ref, o_ref), (m_out, l_out, o_out), sems, 5)
+        sent += fetch([o_ref.at[at]], [o_out.at[at]], sems, 8 + HEADS_A_CALL + h)
+    sent += fetch((m_ref, l_ref), (m_out, l_out), sems, 5)
     for copy in sent:
         copy.wait()
 
 
 def far_body(dilated, *refs):
     parts = HEADS // HEADS_A_CALL
-    count = 6 + 5 * parts
-    core_ref, ins, outs = refs[0], refs[1 : 1 + count], refs[1 + count : 6 + count]
-    held, sems = refs[6 + count : 6 + 2 * count], refs[-1]
-    keys_ref, values_ref, own_ref, far_ref, turned_ref, turned_far_ref = refs[-7:-1]
-    got = fetch(ins, held, sems)
-    rows_ref, wk_ref, wv_ref, g_ref = held[:4]
-    grad_y_ref, normed_ref = held[-2:]
-    att_ref = outs[0]
-    got[0].wait()
+    count = 5 + 5 * parts
+    core_ref, rows_ref = refs[:2]
+    ins, outs, held = refs[2 : 2 + count], refs[2 + count : 7 + count], refs[7 + count : 7 + 2 * count]
+    att_ref, keys_ref, values_ref, own_ref, far_ref, turned_ref, turned_far_ref, sems = refs[-8:]
+    g_ref, grad_y_ref, normed_ref, wk_ref, wv_ref = held[-5:]
+    got = {}
+
+    def ask(*which):
+        for i in which:
+            got[i] = fetch([ins[i]], [held[i]], sems, i)[0]
+
+    ask(count - 2, count - 1)
     rows = rows_ref[...]
     place = lax.broadcasted_iota(jnp.int32, (dilated, 1), 0).astype(jnp.float32)
     pieces = []
     for end in range(dilated, rows.shape[0] + 1, dilated):
         pieces.append(jnp.where(place < rows_ref[end - 1 : end, :1].astype(jnp.float32), 0.0, -1e30))
     bias = jnp.concatenate(pieces, axis=0)
-    got[1].wait()
+    got[count - 2].wait()
+    ask(*range(5), count - 5)
     keys_ref[...] = project_t(wk_ref[...], rows)
-    got[2].wait()
+    got[count - 1].wait()
     values_ref[...] = project_t(wv_ref[...], rows)
-    got[3].wait()
+    got[count - 5].wait()
 
     for part in range(parts):
-        for copy in got[4 + part * 5 : 9 + part * 5]:
-            copy.wait()
-        q_ref, e_ref, m_ref, l_ref, o_ref = held[4 + part * 5 : 9 + part * 5]
+        for i in range(5 * part, 5 * part + 5):
+            got[i].wait()
+        if part + 1 < parts:
+            ask(*range(5 * part + 5, 5 * part + 10))
+        else:
+            ask(count - 4, count - 3)
+        q_ref, e_ref, m_ref, l_ref, o_ref = held[5 * part : 5 * part + 5]
         first = part * HEADS_A_CALL * HEAD
 
         def step(i, _):
@@ -209,8 +215,9 @@
                 pieces.append(ref[pl.ds(start, share)])
             yield jnp.concatenate(pieces, axis=0)
 
-    got[-2].wait()
-    got[-1].wait()
+    kept_copy = fetch([att_ref], [outs[0]], sems, count)[0]
+    got[count - 4].wait()
+    got[count - 3].wait()
     for half, out in zip(halves(att_ref), outs[1:3]):
         out[...] = mm(half, grad_y_ref[...]).astype(out.dtype)
     own_count = normed_ref.shape[0]
@@ -219,6 +226,7 @@
     for half, far, out in zip(halves(turned_ref), halves(turned_far_ref), outs[3:5]):
         total = mm_nt(half[:, :own_count], own_ref[...]) + mm_nt(far, far_ref[...])
         out[...] = total.astype(out.dtype)
+    kept_copy.wait()
 
 
 def attend_own(part, counts, rows, w_query, w_key, w_value):
@@ -234,17 +242,16 @@
     cut = pltpu.VMEM((features, rows.shape[1]), jnp.bfloat16)
     return pl.pallas_call(
         lambda *refs: own_body(part, *refs),
-        in_specs=[pl.BlockSpec(memory_space=pltpu.SMEM)] + [FAR_AWAY] * 4,
+        in_specs=[pl.BlockSpec(memory_space=pltpu.SMEM), NEAR] + [FAR_AWAY] * 3,
         out_specs=[FAR_AWAY] * 5,
         out_shape=outs,
         scratch_shapes=[
-            pltpu.VMEM(rows.shape, jnp.bfloat16),
             cut,
             cut,
             cut,
         ]
         + [pltpu.VMEM(o.shape, o.dtype) for o in outs]
-        + [pltpu.SemaphoreType.DMA((8 + HEADS_A_CALL,))],
+        + [pltpu.SemaphoreType.DMA((8 + 2 * HEADS_A_CALL,))],
         compiler_params=room(24),
         cost_estimate=pl.CostEstimate(
             flops=40 * features * count * count,
@@ -252,21 +259,22 @@
             bytes_accessed=2 * HEADS_A_CALL * count * count,
         ),
         name="attend_own",
-    )(counts, *away(rows, w_query, w_key, w_value))
+    )(counts, *near(rows), *away(w_query, w_key, w_value))
 
 
 def attend_far(dilated, core_bit, rows, w_key, w_value, grads, own, grad_y, normed):
     width, count = grads.shape
-    args = [rows, w_key, w_value, grads]
-    args += [array for arrays in own for array in arrays] + [grad_y, normed]
+    args = [array for arrays in own for array in arrays]
+    args += [grads, grad_y, normed, w_key, w_value]
     low = jnp.bfloat16
     cut = [pltpu.VMEM((width // 2, width), jnp.float32), pltpu.VMEM((width // 2, width), low)]
     return pl.pallas_call(
         lambda *refs: far_body(dilated, *refs),
-        in_specs=[pl.BlockSpec(memory_space=pltpu.SMEM)] + [FAR_AWAY] * len(args),
-        out_specs=[NEAR] * 5,
-        out_shape=[pltpu.VMEM((width, count), low)] + cut + cut,
+        in_specs=[pl.BlockSpec(memory_space=pltpu.SMEM)] + [NEAR] + [FAR_AWAY] * len(args),
+        out_specs=[FAR_AWAY] + [NEAR] * 4,
+        out_shape=[pltpu.HBM((width, count), low)] + cut + cut,
         scratch_shapes=[pltpu.VMEM(a.shape, a.dtype) for a in args]
+        + [pltpu.VMEM((width, count), low)]
         + [pltpu.VMEM((width, rows.shape[0]), low)] * 2
         + [
             pltpu.VMEM((width, count), low),
@@ -274,7 +282,7 @@
             pltpu.VMEM((width, count), low),
             pltpu.VMEM((width, rows.shape[0]), low),
         ]
-        + [pltpu.SemaphoreType.DMA((len(args),))],
+        + [pltpu.SemaphoreType.DMA((len(args) + 1,))],
         compiler_params=room(40),
         cost_estimate=pl.CostEstimate(
             flops=40 * width * count * count,
@@ -282,7 +290,7 @@
             bytes_accessed=2 * HEADS * count * count,
         ),
         name="attend_far",
-    )(core_bit, *away(*args))
+    )(core_bit, *near(rows), *away(*args))
 
 
 def near(*arrays):
@@ -326,10 +334,12 @@
         return lax.ppermute(value, "seq", pairs)
 
     def ring_next(self, value):
+        order = [0, *range(1, self.ring, 2), *range((self.ring - 1) // 2 * 2, 0, -2)]
+        after = {place: order[(i + 1) % self.ring] for i, place in enumerate(order)}
         pairs = []
         for g in range(self.groups):
             for s in range(self.seqs):
-                place = ((g // 2) * self.rests + s // 4 + 1) % self.ring
+                place = after[(g // 2) * self.rests + s // 4]
                 to_g = (place // self.rests) * 2 + g % 2
                 to_s = (place % self.rests) * 4 + s % 4
                 pairs.append((g * self.seqs + s, to_g * self.seqs + to_s))
@@ -496,10 +506,12 @@
     )(counts, *near(level, *sums, w_embed))
 
 
-def tokens_body(part_ref, back_ref, slide_ref, normed_ref):
+def tokens_body(part_ref, back_ref, slide_ref, normed_ref, near_ref):
     slide = jnp.concatenate([part_ref[...], back_ref[...]], axis=0)
     slide_ref[...] = slide
-    normed_ref[...] = norm_rows(slide.astype(jnp.float32)).astype(jnp.bfloat16)
+    normed = norm_rows(slide.astype(jnp.float32)).astype(jnp.bfloat16)
+    normed_ref[...] = normed
+    near_ref[...] = normed
 
 
 def tokens(part, back):
@@ -507,8 +519,8 @@
     return pl.pallas_call(
         tokens_body,
         in_specs=[NEAR] * 2,
-        out_specs=[NEAR] * 2,
-        out_shape=[pltpu.HBM(shape, jnp.bfloat16)] * 2,
+        out_specs=[NEAR] * 3,
+        out_shape=[pltpu.HBM(shape, jnp.bfloat16)] * 2 + [pltpu.VMEM(shape, jnp.bfloat16)],
         compiler_params=room(6),
         name="tokens",
     )(*near(part, back))
@@ -633,7 +645,7 @@
     live = seq_len - BLOCK
     is_valid = jnp.arange(live) < row_count
     grad_y, grad_att = grads_in(tile_counts, cotangent[0], w_out, live)
-    (slide_tok, slide_normed), far_block = encode(
+    (slide_tok, slide_normed, near_normed), far_block = encode(
         moves, tile_counts, tile_rows, row_count, w_gate, w_up, w_down_t, w_embed
     )
     width = slide_tok.shape[1]
@@ -642,7 +654,7 @@
     wq_t, wk_t, wv_t = turn(w_query, w_key, w_value)
     own = []
     for part in range(HEADS // HEADS_A_CALL):
-        own.append(attend_own(part, tile_counts, slide_normed, wq_t, wk_t, wv_t))
+        own.append(attend_own(part, tile_counts, near_normed, wq_t, wk_t, wv_t))
     core_bit = (lax.axis_index("seq") % 2).astype(jnp.int32)[None]
     attended, *parts = attend_far(
         dilated, core_bit, far_rows, wk_t, wv_t, grad_att, own, grad_y, slide_normed

time: 172 us -> 169 us (0.983)
  waiting for transfers between devices: 89.5 us -> 79.6 us
  starting transfers between devices: 27.2 us -> 36.5 us
    ppermute x17, starting transfers between devices: 11.2 us -> 17.5 us  [seq_xor(): return lax.ppermute(value, 'seq', [(s, s ^ bit) for s in range(self.seqs)])]
    ppermute x17, waiting for transfers between devices: 28.9 us -> 24.1 us  [seq_xor(): return lax.ppermute(value, 'seq', [(s, s ^ bit) for s in range(self.seqs)])]
    ppermute x3, waiting for transfers between devices: 32.4 us -> 27.9 us  [ring_next(): return lax.ppermute(value, BOTH, pairs)]
  transfers between devices with their start and end apart: 34 -> 34, of which waited for: 19 -> 21; matrix products, arithmetic and copies ran while one was open for 3% -> 3% of each run, Pallas kernels for 14% -> 14%
where the time goes in v6:
time: 169 us
  waiting for transfers between devices  79.6 us (47%)
  Pallas kernels  42.6 us (25%)
  starting transfers between devices  36.5 us (22%)
  local copies, waits for them, and re-layouts  4.69 us (3%)
  other arithmetic  3.46 us (2%)
    ppermute x3, waiting for transfers between devices, ring_next(): return lax.ppermute(value, BOTH, pairs)  27.9 us
    ppermute x17, waiting for transfers between devices, seq_xor(): return lax.ppermute(value, 'seq', [(s, s ^ bit) for s in range(self.seqs)])  24.1 us
    ppermute x11, waiting for transfers between devices, y(): lax.ppermute(value, 'group', [(g, g ^ 1) for g in range(self.groups)])  22.6 us
    ppermute x17, starting transfers between devices, seq_xor(): return lax.ppermute(value, 'seq', [(s, s ^ bit) for s in range(self.seqs)])  17.5 us
    pallas_call x1, Pallas kernels, attend_far(): pl.pallas_call(lambda *refs: far_body(dilated, *refs), in_specs=[pl.Block...  15.5 us
    pallas_call x2, Pallas kernels, attend_own(): pl.pallas_call(lambda *refs: own_body(part, *refs), in_specs=[pl.BlockSpe...  12.2 us
    ppermute x11, starting transfers between devices, y(): lax.ppermute(value, 'group', [(g, g ^ 1) for g in range(self.groups)])  11.7 us
    pallas_call x3, Pallas kernels, ffn_kernel(): pl.pallas_call(lambda *refs: ffn_body(len(rows), len(chunks), splits, *re...  6.77 us
  transfers between devices with their start and end apart: 34, of which 21 were waited for; matrix products, arithmetic and copies ran while one was open for 3% of the time, Pallas kernels for 14%

profile of v6, /device:TPU:0, one launch (start us, length us, event | category | flops | bytes accessed | tf_op | source)
XLA Modules:
  0.0 169.1 jit_solution(8342348943913876309)
XLA Ops:
  0.6 1.2 slice_bitcast_fusion
  1.8 3.1 %collective-permute-start = (bf16[160,1536]{1,0:T(8,128)(2,1)S(1)}, bf16[160,1536]{1,0:T(8,128)(2,1)S(1)}, u32[]{:S(2)}, u32[]{:S(2)}) collective-permute-start(bf16[160,1536]{1,0:T(8,128)(2,1)S(1)} %slice_bitcast_fusion), channel_id=1, source_target_pairs={{0,16},{16,0},{1,17},{17,1},{2,18},{18,2},{3,19},{19,3},{4,20},{20... | collective-permute-start | bytes 1474568 | tf_op jit(solution)/shard_map/ppermute | solution.py:327
  4.9 1.3 pack.1.refs_4_
  6.2 1.6 collective-permute-start.3
  8.5 7.5 %collective-permute-done = bf16[160,1536]{1,0:T(8,128)(2,1)S(1)} collective-permute-done((bf16[160,1536]{1,0:T(8,128)(2,1)S(1)}, bf16[160,1536]{1,0:T(8,128)(2,1)S(1)}, u32[]{:S(2)}, u32[]{:S(2)}) %collective-permute-start) | collective-permute-done | bytes 491552 | tf_op jit(solution)/shard_map/ppermute | solution.py:327
  16.7 5.3 %collective-permute-done.3.refs_6_ = bf16[2304,128]{1,0:T(8,128)(2,1)S(1)} collective-permute-done((bf16[2304,128]{1,0:T(8,128)(2,1)S(1)}, bf16[2304,128]{1,0:T(8,128)(2,1)S(1)}, u32[]{:S(2)}, u32[]{:S(2)}) %collective-permute-start.3) | collective-permute-done | bytes 589856 | tf_op jit(solution)/shard_map/ppermute | solution.py:346
  21.9 0.8 collective-permute-start.4
  22.8 1.6 collective-permute-start.1
  24.3 0.5 collective-permute-start.2
  25.1 11.7 %collective-permute-done.4.refs_8_ = bf16[2304,128]{1,0:T(8,128)(2,1)S(1)} collective-permute-done((bf16[2304,128]{1,0:T(8,128)(2,1)S(1)}, bf16[2304,128]{1,0:T(8,128)(2,1)S(1)}, u32[]{:S(2)}, u32[]{:S(2)}) %collective-permute-start.4) | collective-permute-done | bytes 589856 | tf_op jit(solution)/shard_map/ppermute | solution.py:346
  36.8 0.8 collective-permute-start.5
  37.6 0.6 collective-permute-start.7
  38.2 1.6 collective-permute-start.8
  39.8 11.0 %collective-permute-done.5.refs_2_ = bf16[2304,128]{1,0:T(8,128)(2,1)S(1)} collective-permute-done((bf16[2304,128]{1,0:T(8,128)(2,1)S(1)}, bf16[2304,128]{1,0:T(8,128)(2,1)S(1)}, u32[]{:S(2)}, u32[]{:S(2)}) %collective-permute-start.5) | collective-permute-done | bytes 589856 | tf_op jit(solution)/shard_map/ppermute | solution.py:346
  50.8 3.8 %shard_map.130 = (f32[96,1536]{1,0:T(8,128)S(1)}, f32[96,1536]{1,0:T(8,128)S(1)}, f32[96,1536]{1,0:T(8,128)S(1)}, f32[96,1536]{1,0:T(8,128)S(1)}, f32[96,1536]{1...) custom-call(bf16[192,1536]{1,0:T(8,128)(2,1)S(1)} %collective-permute-done.7.refs_0_, ...), custom_call_target="tpu_custom_call" | custom-call | flops 2717908992 | bytes 5898240 | tf_op jit(solution)/shard_map/pallas_call | solution.py:424
  54.7 1.5 shard_map.132
  56.1 1.6 collective-permute-start.13
  57.7 0.5 collective-permute-start.12
  58.2 1.5 collective-permute-start.15
  59.7 0.5 collective-permute-start.16
  60.3 1.5 shard_map.131
  61.7 4.4 %collective-permute-done.13 = bf16[96,1536]{1,0:T(8,128)(2,1)S(1)} collective-permute-done((bf16[96,1536]{1,0:T(8,128)(2,1)S(1)}, bf16[96,1536]{1,0:T(8,128)(2,1)S(1)}, u32[]{:S(2)}, u32[]{:S(2)}) %collective-permute-start.13) | collective-permute-done | bytes 294944 | tf_op jit(solution)/shard_map/ppermute | solution.py:327
  66.1 1.5 collective-permute-start.14
  67.7 6.7 %collective-permute-done.16 = bf16[96,1536]{1,0:T(8,128)(2,1)S(1)} collective-permute-done((bf16[96,1536]{1,0:T(8,128)(2,1)S(1)}, bf16[96,1536]{1,0:T(8,128)(2,1)S(1)}, u32[]{:S(2)}, u32[]{:S(2)}) %collective-permute-start.16) | collective-permute-done | bytes 294944 | tf_op jit(solution)/shard_map/ppermute | solution.py:318
  74.5 1.6 collective-permute-start.17
  76.1 3.6 %collective-permute-done.14.refs_2_ = bf16[96,1536]{1,0:T(8,128)(2,1)S(1)} collective-permute-done((bf16[96,1536]{1,0:T(8,128)(2,1)S(1)}, bf16[96,1536]{1,0:T(8,128)(2,1)S(1)}, u32[]{:S(2)}, u32[]{:S(2)}) %collective-permute-start.14) | collective-permute-done | bytes 294944 | tf_op jit(solution)/shard_map/ppermute | solution.py:318
  79.7 1.8 %collective-permute-done.17.refs_5_ = bf16[96,1536]{1,0:T(8,128)(2,1)S(1)} collective-permute-done((bf16[96,1536]{1,0:T(8,128)(2,1)S(1)}, bf16[96,1536]{1,0:T(8,128)(2,1)S(1)}, u32[]{:S(2)}, u32[]{:S(2)}) %collective-permute-start.17) | collective-permute-done | bytes 294944 | tf_op jit(solution)/shard_map/ppermute | solution.py:327
  81.5 1.4 finish.1
  82.9 1.4 collective-permute-start.19
  84.3 3.0 %collective-permute-done.19 = bf16[24,768]{1,0:T(8,128)(2,1)S(1)} collective-permute-done((bf16[24,768]{1,0:T(8,128)(2,1)S(1)}, bf16[24,768]{1,0:T(8,128)(2,1)S(1)}, u32[]{:S(2)}, u32[]{:S(2)}) %collective-permute-start.19) | collective-permute-done | bytes 36896 | tf_op jit(solution)/shard_map/ppermute | solution.py:327
  87.3 2.9 %collective-permute-start.20 = (bf16[24,768]{1,0:T(8,128)(2,1)S(1)}, bf16[24,768]{1,0:T(8,128)(2,1)S(1)}, u32[]{:S(2)}, u32[]{:S(2)}) collective-permute-start(bf16[24,768]{1,0:T(8,128)(2,1)S(1)} %broadcast_select_fusion.2.first_ref), channel_id=1, source_target_pairs={{0,8},{1,9},{2,10},{3,11},{4,12},{5,13},{6,14},{7,15},{8,0},{9,1},... | collective-permute-start | bytes 110600 | tf_op jit(solution)/shard_map/ppermute | solution.py:318
  90.2 1.0 collective-permute-start.18
  91.2 1.0 collective-permute-done.20.second_ref
  92.2 3.1 %collective-permute-start.21 = (bf16[48,768]{1,0:T(8,128)(2,1)S(1)}, bf16[48,768]{1,0:T(8,128)(2,1)S(1)}, u32[]{:S(2)}, u32[]{:S(2)}) collective-permute-start(bf16[48,768]{1,0:T(8,128)(2,1)S(1)} %join.4.first_ref), channel_id=1, source_target_pairs={{0,4},{1,5},{2,6},{3,7},{4,0},{5,1},{6,2},{7,3},{8,12},{9,13},{10,... | collective-permute-start | bytes 221192 | tf_op jit(solution)/shard_map/ppermute | solution.py:318
  95.3 2.3 %collective-permute-done.21.second_ref = bf16[48,768]{1,0:T(8,128)(2,1)S(1)} collective-permute-done((bf16[48,768]{1,0:T(8,128)(2,1)S(1)}, bf16[48,768]{1,0:T(8,128)(2,1)S(1)}, u32[]{:S(2)}, u32[]{:S(2)}) %collective-permute-start.21) | collective-permute-done | bytes 73760 | tf_op jit(solution)/shard_map/ppermute | solution.py:318
  97.6 1.6 collective-permute-start.22
  99.2 0.8 grads_in.1
  100.0 0.9 copy-done.3
  100.9 0.8 copy-done.4
  101.7 3.5 %turn.1 = (bf16[768,768]{1,0:T(8,128)(2,1)}, bf16[768,768]{1,0:T(8,128)(2,1)}, bf16[768,768]{1,0:T(8,128)(2,1)}) custom-call(bf16[768,768]{1,0:T(8,128)(2,1)} %refs_0_.3, bf16[768,768]{1,0:T(8,128)(2,1)} %refs_1_.1, bf16[768,768]{1,0:T(8,128)(2,1)} %refs_2_.1), custom_call_target="tpu_custom_call" | custom-call | tf_op jit(solution)/shard_map/turn/pallas_call | solution.py:102
  105.2 1.0 tokens.1
  106.4 6.2 %attend_own.2 = (bf16[384,352]{1,0:T(8,128)(2,1)}, bf16[8,352,352]{2,1,0:T(8,128)(2,1)}, f32[8,1,352]{2,1,0:T(1,128)}, f32[8,1,352]{2,1,0:T(1,128)}, f32[384,352]{1,0:T(8,128)}) custom-call(s32[1,1]{1,0:T(1,128)} %copy.21.count_ref.refs_0_, bf16[352,768]{1,0:T(8,128)(2,1)S(1)} %get-tuple-element.67.refs_1_, bf16[768,768]{1,0:T(8,128)(2,1)} %get-tuple-element.68.refs_2_, ...), custom_call_target="tpu_custom_call" | custom-call | flops 1903165440 | bytes 1982464 | tf_op jit(solution)/shard_map/attend_own/pallas_call | solution.py:243
  112.6 6.0 %attend_own.3 = (bf16[384,352]{1,0:T(8,128)(2,1)}, bf16[8,352,352]{2,1,0:T(8,128)(2,1)}, f32[8,1,352]{2,1,0:T(1,128)}, f32[8,1,352]{2,1,0:T(1,128)}, f32[384,352]{1,0:T(8,128)}) custom-call(s32[1,1]{1,0:T(1,128)} %copy.21.count_ref.refs_0_, bf16[352,768]{1,0:T(8,128)(2,1)S(1)} %get-tuple-element.67.refs_1_, bf16[768,768]{1,0:T(8,128)(2,1)} %get-tuple-element.68.refs_2_, ...), custom_call_target="tpu_custom_call" | custom-call | flops 1903165440 | bytes 1982464 | tf_op jit(solution)/shard_map/attend_own/pallas_call | solution.py:243
  118.7 15.5 %attend_far.1 = (bf16[768,352]{1,0:T(8,128)(2,1)}, f32[384,768]{1,0:T(8,128)S(1)}, bf16[384,768]{1,0:T(8,128)(2,1)}, f32[384,768]{1,0:T(8,128)S(1)}, bf16[384,768]{1,0:T(8,128)(2,1)}) custom-call(s32[1]{0:T(128)} %bitcast.9.refs_0_, bf16[384,768]{1,0:T(8,128)(2,1)S(1)} %join.7.refs_1_, bf16[384,352]{1,0:T(8,128)(2,1)} %get-tuple-element.71.refs_2_, ...), custom_call_target="tpu_custom_call" | custom-call | flops 3806330880 | bytes 3964928 | tf_op jit(solution)/shard_map/attend_far/pallas_call | solution.py:271
  134.2 0.6 collective-permute-start.24
  134.8 1.9 %collective-permute-done.24 = bf16[384,768]{1,0:T(8,128)(2,1)} collective-permute-done((bf16[384,768]{1,0:T(8,128)(2,1)}, bf16[384,768]{1,0:T(8,128)(2,1)}, u32[]{:S(2)}, u32[]{:S(2)}) %collective-permute-start.24) | collective-permute-done | bytes 589856 | tf_op jit(solution)/shard_map/ppermute | solution.py:318
  136.7 1.2 convert_add_fusion.1
  137.9 0.6 collective-permute-start.25
  138.5 1.2 convert_add_fusion
  140.1 7.2 %collective-permute-done.25 = bf16[4,2,24,768]{3,2,1,0:T(8,128)(2,1)S(1)} collective-permute-done((bf16[4,2,24,768]{3,2,1,0:T(8,128)(2,1)S(1)}, bf16[4,2,24,768]{3,2,1,0:T(8,128)(2,1)S(1)}, u32[]{:S(2)}, u32[]{:S(2)}) %collective-permute-start.25) | collective-permute-done | bytes 294944 | tf_op jit(solution)/shard_map/ppermute | solution.py:318
  147.7 1.1 collective-permute-done.28
  148.9 1.8 %collective-permute-start.29 = (bf16[4,24,768]{2,1,0:T(8,128)(2,1)S(1)}, bf16[4,24,768]{2,1,0:T(8,128)(2,1)S(1)}, u32[]{:S(2)}, u32[]{:S(2)}) collective-permute-start(bf16[4,24,768]{2,1,0:T(8,128)(2,1)S(1)} %fusion.6), channel_id=1, source_target_pairs={{0,2},{1,3},{2,0},{3,1},{4,6},{5,7},{6,4},{7,5},{8,10},{9,11},{10,... | collective-permute-start | bytes 442376 | tf_op jit(solution)/shard_map/ppermute | solution.py:318
  150.7 2.0 %collective-permute-done.26 = bf16[4,24,768]{2,1,0:T(8,128)(2,1)S(1)} collective-permute-done((bf16[4,24,768]{2,1,0:T(8,128)(2,1)S(1)}, bf16[4,24,768]{2,1,0:T(8,128)(2,1)S(1)}, u32[]{:S(2)}, u32[]{:S(2)}) %collective-permute-start.26) | collective-permute-done | bytes 147488 | tf_op jit(solution)/shard_map/ppermute | solution.py:327
  152.7 1.4 collective-permute-done.29
  154.2 3.1 %collective-permute-start.32 = (bf16[24,1536]{1,0:T(8,128)(2,1)S(1)}, bf16[24,1536]{1,0:T(8,128)(2,1)S(1)}, u32[]{:S(2)}, u32[]{:S(2)}) collective-permute-start(bf16[24,1536]{1,0:T(8,128)(2,1)S(1)} %get-tuple-element.94), channel_id=1, source_target_pairs={{0,12},{1,13},{2,14},{3,15},{4,0},{5,1},{6,2},{7,3},{8,4},{9,5},{1... | collective-permute-start | bytes 221192 | tf_op jit(solution)/shard_map/ppermute | solution.py:334
  157.3 0.5 collective-permute-start.31
  157.7 0.5 collective-permute-start.30
  158.2 0.6 select_convert_fusion
  159.2 3.5 %collective-permute-done.31 = bf16[24,1536]{1,0:T(8,128)(2,1)S(1)} collective-permute-done((bf16[24,1536]{1,0:T(8,128)(2,1)S(1)}, bf16[24,1536]{1,0:T(8,128)(2,1)S(1)}, u32[]{:S(2)}, u32[]{:S(2)}) %collective-permute-start.31) | collective-permute-done | bytes 73760 | tf_op jit(solution)/shard_map/ppermute | solution.py:334
  162.7 1.2 collective-permute-done.30
  163.9 0.7 collective-permute-start.33
  164.7 0.9 pad_bitcast_fusion
  165.5 2.8 %collective-permute-done.33 = bf16[24,1536]{1,0:T(8,128)(2,1)S(1)} collective-permute-done((bf16[24,1536]{1,0:T(8,128)(2,1)S(1)}, bf16[24,1536]{1,0:T(8,128)(2,1)S(1)}, u32[]{:S(2)}, u32[]{:S(2)}) %collective-permute-start.33) | collective-permute-done | bytes 73760 | tf_op jit(solution)/shard_map/ppermute | solution.py:327
  168.4 0.7 fusion.16
  (70 shorter events, 3.1 us)
Async XLA Ops:
  0.6 7.9 %copy-start.5 = (bf16[1,384,1536]{2,1,0:T(8,128)(2,1)S(1)}, bf16[1,384,1536]{2,1,0:T(8,128)(2,1)}, u32[]{:S(2)}) copy-start(bf16[1,384,1536]{2,1,0:T(8,128)(2,1)} %param.11) | copy-start | bytes 3538948
  1.8 14.3 %collective-permute-start = (bf16[160,1536]{1,0:T(8,128)(2,1)S(1)}, bf16[160,1536]{1,0:T(8,128)(2,1)S(1)}, u32[]{:S(2)}, u32[]{:S(2)}) collective-permute-start(bf16[160,1536]{1,0:T(8,128)(2,1)S(1)} %slice_bitcast_fusion), channel_id=1, source_target_pairs={{0,16},{16,0},{1,17},{17,1},{2,18},{18,2},{3,19},{19,3},{4,20},{20... | collective-permute-start | bytes 1474568 | tf_op jit(solution)/shard_map/ppermute | solution.py:327
  6.2 15.7 %collective-permute-start.3 = (bf16[2304,128]{1,0:T(8,128)(2,1)S(1)}, bf16[2304,128]{1,0:T(8,128)(2,1)S(1)}, u32[]{:S(2)}, u32[]{:S(2)}) collective-permute-start(bf16[2304,128]{1,0:T(8,128)(2,1)S(1)} %pack.1.refs_4_), channel_id=1, source_target_pairs={{0,4},{1,5},{2,6},{3,7},{4,12},{5,13},{6,14},{7,15},{8,0},{9,1},{1... | collective-permute-start | bytes 1769480 | tf_op jit(solution)/shard_map/ppermute | solution.py:346
  21.9 14.8 %collective-permute-start.4 = (bf16[2304,128]{1,0:T(8,128)(2,1)S(1)}, bf16[2304,128]{1,0:T(8,128)(2,1)S(1)}, u32[]{:S(2)}, u32[]{:S(2)}) collective-permute-start(bf16[2304,128]{1,0:T(8,128)(2,1)S(1)} %collective-permute-done.3.refs_6_), channel_id=1, source_target_pairs={{0,4},{1,5},{2,6},{3,7},{4,12},{5,13},{6,14},{7,15},{8,0},{9,1},{1... | collective-permute-start | bytes 1769480 | tf_op jit(solution)/shard_map/ppermute | solution.py:346
  22.8 14.8 %collective-permute-start.1 = (bf16[96,1536]{1,0:T(8,128)(2,1)S(1)}, bf16[96,1536]{1,0:T(8,128)(2,1)S(1)}, u32[]{:S(2)}, u32[]{:S(2)}) collective-permute-start(bf16[96,1536]{1,0:T(8,128)(2,1)S(1)} %get-tuple-element.90), channel_id=1, source_target_pairs={{0,2},{1,3},{2,0},{3,1},{4,6},{5,7},{6,4},{7,5},{8,10},{9,11},{10,... | collective-permute-start | bytes 884744 | tf_op jit(solution)/shard_map/ppermute | solution.py:318
  24.3 15.5 %collective-permute-start.9 = (bf16[2304,128]{1,0:T(8,128)(2,1)S(1)}, bf16[2304,128]{1,0:T(8,128)(2,1)S(1)}, u32[]{:S(2)}, u32[]{:S(2)}) collective-permute-start(bf16[2304,128]{1,0:T(8,128)(2,1)S(1)} %pack.1.refs_4_), channel_id=1, source_target_pairs={{0,1},{1,0},{2,3},{3,2},{4,5},{5,4},{6,7},{7,6},{8,9},{9,8},{10,11... | collective-permute-start | bytes 1769480 | tf_op jit(solution)/shard_map/ppermute | solution.py:318
  24.3 13.9 %collective-permute-start.2 = (bf16[96,1536]{1,0:T(8,128)(2,1)S(1)}, bf16[96,1536]{1,0:T(8,128)(2,1)S(1)}, u32[]{:S(2)}, u32[]{:S(2)}) collective-permute-start(bf16[96,1536]{1,0:T(8,128)(2,1)S(1)} %get-tuple-element.89), channel_id=1, source_target_pairs={{0,16},{16,0},{1,17},{17,1},{2,18},{18,2},{3,19},{19,3},{4,20},{20... | collective-permute-start | bytes 884744 | tf_op jit(solution)/shard_map/ppermute | solution.py:327
  24.8 25.9 %collective-permute-start.10 = (bf16[2304,128]{1,0:T(8,128)(2,1)S(1)}, bf16[2304,128]{1,0:T(8,128)(2,1)S(1)}, u32[]{:S(2)}, u32[]{:S(2)}) collective-permute-start(bf16[2304,128]{1,0:T(8,128)(2,1)S(1)} %collective-permute-done.3.refs_6_), channel_id=1, source_target_pairs={{0,1},{1,0},{2,3},{3,2},{4,5},{5,4},{6,7},{7,6},{8,9},{9,8},{10,11... | collective-permute-start | bytes 1769480 | tf_op jit(solution)/shard_map/ppermute | solution.py:318
  36.8 14.0 %collective-permute-start.5 = (bf16[2304,128]{1,0:T(8,128)(2,1)S(1)}, bf16[2304,128]{1,0:T(8,128)(2,1)S(1)}, u32[]{:S(2)}, u32[]{:S(2)}) collective-permute-start(bf16[2304,128]{1,0:T(8,128)(2,1)S(1)} %collective-permute-done.4.refs_8_), channel_id=1, source_target_pairs={{0,4},{1,5},{2,6},{3,7},{4,12},{5,13},{6,14},{7,15},{8,0},{9,1},{1... | collective-permute-start | bytes 1769480 | tf_op jit(solution)/shard_map/ppermute | solution.py:346
  37.6 13.2 %collective-permute-start.7 = (bf16[192,1536]{1,0:T(8,128)(2,1)S(1)}, bf16[192,1536]{1,0:T(8,128)(2,1)S(1)}, u32[]{:S(2)}, u32[]{:S(2)}) collective-permute-start(bf16[192,1536]{1,0:T(8,128)(2,1)S(1)} %pad_maximum_fusion.2.refs_2_.refs_0_), channel_id=1, source_target_pairs={{0,16},{16,0},{1,17},{17,1},{2,18},{18,2},{3,19},{19,3},{4,20},{20... | collective-permute-start | bytes 1769480 | tf_op jit(solution)/shard_map/ppermute | solution.py:327
  38.2 12.6 %collective-permute-start.8 = (bf16[192,1536]{1,0:T(8,128)(2,1)S(1)}, bf16[192,1536]{1,0:T(8,128)(2,1)S(1)}, u32[]{:S(2)}, u32[]{:S(2)}) collective-permute-start(bf16[192,1536]{1,0:T(8,128)(2,1)S(1)} %pad_maximum_fusion.3.refs_3_.refs_1_), channel_id=1, source_target_pairs={{0,2},{1,3},{2,0},{3,1},{4,6},{5,7},{6,4},{7,5},{8,10},{9,11},{10,... | collective-permute-start | bytes 1769480 | tf_op jit(solution)/shard_map/ppermute | solution.py:318
  39.8 11.0 %collective-permute-start.11 = (bf16[2304,128]{1,0:T(8,128)(2,1)S(1)}, bf16[2304,128]{1,0:T(8,128)(2,1)S(1)}, u32[]{:S(2)}, u32[]{:S(2)}) collective-permute-start(bf16[2304,128]{1,0:T(8,128)(2,1)S(1)} %collective-permute-done.4.refs_8_), channel_id=1, source_target_pairs={{0,1},{1,0},{2,3},{3,2},{4,5},{5,4},{6,7},{7,6},{8,9},{9,8},{10,11... | collective-permute-start | bytes 1769480 | tf_op jit(solution)/shard_map/ppermute | solution.py:318
  50.7 3.9 %collective-permute-start.6 = (bf16[2304,128]{1,0:T(8,128)(2,1)S(1)}, bf16[2304,128]{1,0:T(8,128)(2,1)S(1)}, u32[]{:S(2)}, u32[]{:S(2)}) collective-permute-start(bf16[2304,128]{1,0:T(8,128)(2,1)S(1)} %collective-permute-done.5.refs_2_), channel_id=1, source_target_pairs={{0,1},{1,0},{2,3},{3,2},{4,5},{5,4},{6,7},{7,6},{8,9},{9,8},{10,11... | collective-permute-start | bytes 1769480 | tf_op jit(solution)/shard_map/ppermute | solution.py:318
  56.1 9.9 %collective-permute-start.13 = (bf16[96,1536]{1,0:T(8,128)(2,1)S(1)}, bf16[96,1536]{1,0:T(8,128)(2,1)S(1)}, u32[]{:S(2)}, u32[]{:S(2)}) collective-permute-start(bf16[96,1536]{1,0:T(8,128)(2,1)S(1)} %get-tuple-element.57), channel_id=1, source_target_pairs={{0,16},{16,0},{1,17},{17,1},{2,18},{18,2},{3,19},{19,3},{4,20},{20... | collective-permute-start | bytes 884744 | tf_op jit(solution)/shard_map/ppermute | solution.py:327
  57.7 18.4 %collective-permute-start.12 = (bf16[96,1536]{1,0:T(8,128)(2,1)S(1)}, bf16[96,1536]{1,0:T(8,128)(2,1)S(1)}, u32[]{:S(2)}, u32[]{:S(2)}) collective-permute-start(bf16[96,1536]{1,0:T(8,128)(2,1)S(1)} %get-tuple-element.55), channel_id=1, source_target_pairs={{0,16},{16,0},{1,17},{17,1},{2,18},{18,2},{3,19},{19,3},{4,20},{20... | collective-permute-start | bytes 884744 | tf_op jit(solution)/shard_map/ppermute | solution.py:327
  58.2 17.9 %collective-permute-start.15 = (bf16[96,1536]{1,0:T(8,128)(2,1)S(1)}, bf16[96,1536]{1,0:T(8,128)(2,1)S(1)}, u32[]{:S(2)}, u32[]{:S(2)}) collective-permute-start(bf16[96,1536]{1,0:T(8,128)(2,1)S(1)} %get-tuple-element.59), channel_id=1, source_target_pairs={{0,2},{1,3},{2,0},{3,1},{4,6},{5,7},{6,4},{7,5},{8,10},{9,11},{10,... | collective-permute-start | bytes 884744 | tf_op jit(solution)/shard_map/ppermute | solution.py:318
  59.7 14.7 %collective-permute-start.16 = (bf16[96,1536]{1,0:T(8,128)(2,1)S(1)}, bf16[96,1536]{1,0:T(8,128)(2,1)S(1)}, u32[]{:S(2)}, u32[]{:S(2)}) collective-permute-start(bf16[96,1536]{1,0:T(8,128)(2,1)S(1)} %get-tuple-element.61), channel_id=1, source_target_pairs={{0,2},{1,3},{2,0},{3,1},{4,6},{5,7},{6,4},{7,5},{8,10},{9,11},{10,... | collective-permute-start | bytes 884744 | tf_op jit(solution)/shard_map/ppermute | solution.py:318
  66.1 13.6 %collective-permute-start.14 = (bf16[96,1536]{1,0:T(8,128)(2,1)S(1)}, bf16[96,1536]{1,0:T(8,128)(2,1)S(1)}, u32[]{:S(2)}, u32[]{:S(2)}) collective-permute-start(bf16[96,1536]{1,0:T(8,128)(2,1)S(1)} %add_convert_fusion.1), channel_id=1, source_target_pairs={{0,2},{1,3},{2,0},{3,1},{4,6},{5,7},{6,4},{7,5},{8,10},{9,11},{10,... | collective-permute-start | bytes 884744 | tf_op jit(solution)/shard_map/ppermute | solution.py:318
  74.4 7.0 %copy-start = (bf16[1536,768]{1,0:T(8,128)(2,1)S(1)}, bf16[1536,768]{1,0:T(8,128)(2,1)}, u32[]{:S(2)}) copy-start(bf16[1536,768]{1,0:T(8,128)(2,1)} %refs_6_.1) | copy-start | bytes 7077892
  74.5 7.0 %collective-permute-start.17 = (bf16[96,1536]{1,0:T(8,128)(2,1)S(1)}, bf16[96,1536]{1,0:T(8,128)(2,1)S(1)}, u32[]{:S(2)}, u32[]{:S(2)}) collective-permute-start(bf16[96,1536]{1,0:T(8,128)(2,1)S(1)} %add_convert_fusion), channel_id=1, source_target_pairs={{0,16},{16,0},{1,17},{17,1},{2,18},{18,2},{3,19},{19,3},{4,20},{20... | collective-permute-start | bytes 884744 | tf_op jit(solution)/shard_map/ppermute | solution.py:327
  81.5 17.7 %copy-start.1 = (bf16[768,768]{1,0:T(8,128)(2,1)S(1)}, bf16[768,768]{1,0:T(8,128)(2,1)}, u32[]{:S(2)}) copy-start(bf16[768,768]{1,0:T(8,128)(2,1)} %w_out_ref.1) | copy-start | bytes 3538948
  81.5 17.7 %copy-start.2 = (bf16[1,384,768]{2,1,0:T(8,128)(2,1)S(1)}, bf16[1,384,768]{2,1,0:T(8,128)(2,1)}, u32[]{:S(2)}) copy-start(bf16[1,384,768]{2,1,0:T(8,128)(2,1)} %param.21) | copy-start | bytes 1769476
  82.9 4.4 %collective-permute-start.19 = (bf16[24,768]{1,0:T(8,128)(2,1)S(1)}, bf16[24,768]{1,0:T(8,128)(2,1)S(1)}, u32[]{:S(2)}, u32[]{:S(2)}) collective-permute-start(bf16[24,768]{1,0:T(8,128)(2,1)S(1)} %get-tuple-element.65), channel_id=1, source_target_pairs={{0,16},{16,0},{1,17},{17,1},{2,18},{18,2},{3,19},{19,3},{4,20},{20... | collective-permute-start | bytes 110600 | tf_op jit(solution)/shard_map/ppermute | solution.py:327
  87.3 4.9 %collective-permute-start.20 = (bf16[24,768]{1,0:T(8,128)(2,1)S(1)}, bf16[24,768]{1,0:T(8,128)(2,1)S(1)}, u32[]{:S(2)}, u32[]{:S(2)}) collective-permute-start(bf16[24,768]{1,0:T(8,128)(2,1)S(1)} %broadcast_select_fusion.2.first_ref), channel_id=1, source_target_pairs={{0,8},{1,9},{2,10},{3,11},{4,12},{5,13},{6,14},{7,15},{8,0},{9,1},... | collective-permute-start | bytes 110600 | tf_op jit(solution)/shard_map/ppermute | solution.py:318
  90.2 15.0 %collective-permute-start.18 = (bf16[160,768]{1,0:T(8,128)(2,1)S(1)}, bf16[160,768]{1,0:T(8,128)(2,1)S(1)}, u32[]{:S(2)}, u32[]{:S(2)}) collective-permute-start(bf16[160,768]{1,0:T(8,128)(2,1)S(1)} %get-tuple-element.63), channel_id=1, source_target_pairs={{0,16},{16,0},{1,17},{17,1},{2,18},{18,2},{3,19},{19,3},{4,20},{20... | collective-permute-start | bytes 737288 | tf_op jit(solution)/shard_map/ppermute | solution.py:327
  92.2 5.4 %collective-permute-start.21 = (bf16[48,768]{1,0:T(8,128)(2,1)S(1)}, bf16[48,768]{1,0:T(8,128)(2,1)S(1)}, u32[]{:S(2)}, u32[]{:S(2)}) collective-permute-start(bf16[48,768]{1,0:T(8,128)(2,1)S(1)} %join.4.first_ref), channel_id=1, source_target_pairs={{0,4},{1,5},{2,6},{3,7},{4,0},{5,1},{6,2},{7,3},{8,12},{9,13},{10,... | collective-permute-start | bytes 221192 | tf_op jit(solution)/shard_map/ppermute | solution.py:318
  97.6 8.6 %collective-permute-start.22 = (bf16[96,768]{1,0:T(8,128)(2,1)S(1)}, bf16[96,768]{1,0:T(8,128)(2,1)S(1)}, u32[]{:S(2)}, u32[]{:S(2)}) collective-permute-start(bf16[96,768]{1,0:T(8,128)(2,1)S(1)} %join.5.first_ref), channel_id=1, source_target_pairs={{0,2},{1,3},{2,0},{3,1},{4,6},{5,7},{6,4},{7,5},{8,10},{9,11},{10,... | collective-permute-start | bytes 442376 | tf_op jit(solution)/shard_map/ppermute | solution.py:318
  100.0 0.9 copy-start.3
  100.9 0.8 copy-start.4
  106.3 12.3 %collective-permute-start.23 = (bf16[192,768]{1,0:T(8,128)(2,1)S(1)}, bf16[192,768]{1,0:T(8,128)(2,1)S(1)}, u32[]{:S(2)}, u32[]{:S(2)}) collective-permute-start(bf16[192,768]{1,0:T(8,128)(2,1)S(1)} %join.6.first_ref), channel_id=1, source_target_pairs={{0,1},{1,0},{2,3},{3,2},{4,5},{5,4},{6,7},{7,6},{8,9},{9,8},{10,11... | collective-permute-start | bytes 884744 | tf_op jit(solution)/shard_map/ppermute | solution.py:318
  134.2 2.5 %collective-permute-start.24 = (bf16[384,768]{1,0:T(8,128)(2,1)}, bf16[384,768]{1,0:T(8,128)(2,1)}, u32[]{:S(2)}, u32[]{:S(2)}) collective-permute-start(bf16[384,768]{1,0:T(8,128)(2,1)} %get-tuple-element.86), channel_id=1, source_target_pairs={{0,1},{1,0},{2,3},{3,2},{4,5},{5,4},{6,7},{7,6},{8,9},{9,8},{10,11... | collective-permute-start | bytes 1769480 | tf_op jit(solution)/shard_map/ppermute | solution.py:318
  134.7 3.8 %collective-permute-start.27 = (bf16[384,768]{1,0:T(8,128)(2,1)}, bf16[384,768]{1,0:T(8,128)(2,1)}, u32[]{:S(2)}, u32[]{:S(2)}) collective-permute-start(bf16[384,768]{1,0:T(8,128)(2,1)} %get-tuple-element.88), channel_id=1, source_target_pairs={{0,1},{1,0},{2,3},{3,2},{4,5},{5,4},{6,7},{7,6},{8,9},{9,8},{10,11... | collective-permute-start | bytes 1769480 | tf_op jit(solution)/shard_map/ppermute | solution.py:318
  137.9 9.4 %collective-permute-start.25 = (bf16[4,2,24,768]{3,2,1,0:T(8,128)(2,1)S(1)}, bf16[4,2,24,768]{3,2,1,0:T(8,128)(2,1)S(1)}, u32[]{:S(2)}, u32[]{:S(2)}) collective-permute-start(bf16[4,2,24,768]{3,2,1,0:T(8,128)(2,1)S(1)} %fusion.3), channel_id=1, source_target_pairs={{0,2},{1,3},{2,0},{3,1},{4,6},{5,7},{6,4},{7,5},{8,10},{9,11},{10,... | collective-permute-start | bytes 884744 | tf_op jit(solution)/shard_map/ppermute | solution.py:318
  139.7 9.1 %collective-permute-start.28 = (bf16[4,2,24,768]{3,2,0,1:T(8,128)(2,1)S(1)}, bf16[4,2,24,768]{3,2,0,1:T(8,128)(2,1)S(1)}, u32[]{:S(2)}, u32[]{:S(2)}) collective-permute-start(bf16[4,2,24,768]{3,2,0,1:T(8,128)(2,1)S(1)} %fusion.4), channel_id=1, source_target_pairs={{0,16},{16,0},{1,17},{17,1},{2,18},{18,2},{3,19},{19,3},{4,20},{20... | collective-permute-start | bytes 884744 | tf_op jit(solution)/shard_map/ppermute | solution.py:327
  147.4 5.3 %collective-permute-start.26 = (bf16[4,24,768]{2,1,0:T(8,128)(2,1)S(1)}, bf16[4,24,768]{2,1,0:T(8,128)(2,1)S(1)}, u32[]{:S(2)}, u32[]{:S(2)}) collective-permute-start(bf16[4,24,768]{2,1,0:T(8,128)(2,1)S(1)} %fusion.5), channel_id=1, source_target_pairs={{0,16},{16,0},{1,17},{17,1},{2,18},{18,2},{3,19},{19,3},{4,20},{20... | collective-permute-start | bytes 442376 | tf_op jit(solution)/shard_map/ppermute | solution.py:327
  148.9 5.2 %collective-permute-start.29 = (bf16[4,24,768]{2,1,0:T(8,128)(2,1)S(1)}, bf16[4,24,768]{2,1,0:T(8,128)(2,1)S(1)}, u32[]{:S(2)}, u32[]{:S(2)}) collective-permute-start(bf16[4,24,768]{2,1,0:T(8,128)(2,1)S(1)} %fusion.6), channel_id=1, source_target_pairs={{0,2},{1,3},{2,0},{3,1},{4,6},{5,7},{6,4},{7,5},{8,10},{9,11},{10,... | collective-permute-start | bytes 442376 | tf_op jit(solution)/shard_map/ppermute | solution.py:318
  152.7 5.5 %copy-start.6 = (bf16[352,768]{1,0:T(8,128)(2,1)S(1)}, bf16[352,768]{1,0:T(8,128)(2,1)}, u32[]{:S(2)}) copy-start(bf16[352,768]{1,0:T(8,128)(2,1)} %get-tuple-element.64) | copy-start | bytes 1622020
  152.7 5.5 %copy-start.7 = (bf16[768,352]{1,0:T(8,128)(2,1)S(1)}, bf16[768,352]{1,0:T(8,128)(2,1)}, u32[]{:S(2)}) copy-start(bf16[768,352]{1,0:T(8,128)(2,1)} %get-tuple-element.84) | copy-start | bytes 1622020
  154.2 5.0 %collective-permute-start.32 = (bf16[24,1536]{1,0:T(8,128)(2,1)S(1)}, bf16[24,1536]{1,0:T(8,128)(2,1)S(1)}, u32[]{:S(2)}, u32[]{:S(2)}) collective-permute-start(bf16[24,1536]{1,0:T(8,128)(2,1)S(1)} %get-tuple-element.94), channel_id=1, source_target_pairs={{0,12},{1,13},{2,14},{3,15},{4,0},{5,1},{6,2},{7,3},{8,4},{9,5},{1... | collective-permute-start | bytes 221192 | tf_op jit(solution)/shard_map/ppermute | solution.py:334
  157.3 5.5 %collective-permute-start.31 = (bf16[24,1536]{1,0:T(8,128)(2,1)S(1)}, bf16[24,1536]{1,0:T(8,128)(2,1)S(1)}, u32[]{:S(2)}, u32[]{:S(2)}) collective-permute-start(bf16[24,1536]{1,0:T(8,128)(2,1)S(1)} %get-tuple-element.95), channel_id=1, source_target_pairs={{0,8},{1,9},{2,10},{3,11},{4,12},{5,13},{6,14},{7,15},{8,0},{9,1},... | collective-permute-start | bytes 221192 | tf_op jit(solution)/shard_map/ppermute | solution.py:334
  157.7 6.2 %collective-permute-start.30 = (bf16[24,1536]{1,0:T(8,128)(2,1)S(1)}, bf16[24,1536]{1,0:T(8,128)(2,1)S(1)}, u32[]{:S(2)}, u32[]{:S(2)}) collective-permute-start(bf16[24,1536]{1,0:T(8,128)(2,1)S(1)} %get-tuple-element.93), channel_id=1, source_target_pairs={{0,4},{1,5},{2,6},{3,7},{4,8},{5,9},{6,10},{7,11},{8,12},{9,13},{1... | collective-permute-start | bytes 221192 | tf_op jit(solution)/shard_map/ppermute | solution.py:334
  163.9 4.4 %collective-permute-start.33 = (bf16[24,1536]{1,0:T(8,128)(2,1)S(1)}, bf16[24,1536]{1,0:T(8,128)(2,1)S(1)}, u32[]{:S(2)}, u32[]{:S(2)}) collective-permute-start(bf16[24,1536]{1,0:T(8,128)(2,1)S(1)} %fusion.12), channel_id=1, source_target_pairs={{0,16},{16,0},{1,17},{17,1},{2,18},{18,2},{3,19},{19,3},{4,20},{20... | collective-permute-start | bytes 221192 | tf_op jit(solution)/shard_map/ppermute | solution.py:327
